TPU v7x, 32 devices: a whole 2x2x4 slice. The times are simulated.
32 devices in a mesh: ens: 2 (over y), gx: 4 (over x, core), gy: 4 (over z).
Axes of the slice: x: 2, y: 2, z: 4, core: 2. Of those that a mesh axis runs over, the one named last changes fastest.
Arguments:
- log_conductivity: float32 [64, 64, 256], P(('ens', 'gx'), 'gy'), parts along dimension 0, may hold values from -3 to 3
- state: float32 [64, 64, 256], P(('ens', 'gx'), 'gy'), parts along dimension 0, may hold values from -6 to 6
- gradient: float32 [64, 64, 256], P(('ens', 'gx'), 'gy'), parts along dimension 0, may hold values from -60 to 60
- prior_sample: float32 [64, 64, 256], P(('ens', 'gx'), 'gy'), parts along dimension 0, may hold values from -6 to 6
- sensor_cells: int32 [16384], P(('ens', 'gx', 'gy')), parts along dimension 0, may hold values from 0 to 524287, as said below
- noise_precision: float32 [16384], P(('ens', 'gx', 'gy')), parts along dimension 0, may hold values from 20 to 200
Outputs:
- step_field: float32 [64, 64, 256], P(('ens', 'gx'), 'gy'), parts along dimension 0
- residual: float32 [64, 64, 256], P(('ens', 'gx'), 'gy'), parts along dimension 0
There are 2 independent parts, one for each index of `ens`. A program takes and returns all parts, laid end to end along the dimension named above; each array names one. Nothing has to cross between parts.
Inputs may be any that keep to these rules, and one draw needn't show every extreme that they name: `sensor_cells`: sensors t * 512 to (t + 1) * 512 - 1 observe cells inside the block of cells held by the t-th device in the order gx, then gy (blocks of 8 x 16 x 256 cells); a cell may be observed by several sensors.
All inputs are finite; a program needn't handle non-finite values.
Results may differ from a plain program's by a relative error of at most 0.00015.
Values sent between devices are 32-bit elements; how exact they have to be, the bound alone decides.
No kernel may reach another device: no remote copies, remote signals or barrier semaphores. Data moves between devices by JAX's collectives and lax.ppermute only.
A program may use at most 128 MiB of HBM per device.

v0:
```python
import jax
import jax.numpy as jnp
from jax import lax
from jax.sharding import PartitionSpec as P

LEVELS = 3
SWEEPS = 1
COARSE_SWEEPS = 6
CG_ITERS = 2


DAMPING = 0.8
PRIOR_MASS = 0.5
PRIOR_STIFF = 1.0


def extended(x, sides, width):
    for axis, dim in sides:
        peers, length = (lax.axis_size(axis), x.shape[dim])
        up = [(i, (i + 1) % peers) for i in range(peers - 1)]
        down = [(j, i) for i, j in up]
        last = lax.slice_in_dim(x, length - width, length, axis=dim)
        leading = lax.slice_in_dim(x, 0, width, axis=dim)
        before = lax.ppermute(last, axis, up)
        after = lax.ppermute(leading, axis, down)
        x = jnp.concatenate([before, x, after], axis=dim)
    return x


def coarsen_sum(values):
    extent_x, extent_y, extent_z = values.shape
    blocks = values.reshape(extent_x // 2, 2, extent_y // 2, 2, extent_z // 2, 2)
    return blocks.sum(axis=(1, 3, 5))


def refine(values):
    return jnp.repeat(jnp.repeat(jnp.repeat(values, 2, axis=0), 2, axis=1), 2, axis=2)


def neighbours(padded):
    centre = padded[1:-1, 1:-1, :]
    border = jnp.zeros_like(centre[:, :, :1])
    beside = (
        padded[:-2, 1:-1, :],
        padded[2:, 1:-1, :],
        padded[1:-1, :-2, :],
        padded[1:-1, 2:, :],
        jnp.concatenate([border, centre[:, :, :-1]], axis=2),
        jnp.concatenate([centre[:, :, 1:], border], axis=2),
    )
    return (beside, centre)


def summed(entries):
    result = entries[0]
    for entry in entries[1:]:
        result = result + entry
    return result


def inside_flags(index_x, index_y, extent_x, extent_y, extent_z):
    index_z = jnp.arange(extent_z, dtype=jnp.int32)[None, None, :]
    return (
        index_x > 0,
        index_x < extent_x - 1,
        index_y > 0,
        index_y < extent_y - 1,
        index_z > 0,
        index_z < extent_z - 1,
    )


def face_weights(cond_padded, level_scale, interior):
    beside, centre = neighbours(cond_padded)
    return tuple(
        (
            level_scale * jnp.where(is_inner, 0.5 * (centre + neighbour), centre)
            for is_inner, neighbour in zip(interior, beside)
        )
    )


def apply_operator(padded, couplings, diagonal):
    beside, centre = neighbours(padded)
    return diagonal * centre - summed(
        [weight * neighbour for weight, neighbour in zip(couplings, beside)]
    )


def prior_apply(padded):
    beside, centre = neighbours(padded)
    return PRIOR_MASS * centre + PRIOR_STIFF * (6.0 * centre - summed(list(beside)))


def sensitivity(cond_padded, state_padded, probe_padded, interior):
    cond_side, cond_mid = neighbours(cond_padded)
    state_side, state_mid = neighbours(state_padded)
    probe_side, probe_mid = neighbours(probe_padded)
    flux_mid = cond_mid * probe_mid
    return summed(
        [
            jnp.where(is_inner, 0.5 * (flux_mid + cond_near * probe_near), flux_mid)
            * (state_mid - state_near)
            for is_inner, cond_near, probe_near, state_near in zip(
                interior, cond_side, probe_side, state_side
            )
        ]
    )


def misfit_gradient(cond_padded, state_padded, adjoint_padded, interior):
    cond_mid = neighbours(cond_padded)[1]
    state_side, state_mid = neighbours(state_padded)
    adjoint_side, adjoint_mid = neighbours(adjoint_padded)
    return cond_mid * summed(
        [
            jnp.where(is_inner, 0.5, 1.0) * (state_mid - state_near) * (adjoint_mid - adjoint_near)
            for is_inner, state_near, adjoint_near in zip(interior, state_side, adjoint_side)
        ]
    )


def smooth(iterate, source, couplings, diagonal, padder, sweeps):
    for sweep_index in range(sweeps):
        if iterate is None:
            iterate = DAMPING * source / diagonal
        else:
            iterate = (
                iterate
                + DAMPING
                * (source - apply_operator(padder(iterate), couplings, diagonal))
                / diagonal
            )
    return iterate


def vcycle(source, depth_index, operators, padders, coarse_solve):
    if depth_index == len(operators):
        return coarse_solve(source)
    couplings, diagonal = operators[depth_index]
    iterate = smooth(None, source, couplings, diagonal, padders[depth_index], SWEEPS)
    defect = source - apply_operator(padders[depth_index](iterate), couplings, diagonal)
    iterate = iterate + refine(
        vcycle(coarsen_sum(defect), depth_index + 1, operators, padders, coarse_solve)
    )
    return smooth(iterate, source, couplings, diagonal, padders[depth_index], SWEEPS)


def solve(source, operators, padders, coarse_solve):
    iterate = None
    iterate = vcycle(source, 0, operators, padders, coarse_solve)
    return iterate


def plain_pad(values):
    return jnp.pad(values, ((1, 1), (1, 1), (0, 0)))


def assemble(stacked, devices_x):
    pieces, extent_x, extent_y, extent_z = stacked.shape
    arranged = stacked.reshape(devices_x, pieces // devices_x, extent_x, extent_y, extent_z)
    return arranged.transpose(0, 2, 1, 3, 4).reshape(
        devices_x * extent_x, pieces // devices_x * extent_y, extent_z
    )


def norm_sum(residual):
    return lax.psum(jnp.sum(residual * residual), ("gx", "gy"))


def on_device(log_conductivity, state, gradient, prior_sample, sensor_cells, noise_precision):
    devices_x = lax.axis_size("gx")
    devices_y = lax.axis_size("gy")
    place_x = lax.axis_index("gx")
    place_y = lax.axis_index("gy")
    cells_x, cells_y, cells_z = log_conductivity.shape

    def fine_pad(values):
        return extended(values, (("gx", 0), ("gy", 1)), 1)

    def inner_pad(values):
        return extended(values, (("gx", 0), ("gy", 1)), 1)

    def local_flags(depth_index):
        factor = 2**depth_index
        extent_x = cells_x // factor
        extent_y = cells_y // factor
        index_x = place_x * extent_x + jnp.arange(extent_x, dtype=jnp.int32)[:, None, None]
        index_y = place_y * extent_y + jnp.arange(extent_y, dtype=jnp.int32)[None, :, None]
        return inside_flags(
            index_x, index_y, extent_x * devices_x, extent_y * devices_y, cells_z // factor
        )

    cond_levels = [jnp.exp(log_conductivity)]
    for depth_index in range(LEVELS - 1):
        cond_levels.append(coarsen_sum(cond_levels[-1]) / 8.0)
    padders = [fine_pad] + [inner_pad] * (LEVELS - 2)
    operators = []
    cond_padded = None
    for depth_index in range(LEVELS - 1):
        level_padded = padders[depth_index](cond_levels[depth_index])
        if depth_index == 0:
            cond_padded = level_padded
        couplings = face_weights(level_padded, float(2**depth_index), local_flags(depth_index))
        operators.append((couplings, summed(list(couplings))))
    coarsest = LEVELS - 1
    extent_x, extent_y, extent_z = cond_levels[coarsest].shape
    cond_whole = assemble(
        lax.all_gather(cond_levels[coarsest][None], ("gx", "gy"), axis=0, tiled=True), devices_x
    )
    whole_flags = inside_flags(
        jnp.arange(extent_x * devices_x, dtype=jnp.int32)[:, None, None],
        jnp.arange(extent_y * devices_y, dtype=jnp.int32)[None, :, None],
        extent_x * devices_x,
        extent_y * devices_y,
        extent_z,
    )
    coarse_couplings = face_weights(plain_pad(cond_whole), float(2**coarsest), whole_flags)
    coarse_diagonal = summed(list(coarse_couplings))

    def coarse_solve(source):
        gathered = assemble(
            lax.all_gather(source[None], ("gx", "gy"), axis=0, tiled=True), devices_x
        )
        answer = smooth(None, gathered, coarse_couplings, coarse_diagonal, plain_pad, COARSE_SWEEPS)
        return lax.dynamic_slice(
            answer,
            (place_x * extent_x, place_y * extent_y, place_x * 0),
            (extent_x, extent_y, extent_z),
        )

    fine_flags = local_flags(0)
    rows_all = cells_y * devices_y
    sensor_row = sensor_cells // (rows_all * cells_z)
    sensor_column = sensor_cells // cells_z % rows_all
    sensor_depth = sensor_cells % cells_z
    local_cell = (
        (sensor_row - place_x * cells_x) * cells_y + (sensor_column - place_y * cells_y)
    ) * cells_z + sensor_depth
    weight_field = (
        jnp.zeros((cells_x * cells_y * cells_z,), jnp.float32).at[local_cell].add(noise_precision)
    )
    weight_field = weight_field.reshape(cells_x, cells_y, cells_z)
    state_padded = fine_pad(state)
    source = prior_apply(fine_pad(prior_sample)) - gradient
    step_field = jnp.zeros_like(source)
    residual = source
    direction = residual
    norm_now = norm_sum(residual)
    for iteration in range(CG_ITERS):
        direction_padded = fine_pad(direction)
        change = solve(
            sensitivity(cond_padded, state_padded, direction_padded, fine_flags),
            operators,
            padders,
            coarse_solve,
        )
        adjoint = solve(weight_field * change, operators, padders, coarse_solve)
        curved = misfit_gradient(
            cond_padded, state_padded, fine_pad(adjoint), fine_flags
        ) + prior_apply(direction_padded)
        step_length = norm_now / lax.psum(jnp.sum(direction * curved), ("gx", "gy"))
        step_field = step_field + step_length * direction
        residual = residual - step_length * curved
        if iteration + 1 < CG_ITERS:
            norm_next = norm_sum(residual)
            direction = residual + norm_next / norm_now * direction
            norm_now = norm_next
    return (step_field, residual)


def solution(mesh):
    placed = (
        P(("ens", "gx"), "gy", None),
        P(("ens", "gx"), "gy", None),
        P(("ens", "gx"), "gy", None),
        P(("ens", "gx"), "gy", None),
        P(("ens", "gx", "gy")),
        P(("ens", "gx", "gy")),
    )
    return jax.shard_map(
        on_device,
        mesh=mesh,
        in_specs=placed,
        out_specs=(P(("ens", "gx"), "gy", None), P(("ens", "gx"), "gy", None)),
        check_vma=False,
    )
```

profile of v0, /device:TPU:0, one launch (start us, length us, event | category | flops | bytes accessed | tf_op | source)
XLA Modules:
  0.0 712.4 jit_solution(8180663991162468907)
XLA Ops:
  6.0 5.1 collective-permute-start.5
  19.7 9.7 %reshape.259 = f32[4,2,8,2,128,2]{5,4,3,2,1,0:T(8,128)} reshape(f32[8,16,256]{2,1,0:T(8,128)S(1)} %exp.3) | data formatting | bytes 262144 | tf_op jit(solution)/shard_map/reshape | solution.py:32
  38.8 31.3 %all-gather.1 = f32[32,4,64]{2,1,0:T(4,128)S(1)} all-gather(f32[2,4,64]{2,1,0:T(4,128)S(1)} %broadcast_multiply_fusion.1), channel_id=3, replica_groups=mesh['ens'=2,'gx'=4,'gy'=4] {'gx','gy'}, dimensions={0}, use_global_device_ids=true | all-gather | bytes 34816 | tf_op jit(solution)/shard_map/all_gather | solution.py:209
  74.8 4.5 collective-permute-start.10
  90.1 4.5 collective-permute-start.11
  96.1 6.0 collective-permute-start.20
  104.1 5.1 collective-permute-start.16
  110.5 4.5 collective-permute-start.22
  116.4 4.5 collective-permute-start.18
  126.9 9.7 %reshape.258 = f32[4,2,8,2,128,2]{5,4,3,2,1,0:T(8,128)} reshape(f32[8,16,256]{2,1,0:T(8,128)S(1)} %fusion.126) | data formatting | bytes 262144 | tf_op jit(solution)/shard_map/reshape | solution.py:32
  159.0 29.9 %all-gather = f32[32,4,64]{2,1,0:T(4,128)S(1)} all-gather(f32[2,4,64]{2,1,0:T(4,128)S(1)} %reduce_sum.129), channel_id=2, replica_groups=mesh['ens'=2,'gx'=4,'gy'=4] {'gx','gy'}, dimensions={0}, use_global_device_ids=true | all-gather | bytes 34816 | tf_op jit(solution)/shard_map/all_gather | solution.py:223
  230.2 4.4 collective-permute-done.37
  243.1 9.7 %reshape.271 = f32[4,2,8,2,128,2]{5,4,3,2,1,0:T(8,128)} reshape(f32[8,16,256]{2,1,0:T(8,128)S(1)} %fusion.100) | data formatting | bytes 262144 | tf_op jit(solution)/shard_map/reshape | solution.py:32
  272.5 28.9 %all-gather.2 = f32[32,4,64]{2,1,0:T(4,128)S(1)} all-gather(f32[2,4,64]{2,1,0:T(4,128)S(1)} %reduce_sum.132), channel_id=4, replica_groups=mesh['ens'=2,'gx'=4,'gy'=4] {'gx','gy'}, dimensions={0}, use_global_device_ids=true | all-gather | bytes 34816 | tf_op jit(solution)/shard_map/all_gather | solution.py:223
  354.7 30.3 %all-reduce.111 = (f32[]{:T(128)}, f32[]{:T(128)}) all-reduce(f32[]{:T(128)} %get-tuple-element.5, f32[]{:T(128)} %get-tuple-element.4), channel_id=1, replica_groups=mesh['ens'=2,'gx'=4,'gy'=4] {'gx','gy'}, use_global_device_ids=true, to_apply=%region_1.0 | all-reduce | flops 2 | bytes 16 | tf_op jit(solution)/shard_map/psum | solution.py:168
  387.0 32.6 %psum.30 = f32[]{:T(128)} all-reduce(f32[]{:T(128)} %multiply_reduce_fusion.1), channel_id=1, replica_groups=mesh['ens'=2,'gx'=4,'gy'=4] {'gx','gy'}, use_global_device_ids=true, to_apply=%region_12.13 | all-reduce | flops 1 | bytes 8 | tf_op jit(solution)/shard_map/psum | solution.py:168
  423.5 4.3 collective-permute-done.57
  452.3 9.7 %reshape.281 = f32[4,2,8,2,128,2]{5,4,3,2,1,0:T(8,128)} reshape(f32[8,16,256]{2,1,0:T(8,128)S(1)} %fusion.60) | data formatting | bytes 262144 | tf_op jit(solution)/shard_map/reshape | solution.py:32
  481.8 28.9 %all-gather.3 = f32[32,4,64]{2,1,0:T(4,128)S(1)} all-gather(f32[2,4,64]{2,1,0:T(4,128)S(1)} %reduce_sum.136), channel_id=5, replica_groups=mesh['ens'=2,'gx'=4,'gy'=4] {'gx','gy'}, dimensions={0}, use_global_device_ids=true | all-gather | bytes 34816 | tf_op jit(solution)/shard_map/all_gather | solution.py:223
  515.4 4.3 collective-permute-done.69
  563.0 9.7 %reshape.291 = f32[4,2,8,2,128,2]{5,4,3,2,1,0:T(8,128)} reshape(f32[8,16,256]{2,1,0:T(8,128)S(1)} %fusion.34) | data formatting | bytes 262144 | tf_op jit(solution)/shard_map/reshape | solution.py:32
  594.5 29.3 %all-gather.4 = f32[32,4,64]{2,1,0:T(4,128)S(1)} all-gather(f32[2,4,64]{2,1,0:T(4,128)} %reduce_sum.138), channel_id=6, replica_groups=mesh['ens'=2,'gx'=4,'gy'=4] {'gx','gy'}, dimensions={0}, use_global_device_ids=true | all-gather | bytes 34816 | tf_op jit(solution)/shard_map/all_gather | solution.py:223
  629.4 4.3 collective-permute-done.85
  680.0 30.3 %psum.31 = f32[]{:T(128)} all-reduce(f32[]{:T(128)} %get-tuple-element.8), channel_id=1, replica_groups=mesh['ens'=2,'gx'=4,'gy'=4] {'gx','gy'}, use_global_device_ids=true, to_apply=%region_18.19 | all-reduce | flops 1 | bytes 8 | tf_op jit(solution)/shard_map/psum | solution.py:262
  (570 shorter events, 362.7 us)
Async XLA Ops:
  1.4 68.9 %collective-permute-start = (f32[1,16,256]{2,1,0:T(8,128)S(1)}, f32[1,16,256]{2,1,0:T(8,128)S(1)}, u32[]{:S(2)}, u32[]{:S(2)}) collective-permute-start(f32[1,16,256]{2,1,0:T(8,128)S(1)} %get-tuple-element.130), channel_id=1, source_target_pairs={{0,4},{4,8},{8,12},{1,5},{5,9},{9,13},{2,6},{6,10},{10,14},{3,7},{... | collective-permute-start | bytes 49160 | tf_op jit(solution)/shard_map/ppermute | solution.py:24
  3.8 67.9 %collective-permute-start.1 = (f32[1,16,256]{2,1,0:T(8,128)S(1)}, f32[1,16,256]{2,1,0:T(8,128)S(1)}, u32[]{:S(2)}, u32[]{:S(2)}) collective-permute-start(f32[1,16,256]{2,1,0:T(8,128)S(1)} %get-tuple-element.129), channel_id=1, source_target_pairs={{4,0},{8,4},{12,8},{5,1},{9,5},{13,9},{6,2},{10,6},{14,10},{7,3},{... | collective-permute-start | bytes 49160 | tf_op jit(solution)/shard_map/ppermute | solution.py:25
  6.0 67.4 %collective-permute-start.5 = (f32[1,16,256]{2,1,0:T(8,128)S(1)}, f32[1,16,256]{2,1,0:T(8,128)S(1)}, u32[]{:S(2)}, u32[]{:S(2)}) collective-permute-start(f32[1,16,256]{2,1,0:T(8,128)S(1)} %get-tuple-element.121), channel_id=1, source_target_pairs={{0,4},{4,8},{8,12},{1,5},{5,9},{9,13},{2,6},{6,10},{10,14},{3,7},{... | collective-permute-start | bytes 49160 | tf_op jit(solution)/shard_map/ppermute | solution.py:24
  11.1 63.6 %collective-permute-start.7 = (f32[1,16,256]{2,1,0:T(8,128)S(1)}, f32[1,16,256]{2,1,0:T(8,128)S(1)}, u32[]{:S(2)}, u32[]{:S(2)}) collective-permute-start(f32[1,16,256]{2,1,0:T(8,128)S(1)} %get-tuple-element.122), channel_id=1, source_target_pairs={{4,0},{8,4},{12,8},{5,1},{9,5},{13,9},{6,2},{10,6},{14,10},{7,3},{... | collective-permute-start | bytes 49160 | tf_op jit(solution)/shard_map/ppermute | solution.py:25
  13.2 66.2 %collective-permute-start.4 = (f32[1,16,256]{2,1,0:T(8,128)S(1)}, f32[1,16,256]{2,1,0:T(8,128)S(1)}, u32[]{:S(2)}, u32[]{:S(2)}) collective-permute-start(f32[1,16,256]{2,1,0:T(8,128)S(1)} %get-tuple-element.116), channel_id=1, source_target_pairs={{0,4},{4,8},{8,12},{1,5},{5,9},{9,13},{2,6},{6,10},{10,14},{3,7},{... | collective-permute-start | bytes 49160 | tf_op jit(solution)/shard_map/ppermute | solution.py:24
  70.3 10.4 %collective-permute-start.9 = (f32[1,16,256]{2,1,0:T(8,128)S(1)}, f32[1,16,256]{2,1,0:T(8,128)S(1)}, u32[]{:S(2)}, u32[]{:S(2)}) collective-permute-start(f32[1,16,256]{2,1,0:T(8,128)S(1)} %get-tuple-element.115), channel_id=1, source_target_pairs={{4,0},{8,4},{12,8},{5,1},{9,5},{13,9},{6,2},{10,6},{14,10},{7,3},{... | collective-permute-start | bytes 49160 | tf_op jit(solution)/shard_map/ppermute | solution.py:25
  71.7 9.0 %collective-permute-start.2 = (f32[10,1,256]{2,1,0:T(1,128)S(1)}, f32[10,1,256]{2,1,0:T(1,128)S(1)}, u32[]{:S(2)}, u32[]{:S(2)}) collective-permute-start(f32[10,1,256]{2,1,0:T(1,128)S(1)} %get-tuple-element.67), channel_id=1, source_target_pairs={{0,1},{1,2},{2,3},{4,5},{5,6},{6,7},{8,9},{9,10},{10,11},{12,13},{... | collective-permute-start | bytes 30728 | tf_op jit(solution)/shard_map/ppermute | solution.py:24
  73.4 7.3 %collective-permute-start.3 = (f32[10,1,256]{2,1,0:T(1,128)S(1)}, f32[10,1,256]{2,1,0:T(1,128)S(1)}, u32[]{:S(2)}, u32[]{:S(2)}) collective-permute-start(f32[10,1,256]{2,1,0:T(1,128)S(1)} %get-tuple-element.68), channel_id=1, source_target_pairs={{1,0},{2,1},{3,2},{5,4},{6,5},{7,6},{9,8},{10,9},{11,10},{13,12},{... | collective-permute-start | bytes 30728 | tf_op jit(solution)/shard_map/ppermute | solution.py:25
  74.8 19.8 %collective-permute-start.10 = (f32[10,1,256]{2,1,0:T(1,128)S(1)}, f32[10,1,256]{2,1,0:T(1,128)S(1)}, u32[]{:S(2)}, u32[]{:S(2)}) collective-permute-start(f32[10,1,256]{2,1,0:T(1,128)S(1)} %get-tuple-element.64), channel_id=1, source_target_pairs={{0,1},{1,2},{2,3},{4,5},{5,6},{6,7},{8,9},{9,10},{10,11},{12,13},{... | collective-permute-start | bytes 30728 | tf_op jit(solution)/shard_map/ppermute | solution.py:24
  79.4 16.7 %collective-permute-start.13 = (f32[10,1,256]{2,1,0:T(1,128)S(1)}, f32[10,1,256]{2,1,0:T(1,128)S(1)}, u32[]{:S(2)}, u32[]{:S(2)}) collective-permute-start(f32[10,1,256]{2,1,0:T(1,128)S(1)} %get-tuple-element.63), channel_id=1, source_target_pairs={{1,0},{2,1},{3,2},{5,4},{6,5},{7,6},{9,8},{10,9},{11,10},{13,12},{... | collective-permute-start | bytes 30728 | tf_op jit(solution)/shard_map/ppermute | solution.py:25
  80.9 7.8 %collective-permute-start.6 = (f32[1,16,256]{2,1,0:T(8,128)S(1)}, f32[1,16,256]{2,1,0:T(8,128)S(1)}, u32[]{:S(2)}, u32[]{:S(2)}) collective-permute-start(f32[1,16,256]{2,1,0:T(8,128)S(1)} %get-tuple-element.123), channel_id=1, source_target_pairs={{0,4},{4,8},{8,12},{1,5},{5,9},{9,13},{2,6},{6,10},{10,14},{3,7},{... | collective-permute-start | bytes 49160 | tf_op jit(solution)/shard_map/ppermute | solution.py:24
  83.1 6.9 collective-permute-start.8
  84.4 17.7 %collective-permute-start.12 = (f32[10,1,256]{2,1,0:T(1,128)S(1)}, f32[10,1,256]{2,1,0:T(1,128)S(1)}, u32[]{:S(2)}, u32[]{:S(2)}) collective-permute-start(f32[10,1,256]{2,1,0:T(1,128)S(1)} %get-tuple-element.61), channel_id=1, source_target_pairs={{0,1},{1,2},{2,3},{4,5},{5,6},{6,7},{8,9},{9,10},{10,11},{12,13},{... | collective-permute-start | bytes 30728 | tf_op jit(solution)/shard_map/ppermute | solution.py:24
  88.7 14.7 %collective-permute-start.15 = (f32[10,1,256]{2,1,0:T(1,128)S(1)}, f32[10,1,256]{2,1,0:T(1,128)S(1)}, u32[]{:S(2)}, u32[]{:S(2)}) collective-permute-start(f32[10,1,256]{2,1,0:T(1,128)S(1)} %get-tuple-element.62), channel_id=1, source_target_pairs={{1,0},{2,1},{3,2},{5,4},{6,5},{7,6},{9,8},{10,9},{11,10},{13,12},{... | collective-permute-start | bytes 30728 | tf_op jit(solution)/shard_map/ppermute | solution.py:25
  90.1 13.4 %collective-permute-start.11 = (f32[10,1,256]{2,1,0:T(1,128)S(1)}, f32[10,1,256]{2,1,0:T(1,128)S(1)}, u32[]{:S(2)}, u32[]{:S(2)}) collective-permute-start(f32[10,1,256]{2,1,0:T(1,128)S(1)} %get-tuple-element.65), channel_id=1, source_target_pairs={{0,1},{1,2},{2,3},{4,5},{5,6},{6,7},{8,9},{9,10},{10,11},{12,13},{... | collective-permute-start | bytes 30728 | tf_op jit(solution)/shard_map/ppermute | solution.py:24
  94.6 8.8 %collective-permute-start.14 = (f32[10,1,256]{2,1,0:T(1,128)S(1)}, f32[10,1,256]{2,1,0:T(1,128)S(1)}, u32[]{:S(2)}, u32[]{:S(2)}) collective-permute-start(f32[10,1,256]{2,1,0:T(1,128)S(1)} %get-tuple-element.66), channel_id=1, source_target_pairs={{1,0},{2,1},{3,2},{5,4},{6,5},{7,6},{9,8},{10,9},{11,10},{13,12},{... | collective-permute-start | bytes 30728 | tf_op jit(solution)/shard_map/ppermute | solution.py:25
  96.1 14.4 %collective-permute-start.20 = (f32[1,8,128]{2,1,0:T(8,128)S(1)}, f32[1,8,128]{2,1,0:T(8,128)S(1)}, u32[]{:S(2)}, u32[]{:S(2)}) collective-permute-start(f32[1,8,128]{2,1,0:T(8,128)S(1)} %get-tuple-element.225), channel_id=1, source_target_pairs={{0,4},{4,8},{8,12},{1,5},{5,9},{9,13},{2,6},{6,10},{10,14},{3,7},{... | collective-permute-start | bytes 12296 | tf_op jit(solution)/shard_map/ppermute | solution.py:24
  102.1 8.4 %collective-permute-start.21 = (f32[1,8,128]{2,1,0:T(8,128)S(1)}, f32[1,8,128]{2,1,0:T(8,128)S(1)}, u32[]{:S(2)}, u32[]{:S(2)}) collective-permute-start(f32[1,8,128]{2,1,0:T(8,128)S(1)} %get-tuple-element.226), channel_id=1, source_target_pairs={{4,0},{8,4},{12,8},{5,1},{9,5},{13,9},{6,2},{10,6},{14,10},{7,3},{... | collective-permute-start | bytes 12296 | tf_op jit(solution)/shard_map/ppermute | solution.py:25
  104.1 12.3 %collective-permute-start.16 = (f32[1,16,256]{2,1,0:T(8,128)S(1)}, f32[1,16,256]{2,1,0:T(8,128)S(1)}, u32[]{:S(2)}, u32[]{:S(2)}) collective-permute-start(f32[1,16,256]{2,1,0:T(8,128)S(1)} %get-tuple-element.113), channel_id=1, source_target_pairs={{0,4},{4,8},{8,12},{1,5},{5,9},{9,13},{2,6},{6,10},{10,14},{3,7},{... | collective-permute-start | bytes 49160 | tf_op jit(solution)/shard_map/ppermute | solution.py:24
  109.2 7.2 %collective-permute-start.17 = (f32[1,16,256]{2,1,0:T(8,128)S(1)}, f32[1,16,256]{2,1,0:T(8,128)S(1)}, u32[]{:S(2)}, u32[]{:S(2)}) collective-permute-start(f32[1,16,256]{2,1,0:T(8,128)S(1)} %get-tuple-element.114), channel_id=1, source_target_pairs={{4,0},{8,4},{12,8},{5,1},{9,5},{13,9},{6,2},{10,6},{14,10},{7,3},{... | collective-permute-start | bytes 49160 | tf_op jit(solution)/shard_map/ppermute | solution.py:25
  110.5 30.2 %collective-permute-start.22 = (f32[6,1,128]{2,1,0:T(1,128)S(1)}, f32[6,1,128]{2,1,0:T(1,128)S(1)}, u32[]{:S(2)}, u32[]{:S(2)}) collective-permute-start(f32[6,1,128]{2,1,0:T(1,128)S(1)} %get-tuple-element.190), channel_id=1, source_target_pairs={{0,1},{1,2},{2,3},{4,5},{5,6},{6,7},{8,9},{9,10},{10,11},{12,13},{... | collective-permute-start | bytes 9224 | tf_op jit(solution)/shard_map/ppermute | solution.py:24
  115.1 25.7 %collective-permute-start.23 = (f32[6,1,128]{2,1,0:T(1,128)S(1)}, f32[6,1,128]{2,1,0:T(1,128)S(1)}, u32[]{:S(2)}, u32[]{:S(2)}) collective-permute-start(f32[6,1,128]{2,1,0:T(1,128)S(1)} %get-tuple-element.189), channel_id=1, source_target_pairs={{1,0},{2,1},{3,2},{5,4},{6,5},{7,6},{9,8},{10,9},{11,10},{13,12},{... | collective-permute-start | bytes 9224 | tf_op jit(solution)/shard_map/ppermute | solution.py:25
  143.3 6.3 collective-permute-start.25
  209.3 8.6 %collective-permute-start.32 = (f32[1,16,256]{2,1,0:T(8,128)S(1)}, f32[1,16,256]{2,1,0:T(8,128)S(1)}, u32[]{:S(2)}, u32[]{:S(2)}) collective-permute-start(f32[1,16,256]{2,1,0:T(8,128)S(1)} %get-tuple-element.107), channel_id=1, source_target_pairs={{0,4},{4,8},{8,12},{1,5},{5,9},{9,13},{2,6},{6,10},{10,14},{3,7},{... | collective-permute-start | bytes 49160 | tf_op jit(solution)/shard_map/ppermute | solution.py:24
  (139 other events, 3398.1 us)
where the time goes:
time: 717 us; the launch traced here: 712 us
  blocking collectives  242 us (34%)
  starting transfers between devices  199 us (28%)
  waiting for transfers between devices  135 us (19%)
  local copies, waits for them, and re-layouts  75.6 us (11%)
  other arithmetic  53.2 us (7%)
  between operations  7.76 us (1%)
    ppermute x48, starting transfers between devices, extended(): before = lax.ppermute(last, axis, up)  137 us
    ppermute x48, waiting for transfers between devices, extended(): after = lax.ppermute(leading, axis, down)  135 us
    all_gather x4, blocking collectives, coarse_solve(): lax.all_gather(source[None], ('gx', 'gy'), axis=0, tiled=True)  117 us
    psum x2, blocking collectives, norm_sum(): return lax.psum(jnp.sum(residual * residual), ('gx', 'gy'))  62.9 us
    ppermute x48, starting transfers between devices, extended(): after = lax.ppermute(leading, axis, down)  62.4 us
    reshape x9, local copies, waits for them, and re-layouts, coarsen_sum(): values.reshape(extent_x // 2, 2, extent_y // 2, 2, extent_z // 2, 2)  53.3 us
    all_gather x1, blocking collectives, on_device(): lax.all_gather(cond_levels[coarsest][None], ('gx', 'gy'), axis=0, tiled=T...  31.3 us
    psum x1, blocking collectives, on_device(): step_length = norm_now / lax.psum(jnp.sum(direction * curved), ('gx', 'gy'))  30.3 us
  transfers between devices with their start and end apart: 96, of which 36 were waited for; matrix products, arithmetic and copies ran while one was open for 6% of the time, Pallas kernels for 0%

commit v1 on v0

v1 whole, which is shorter than its diff:
```python
import jax
import jax.numpy as jnp
from jax import lax
from jax.experimental import pallas as pl
from jax.experimental.pallas import tpu as pltpu
from jax.sharding import PartitionSpec as P

DAMPING = 0.8
KEPT = 0.2
PRIOR_MASS = 0.5
COARSE_SWEEPS = 6
HALO = 4
DEEP = 5
WIDE = 2
VMEM_LIMIT = 24 * 1024 * 1024
EXACT = lax.Precision.HIGHEST


def rotate(x, axis, shift):
    size = lax.axis_size(axis)
    return lax.ppermute(x, axis, [(i, (i + shift) % size) for i in range(size)])


def shifted(v, step, dim):
    size = v.shape[dim]
    return pltpu.roll(v, step % size, dim)


def dot(a, b):
    return lax.dot_general(
        a, b, (((1,), (0,)), ((), ())), precision=EXACT, preferred_element_type=jnp.float32
    )


def iota(shape, dim):
    return lax.broadcasted_iota(jnp.int32, shape, dim)


def total(tile):
    return jnp.sum(jnp.sum(tile, axis=1, keepdims=True), axis=0, keepdims=True)


def fold(plane):
    rows, lanes = plane.shape
    parts = [
        plane[r : r + 8, c : c + 128] for r in range(0, rows, 8) for c in range(0, lanes, 128)
    ]
    out = parts[0]
    for part in parts[1:]:
        out = out + part
    return out


def z_pairs(lanes):
    half = lanes // 2
    return (iota((lanes, half), 0) // 2 == iota((lanes, half), 1)).astype(jnp.float32)


def z_copies(lanes):
    return (iota((lanes, 2 * lanes), 0) == iota((lanes, 2 * lanes), 1) // 2).astype(jnp.float32)


def restrict_rows(planes, first_row, rows):
    extent = planes[0].shape[0]
    here = iota(planes[0].shape, 0)
    inside = (here >= first_row) & (here < first_row + rows)
    pick = (
        (iota((rows // 2, extent), 1) - first_row + 2) // 2 - 1 == iota((rows // 2, extent), 0)
    ).astype(jnp.float32)
    halves = []
    for x in range(0, len(planes), 2):
        pair = jnp.where(inside, planes[x] + planes[x + 1], 0.0)
        halves.append(dot(pick, pair))
    packed = dot(jnp.concatenate(halves, axis=0), z_pairs(planes[0].shape[1]))
    return packed.reshape(len(planes) // 2, rows // 2, packed.shape[1])


def swap_sum(v, dim, stride):
    even = (iota(v.shape, dim) // stride) % 2 == 0
    return v + jnp.where(even, shifted(v, -stride, dim), shifted(v, stride, dim))


def off_diagonal(v, low, high, fx, fx_high, fy, fz, step):
    out = fy * shifted(v, step, 0) + shifted(fy * v, -step, 0)
    out = out + (fz * shifted(v, step, 1) + shifted(fz * v, -step, 1))
    if low is not None:
        out = out + fx * low
    if high is not None:
        out = out + fx_high * high
    return out


def coefficients(planes, scale, step, x_mask, y_mask, z_mask, outside):
    count = len(planes)
    faces = [None] * count
    for x in range(count):
        low = planes[x] if x == 0 else planes[x - 1]
        faces[x] = (scale * x_mask(x)) * (0.5 * (planes[x] + low))
    out = []
    for x in range(count):
        k = planes[x]
        fy = (scale * y_mask) * (0.5 * (k + shifted(k, step, 0)))
        fz = (scale * z_mask) * (0.5 * (k + shifted(k, step, 1)))
        diag = (scale * outside(x)) * k + fy + shifted(fy, -step, 0) + fz + shifted(fz, -step, 1)
        diag = diag + faces[x]
        if x + 1 < count:
            diag = diag + faces[x + 1]
        out.append((faces[x], fy, fz, DAMPING / diag))
    return out


def flag(condition):
    return jnp.where(condition, 1.0, 0.0).astype(jnp.float32)


def place_blocks(refs, place, sizes, planes, rows, put):
    size_x, size_y = sizes
    for s in range(size_x):
        at_x = lax.rem(place[0] - s + size_x, size_x)
        for t in range(size_y):
            at_y = lax.rem(place[1] - t + size_y, size_y)
            put(at_x, at_y, refs[s], t)


def placed_whole(refs, place, sizes, planes, per, whole_ref):
    block_rows = whole_ref.shape[1] // sizes[1]

    def put(at_x, at_y, ref, t):
        row = pl.multiple_of(at_y * block_rows, block_rows)
        for x in range(planes):
            whole_ref[at_x * planes + x, pl.ds(row, block_rows), :] = ref[t * per + x]

    place_blocks(refs, place, sizes, planes, block_rows, put)


def summed_tiles(refs, sizes, per, index):
    tile = None
    for s in range(sizes[0]):
        for t in range(sizes[1]):
            part = refs[s][t * per + index]
            tile = part if tile is None else tile + part
    return total(tile)


def coarse_correction(source, mid, out, level1, level2):
    fx1, fy1, fz1, rd1 = level1
    fx2, fy2, fz2, rd2 = level2
    count = source.shape[0]

    def off1(ref, x):
        low = ref[x - 1] if x > 0 else None
        high = ref[x + 1] if x + 1 < count else None
        fx_high = fx1[x + 1] if x + 1 < count else None
        return off_diagonal(ref[x], low, high, fx1[x], fx_high, fy1[x], fz1[x], 1)

    for x in range(count):
        mid[x] = rd1[x] * source[x]
    coarse = []
    for x in range(0, count, 2):
        pair = KEPT * (source[x] + source[x + 1]) + (off1(mid, x) + off1(mid, x + 1))
        coarse.append(swap_sum(swap_sum(pair, 0, 1), 1, 1))
    half = count // 2
    iterate = [rd2[x] * coarse[x] for x in range(half)]
    for sweep in range(COARSE_SWEEPS - 1):
        new = []
        for x in range(half):
            low = iterate[x - 1] if x > 0 else None
            high = iterate[x + 1] if x + 1 < half else None
            fx_high = fx2[x + 1] if x + 1 < half else None
            off = off_diagonal(iterate[x], low, high, fx2[x], fx_high, fy2[x], fz2[x], 2)
            new.append(KEPT * iterate[x] + rd2[x] * (coarse[x] + off))
        iterate = new
    for x in range(count):
        mid[x] = mid[x] + iterate[x // 2]
    for x in range(count):
        out[x] = KEPT * mid[x] + rd1[x] * (source[x] + off1(mid, x))


def prolonged(whole_ref, place, planes, rows, pad):
    count, extent, lanes = whole_ref.shape
    own_x = planes - 2 * (pad // 2)
    own_y = (rows - 2 * pad) // 2
    first = place[1] * own_y - pad // 2
    pick = (iota((rows, extent), 1) == first + iota((rows, extent), 0) // 2).astype(jnp.float32)
    parts = []
    for x in range(planes):
        at = jnp.clip(place[0] * own_x - pad // 2 + x, 0, count - 1)
        parts.append(dot(pick, whole_ref[at]))
    wide = dot(jnp.concatenate(parts, axis=0), z_copies(lanes))
    return [wide[x * rows : (x + 1) * rows] for x in range(planes)]


def frame_masks(place, shape, pad, sizes):
    planes, rows, lanes = shape
    own_x, own_y = planes - 2 * pad, rows - 2 * pad
    all_x, all_y = own_x * sizes[0], own_y * sizes[1]
    base_x, base_y = place[0] * own_x - pad, place[1] * own_y - pad
    at_y = base_y + iota((rows, lanes), 0)
    at_z = iota((rows, lanes), 1)
    y_mask = flag((at_y >= 1) & (at_y < all_y))
    z_mask = flag(at_z >= 1)
    edges = flag(at_y == 0) + flag(at_y == all_y - 1) + flag(at_z == 0) + flag(at_z == lanes - 1)

    def x_mask(x):
        at = base_x + x
        return flag((at >= 1) & (at < all_x))

    def outside(x):
        at = base_x + x
        return edges + (flag(at == 0) + flag(at == all_x - 1))

    return x_mask, y_mask, z_mask, outside


def prior_rows(center, low, high, up, down, x_low, x_high, y_mask, z_mask, outside):
    rows, lanes = center.shape
    y_next = shifted(y_mask, -1, 0)
    z_next = shifted(z_mask, -1, 1)
    out = (PRIOR_MASS + outside) * center + x_low * (center - low) + x_high * (center - high)
    out = out + y_mask * (center - up) + y_next * (center - down)
    out = out + z_mask * (center - shifted(center, 1, 1))
    return out + z_next * (center - shifted(center, -1, 1))


def fine_restricted(base, fields, fx, fy, fz, out_ref, first, own):
    planes = []
    for x in range(first, first + own):
        off = off_diagonal(
            fields[x], fields[x - 1], fields[x + 1], fx[x], fx[x + 1], fy[x], fz[x], 1
        )
        planes.append(KEPT * base[x] + off)
    rows = planes[0].shape[0]
    coarse = restrict_rows(planes, first, rows - 2 * first)
    for x in range(coarse.shape[0]):
        out_ref[x] = coarse[x]


def sensitivity_planes(q, hux, huy, huz, nbu, first, last):
    faces = {x: hux[x] * (q(x) + q(x - 1)) for x in range(first, last + 1)}
    out = {}
    for x in range(first, last):
        mid = q(x)
        along_y = huy[x] * (mid + shifted(mid, 1, 0))
        along_z = huz[x] * (mid + shifted(mid, 1, 1))
        z = faces[x] - faces[x + 1] + nbu[x] * mid
        z = z + (along_y - shifted(along_y, -1, 0))
        out[x] = z + (along_z - shifted(along_z, -1, 1))
    return out


def first_residual_stage(z, fx, fy, fz, rd, z_ref, out_ref, planes):
    for x in z:
        z_ref[x] = z[x]
    iterate = {x: rd[x] * z[x] for x in range(HALO - 1, planes - HALO + 1)}
    fine_restricted(z, iterate, fx, fy, fz, out_ref, HALO, planes - 2 * HALO)


def call(kernel, outs, scratch, inputs, smem_first=True):
    vmem = pl.BlockSpec(memory_space=pltpu.VMEM)
    smem = pl.BlockSpec(memory_space=pltpu.SMEM)
    return pl.pallas_call(
        kernel,
        out_shape=[jax.ShapeDtypeStruct(shape, jnp.float32) for shape in outs],
        in_specs=[smem if smem_first and i == 0 else vmem for i in range(len(inputs))],
        out_specs=[vmem] * len(outs),
        scratch_shapes=[pltpu.VMEM(shape, jnp.float32) for shape in scratch],
        compiler_params=pltpu.CompilerParams(vmem_limit_bytes=VMEM_LIMIT),
    )(*inputs)


def own_coarse_conductivity(log_cond):
    def kernel(log_ref, out_ref):
        planes = [jnp.exp(log_ref[x]) for x in range(log_ref.shape[0])]
        coarse = restrict_rows(planes, 0, planes[0].shape[0])
        for x in range(coarse.shape[0]):
            out_ref[x] = coarse[x] * 0.125

    x, y, z = log_cond.shape
    return call(kernel, [(x // 2, y // 2, z // 2)], [], [log_cond], smem_first=False)[0]


def gathered(own):
    size_x, size_y = lax.axis_size("gx"), lax.axis_size("gy")
    row = jnp.concatenate([own] + [rotate(own, "gy", t) for t in range(1, size_y)], axis=0)
    return [row] + [rotate(row, "gx", s) for s in range(1, size_x)]


FIELD_DEPTHS = (DEEP, HALO, HALO, HALO, WIDE)


def setup_rows(own_x):
    starts, at = [], 0
    for depth in FIELD_DEPTHS:
        starts.append(at)
        at += (own_x + 2 * depth) * depth
    return starts, -(-at // 8) * 8


def field_plane(fields, low, high, index, x):
    depth = FIELD_DEPTHS[index]
    start = sum(FIELD_DEPTHS[:index])
    own = fields[index].shape[0]
    if x < depth:
        return low[start + x]
    if x < depth + own:
        return fields[index][x - depth]
    return high[start + x - depth - own]


def pack_setup_edges(fields, low, high):
    own_x, own_y, lanes = fields[0].shape
    starts, rows = setup_rows(own_x)
    number = len(fields)

    def kernel(*refs):
        fields = refs[:number]
        low, high, first_ref, last_ref = refs[number:]
        for index, depth in enumerate(FIELD_DEPTHS):
            for x in range(own_x + 2 * depth):
                plane = field_plane(fields, low, high, index, x)
                at = starts[index] + x * depth
                first_ref[at : at + depth, :] = plane[:depth]
                last_ref[at : at + depth, :] = plane[own_y - depth :]

    inputs = list(fields) + [low, high]
    return call(kernel, [(rows, lanes)] * 2, [], inputs, smem_first=False)


def setup(place, sizes, fields, low, high, before, after):
    own_x, own_y, lanes = fields[0].shape
    frame = (own_x + 2 * HALO, own_y + 2 * HALO, lanes)
    starts, _ = setup_rows(own_x)
    number = len(fields)
    coarse = (own_x // 2, own_y // 2, lanes // 2)

    def kernel(*refs):
        place = refs[0]
        fields = refs[1 : 1 + number]
        low, high, before, after = refs[1 + number : 5 + number]
        outs = refs[5 + number : 18 + number]
        cond, hux, huy, huz, nbu, fx, fy, fz, rd, weight, source, z_out, b1 = outs
        prior = refs[18 + number]
        state = refs[19 + number]
        grad = refs[20 + number]

        def assemble(index, ref, x_skip, first_row):
            depth = FIELD_DEPTHS[index]
            for x in range(own_x + 2 * depth):
                at = starts[index] + x * depth
                ref[x + x_skip, first_row : first_row + depth, :] = before[at : at + depth, :]
                ref[x + x_skip, first_row + depth : first_row + depth + own_y, :] = field_plane(
                    fields, low, high, index, x
                )
                end = first_row + depth + own_y
                ref[x + x_skip, end : end + depth, :] = after[at : at + depth, :]

        zero = jnp.zeros(frame[1:], jnp.float32)
        for x in range(frame[0]):
            weight[x] = zero
        assemble(0, prior, 0, 0)
        assemble(1, grad, 0, 0)
        assemble(2, cond, 0, 0)
        assemble(3, state, 0, 0)
        assemble(4, weight, HALO - WIDE, HALO - WIDE)
        x_mask, y_mask, z_mask, outside = frame_masks(place, frame, HALO, sizes)
        planes, rows = frame[:2]
        for x in range(planes):
            center = prior[x + 1, 1 : 1 + rows, :]
            value = prior_rows(
                center,
                prior[x, 1 : 1 + rows, :],
                prior[x + 2, 1 : 1 + rows, :],
                prior[x + 1, 0:rows, :],
                prior[x + 1, 2 : 2 + rows, :],
                x_mask(x),
                x_mask(x + 1),
                y_mask,
                z_mask,
                outside(x),
            )
            source[x] = value - grad[x]
        for x in range(planes):
            cond[x] = jnp.exp(cond[x])
        for x in range(planes):
            u = state[x]
            if x > 0:
                hux[x] = (0.5 * x_mask(x)) * (u - state[x - 1])
            else:
                hux[x] = zero
            huy[x] = (0.5 * y_mask) * (u - shifted(u, 1, 0))
            huz[x] = (0.5 * z_mask) * (u - shifted(u, 1, 1))
            nbu[x] = outside(x) * u
        found = coefficients(
            [cond[x] for x in range(planes)], 1.0, 1, x_mask, y_mask, z_mask, outside
        )
        for x in range(planes):
            fx[x], fy[x], fz[x], rd[x] = found[x]
        z = sensitivity_planes(
            lambda x: cond[x] * source[x], hux, huy, huz, nbu, 1, planes - 1
        )
        z_out[0] = zero
        z_out[planes - 1] = zero
        first_residual_stage(z, fx, fy, fz, rd, z_out, b1, planes)

    deep = (own_x + 2 * DEEP, -(-(own_y + 2 * DEEP) // 8) * 8, lanes)
    return call(
        kernel,
        [frame] * 12 + [coarse],
        [deep, frame, frame],
        [place] + list(fields) + [low, high, before, after],
    )


def coarse_setup(place, sizes, blocks, shape):
    planes, rows, lanes = shape
    whole = (planes * sizes[0], rows * sizes[1], lanes)
    half = (whole[0] // 2,) + whole[1:]

    def kernel(*refs):
        place = refs[0]
        blocks = refs[1 : 1 + sizes[0]]
        outs = refs[1 + sizes[0] : 9 + sizes[0]]
        cond = refs[9 + sizes[0]]
        placed_whole(blocks, place, sizes, planes, planes, cond)
        at_y = iota(whole[1:], 0)
        at_z = iota(whole[1:], 1)

        def level(values, scale, step, refs):
            count = len(values)
            y_mask = flag(at_y >= step)
            z_mask = flag(at_z >= step)
            edges = (
                flag(at_y < step)
                + flag(at_y >= whole[1] - step)
                + flag(at_z < step)
                + flag(at_z >= lanes - step)
            )

            def x_mask(x):
                return 1.0 if x > 0 else 0.0

            def outside(x):
                return edges + float((x == 0) + (x == count - 1))

            found = coefficients(values, scale, step, x_mask, y_mask, z_mask, outside)
            for x in range(count):
                for ref, value in zip(refs, found[x]):
                    ref[x] = value

        level([cond[x] for x in range(whole[0])], 2.0, 1, outs[:4])
        coarse = []
        for x in range(half[0]):
            pair = cond[2 * x] + cond[2 * x + 1]
            coarse.append(0.125 * swap_sum(swap_sum(pair, 0, 1), 1, 1))
        level(coarse, 4.0, 2, outs[4:])

    return call(kernel, [whole] * 4 + [half] * 4, [whole], [place] + list(blocks))


def middle(place, sizes, blocks, per, levels, fine, z, direction, weight, earlier):
    planes, rows, lanes = z.shape
    own_x = planes - 2 * HALO
    coarse = (own_x // 2, (rows - 2 * HALO) // 2, lanes // 2)
    whole = levels[0].shape
    first_time = earlier is None
    sums = 2 if first_time else 1
    extra = [] if first_time else [earlier[0], earlier[1], earlier[2]]
    inputs = [place] + list(blocks) + list(levels) + list(fine) + [z, direction, weight] + extra

    def kernel(*refs):
        at = 0

        def take(number):
            nonlocal at
            at += number
            return refs[at - number : at]

        (place,) = take(1)
        blocks = take(sizes[0])
        levels = take(8)
        fx, fy, fz, rd = take(4)
        z, direction, weight = take(3)
        old = take(len(extra))
        b1, second, curved, kept, combined, ratio_ref = take(6)
        whole_source, whole_mid, whole_out, mid = take(4)
        frame_rows = iota((rows, lanes), 0)
        own_rows = flag((frame_rows >= HALO) & (frame_rows < rows - HALO))
        placed_whole(blocks, place, sizes, coarse[0], per, whole_source)
        coarse_correction(whole_source, whole_mid, whole_out, levels[:4], levels[4:])
        correction = prolonged(whole_out, place, planes // 2, rows, HALO)
        if first_time:
            ratio = None
            for x in range(planes):
                combined[x] = direction[x]
            ratio_ref[...] = jnp.zeros((8, 128), jnp.float32)
        else:
            norm = summed_tiles(blocks, sizes, per, coarse[0])
            ratio = norm / old[2][0:1, 0:1]
            for x in range(planes):
                combined[x] = direction[x] + ratio * old[1][x]
            ratio_ref[...] = jnp.broadcast_to(norm, (8, 128))
        for x in range(1, planes - 1):
            mid[x] = rd[x] * z[x] + correction[x // 2]
        zero = jnp.zeros((rows, lanes), jnp.float32)
        forms = zero
        rights = {}
        for x in range(2, planes - 2):
            off = off_diagonal(mid[x], mid[x - 1], mid[x + 1], fx[x], fx[x + 1], fy[x], fz[x], 1)
            change = KEPT * mid[x] + rd[x] * (z[x] + off)
            if first_time:
                kept[x] = change
            else:
                change = change + ratio * old[0][x]
            right = weight[x] * change
            second[x] = right
            rights[x] = right
            if HALO <= x < planes - HALO:
                forms = forms + right * change
        for x in (0, 1, planes - 2, planes - 1):
            second[x] = zero
            if first_time:
                kept[x] = zero
        if not first_time:
            kept[...] = jnp.zeros(kept.shape, jnp.float32)
        x_mask, y_mask, z_mask, outside = frame_masks(place, (planes, rows, lanes), HALO, sizes)
        squares = zero
        for x in range(HALO, planes - HALO):
            center = combined[x]
            value = prior_rows(
                center,
                combined[x - 1],
                combined[x + 1],
                shifted(center, 1, 0),
                shifted(center, -1, 0),
                x_mask(x),
                x_mask(x + 1),
                y_mask,
                z_mask,
                outside(x),
            )
            curved[x - HALO] = value
            forms = forms + center * value
            if first_time:
                squares = squares + center * center
        iterate = {x: rd[x] * rights[x] for x in range(HALO - 1, planes - HALO + 1)}
        fine_restricted(rights, iterate, fx, fy, fz, b1, HALO, own_x)
        b1[coarse[0]] = fold(jnp.where(own_rows > 0, forms, 0.0))
        if first_time:
            b1[coarse[0] + 1] = fold(jnp.where(own_rows > 0, squares, 0.0))

    frame = (planes, rows, lanes)
    return call(
        kernel,
        [
            (coarse[0] + sums,) + coarse[1:],
            frame,
            (own_x, rows, lanes),
            frame if first_time else (8, 128),
            frame,
            (8, 128),
        ],
        [whole, whole, whole, frame],
        inputs,
    )


def image_planes(levels, fine, place, sizes, blocks, per, second, curved, cond, faces, scratch):
    fx, fy, fz, rd = fine
    hux, huy, huz, nbu = faces
    whole_source, whole_mid, whole_out, mid = scratch
    planes, rows, lanes = second.shape
    placed_whole(blocks, place, sizes, (planes - 2 * HALO) // 2, per, whole_source)
    coarse_correction(whole_source, whole_mid, whole_out, levels[:4], levels[4:])
    correction = prolonged(whole_out, place, planes // 2, rows, HALO)
    for x in range(2, planes - 2):
        mid[x] = rd[x] * second[x] + correction[x // 2]
    adjoint = {}
    for x in range(3, planes - 3):
        off = off_diagonal(mid[x], mid[x - 1], mid[x + 1], fx[x], fx[x + 1], fy[x], fz[x], 1)
        adjoint[x] = KEPT * mid[x] + rd[x] * (second[x] + off)
    out = {}
    along_x = {
        x: hux[x] * (adjoint[x] - adjoint[x - 1]) for x in range(HALO, planes - HALO + 1)
    }
    for x in range(HALO, planes - HALO):
        p = adjoint[x]
        along_y = huy[x] * (p - shifted(p, 1, 0))
        along_z = huz[x] * (p - shifted(p, 1, 1))
        value = along_x[x] + along_x[x + 1] + nbu[x] * p
        value = value + (along_y + shifted(along_y, -1, 0))
        value = value + (along_z + shifted(along_z, -1, 1))
        out[x] = cond[x] * value + curved[x - HALO]
    return out


def end_first(place, sizes, blocks, per, levels, fine, second, curved, cond, faces, source):
    planes, rows, lanes = second.shape
    own_x, own_y = planes - 2 * HALO, rows - 2 * HALO
    whole = levels[0].shape
    coarse = own_x // 2
    inputs = (
        [place] + list(blocks) + list(levels) + list(fine)
        + [second, curved, cond] + list(faces) + [source]
    )

    def kernel(*refs):
        place = refs[0]
        n = sizes[0]
        blocks = refs[1 : 1 + n]
        levels = refs[1 + n : 9 + n]
        fine = refs[9 + n : 13 + n]
        second, curved, cond = refs[13 + n : 16 + n]
        faces = refs[16 + n : 20 + n]
        source = refs[20 + n]
        first_ref, last_ref, own_ref, tile_ref, norm_ref, step_ref = refs[21 + n : 27 + n]
        *scratch, hold = refs[27 + n : 32 + n]
        image = image_planes(
            levels, fine, place, sizes, blocks, per, second, curved, cond, faces, scratch
        )
        form = summed_tiles(blocks, sizes, per, coarse)
        norm = summed_tiles(blocks, sizes, per, coarse + 1)
        step = norm / form
        norm_ref[...] = jnp.broadcast_to(norm, (8, 128))
        step_ref[...] = jnp.broadcast_to(step, (8, 128))
        squares = jnp.zeros((own_y, lanes), jnp.float32)
        for x in range(HALO, planes - HALO):
            hold[x - HALO] = source[x] - step * image[x]
        for x in range(own_x):
            value = hold[x, HALO : HALO + own_y, :]
            squares = squares + value * value
            own_ref[x] = value
            if x < HALO:
                first_ref[x] = value
            if x >= own_x - HALO:
                last_ref[x - own_x + HALO] = value
        tile_ref[0] = fold(squares)

    strip = (HALO, own_y, lanes)
    return call(
        kernel,
        [strip, strip, (own_x, own_y, lanes), (1, 8, 128), (8, 128), (8, 128)],
        [whole, whole, whole, (planes, rows, lanes), (own_x, rows, lanes)],
        inputs,
    )


def end_second(
    place, sizes, blocks, per, levels, fine, second, curved, cond, faces,
    source, remaining, combined, norm, step
):
    planes, rows, lanes = second.shape
    own_x, own_y = planes - 2 * HALO, rows - 2 * HALO
    whole = levels[0].shape
    coarse = own_x // 2
    inputs = (
        [place] + list(blocks) + list(levels) + list(fine)
        + [second, curved, cond] + list(faces) + [source, remaining, combined, norm, step]
    )

    def kernel(*refs):
        place = refs[0]
        n = sizes[0]
        blocks = refs[1 : 1 + n]
        levels = refs[1 + n : 9 + n]
        fine = refs[9 + n : 13 + n]
        second, curved, cond = refs[13 + n : 16 + n]
        faces = refs[16 + n : 20 + n]
        source, remaining, combined, norm, step = refs[20 + n : 25 + n]
        step_out, residual_out = refs[25 + n : 27 + n]
        *scratch, hold, hold_step = refs[27 + n : 33 + n]
        image = image_planes(
            levels, fine, place, sizes, blocks, per, second, curved, cond, faces, scratch
        )
        form = summed_tiles(blocks, sizes, per, coarse)
        now = norm[0:1, 0:1] / form
        before = step[0:1, 0:1]
        for x in range(HALO, planes - HALO):
            hold[x - HALO] = now * image[x]
            hold_step[x - HALO] = before * source[x] + now * combined[x]
        for x in range(own_x):
            residual_out[x] = remaining[x] - hold[x, HALO : HALO + own_y, :]
            step_out[x] = hold_step[x, HALO : HALO + own_y, :]

    own = (own_x, own_y, lanes)
    hold = (own_x, rows, lanes)
    return call(
        kernel,
        [own, own],
        [whole, whole, whole, (planes, rows, lanes), hold, hold],
        inputs,
    )


def pack_edges(own, low, high):
    own_x, own_y, lanes = own.shape
    planes = own_x + 2 * HALO

    def kernel(own, low, high, first_ref, last_ref):
        for x in range(planes):
            if x < HALO:
                ref, at = low, x
            elif x < HALO + own_x:
                ref, at = own, x - HALO
            else:
                ref, at = high, x - HALO - own_x
            first_ref[x] = ref[at, :HALO, :]
            last_ref[x] = ref[at, own_y - HALO :, :]

    strip = (planes, HALO, lanes)
    return call(kernel, [strip] * 2, [], [own, low, high], smem_first=False)


def begin(own, low, high, before, after, tile, cond, faces, fine):
    own_x, own_y, lanes = own.shape
    planes, rows = own_x + 2 * HALO, own_y + 2 * HALO
    frame = (planes, rows, lanes)
    coarse = (own_x // 2, own_y // 2, lanes // 2)

    def kernel(
        own, low, high, before, after, tile, cond, hux, huy, huz, nbu, fx, fy, fz, rd,
        direction, z_out, b1,
    ):
        for x in range(planes):
            if x < HALO:
                value = low[x]
            elif x < HALO + own_x:
                value = own[x - HALO]
            else:
                value = high[x - HALO - own_x]
            direction[x, HALO : HALO + own_y, :] = value
            direction[x, :HALO, :] = before[x]
            direction[x, HALO + own_y :, :] = after[x]
        z = sensitivity_planes(
            lambda x: cond[x] * direction[x], hux, huy, huz, nbu, 1, planes - 1
        )
        zero = jnp.zeros((rows, lanes), jnp.float32)
        z_out[0] = zero
        z_out[planes - 1] = zero
        first_residual_stage(z, fx, fy, fz, rd, z_out, b1, planes)
        b1[coarse[0]] = tile[0]

    return call(
        kernel,
        [frame, frame, (coarse[0] + 1,) + coarse[1:]],
        [],
        [own, low, high, before, after, tile, cond] + list(faces) + list(fine),
        smem_first=False,
    )


def on_device(log_conductivity, state, gradient, prior_sample, sensor_cells, noise_precision):
    sizes = (lax.axis_size("gx"), lax.axis_size("gy"))
    place_x = lax.axis_index("gx")
    place_y = lax.axis_index("gy")
    place = jnp.stack([place_x, place_y]).astype(jnp.int32)
    cells_x, cells_y, cells_z = log_conductivity.shape
    coarse = (cells_x // 2, cells_y // 2, cells_z // 2)

    cond_blocks = gathered(own_coarse_conductivity(log_conductivity))

    rows_all = cells_y * sizes[1]
    sensor_row = sensor_cells // (rows_all * cells_z)
    sensor_column = sensor_cells // cells_z % rows_all
    sensor_depth = sensor_cells % cells_z
    local_cell = (
        (sensor_row - place_x * cells_x) * cells_y + (sensor_column - place_y * cells_y)
    ) * cells_z + sensor_depth
    weight = (
        jnp.zeros((cells_x * cells_y * cells_z,), jnp.float32)
        .at[local_cell]
        .add(noise_precision)
        .reshape(cells_x, cells_y, cells_z)
    )

    fields = (prior_sample, gradient, log_conductivity, state, weight)
    first = jnp.concatenate([v[:d] for v, d in zip(fields, FIELD_DEPTHS)], axis=0)
    last = jnp.concatenate([v[cells_x - d :] for v, d in zip(fields, FIELD_DEPTHS)], axis=0)
    low, high = rotate(last, "gx", 1), rotate(first, "gx", -1)
    first, last = pack_setup_edges(fields, low, high)
    before, after = rotate(last, "gy", 1), rotate(first, "gy", -1)
    (cond, hux, huy, huz, nbu, fx, fy, fz, rd, weight, source, z, b1) = setup(
        place, sizes, fields, low, high, before, after
    )
    faces = (hux, huy, huz, nbu)
    fine = (fx, fy, fz, rd)
    levels = coarse_setup(place, sizes, cond_blocks, coarse)

    b1, second, curved, kept, _, _ = middle(
        place, sizes, gathered(b1), coarse[0], levels, fine, z, source, weight, None
    )
    first, last, remaining, tile, norm, step = end_first(
        place, sizes, gathered(b1), coarse[0] + 2, levels, fine, second, curved, cond, faces,
        source,
    )
    low, high = rotate(last, "gx", 1), rotate(first, "gx", -1)
    first, last = pack_edges(remaining, low, high)
    before, after = rotate(last, "gy", 1), rotate(first, "gy", -1)
    direction, z, b1 = begin(remaining, low, high, before, after, tile, cond, faces, fine)
    b1, second, curved, _, combined, norm = middle(
        place, sizes, gathered(b1), coarse[0] + 1, levels, fine, z, direction, weight,
        (kept, source, norm),
    )
    return tuple(
        end_second(
            place, sizes, gathered(b1), coarse[0] + 1, levels, fine, second, curved, cond,
            faces, source, remaining, combined, norm, step,
        )
    )


def solution(mesh):
    field = P(("ens", "gx"), "gy", None)
    sensors = P(("ens", "gx", "gy"))
    return jax.shard_map(
        on_device,
        mesh=mesh,
        in_specs=(field, field, field, field, sensors, sensors),
        out_specs=(field, field),
        check_vma=False,
    )
```

time: 717 us -> 128 us (0.18)
  blocking collectives: 242 us -> 0 us
  starting transfers between devices: 199 us -> 33.7 us
  local copies, waits for them, and re-layouts: 75.6 us -> 4.37 us
  waiting for transfers between devices: 135 us -> 65.9 us
  other arithmetic: 53.2 us -> 3.56 us
  Pallas kernels: 0 us -> 19.5 us
    ppermute x96 -> x38, starting transfers between devices: 199 us -> 33.7 us  [rotate(): return lax.ppermute(x, axis, [(i, (i + shift) % size) for i in range(size)])]
    all_gather x5 -> x0, blocking collectives: 148 us -> none  [the longest x4 117 us: coarse_solve(): lax.all_gather(source[None], ('gx', 'gy'), axis=0, tiled=True)]
    psum x3 -> x0, blocking collectives: 93.2 us -> none  [the longest x2 62.9 us: norm_sum(): return lax.psum(jnp.sum(residual * residual), ('gx', 'gy'))]
    ppermute x96 -> x38, waiting for transfers between devices: 135 us -> 65.9 us  [rotate(): return lax.ppermute(x, axis, [(i, (i + shift) % size) for i in range(size)])]
    reshape x26 -> x1, local copies, waits for them, and re-layouts: 60.3 us -> 0.04 us  [on_device(): weight = jnp.zeros((cells_x * cells_y * cells_z,), jnp.float32).at[local_...]
    reduce_sum x13 -> x0, other arithmetic: 26 us -> none  [the longest x10 21.5 us: coarsen_sum(): return blocks.sum(axis=(1, 3, 5))]
    pallas_call x0 -> x10, Pallas kernels: none -> 19.5 us  [call(): pl.pallas_call(kernel, out_shape=[jax.ShapeDtypeStruct(shape, jnp.float32...]
    add x40 -> x0, other arithmetic: 10.3 us -> none  [the longest x26 7.32 us: smooth(): iterate + DAMPING * (source - apply_operator(padder(iterate), couplings,...]
  transfers between devices with their start and end apart: 96 -> 38, of which waited for: 36 -> 22; matrix products, arithmetic and copies ran while one was open for 6% -> 0% of each run, Pallas kernels for 0% -> 4%
where the time goes in v1:
time: 128 us
  waiting for transfers between devices  65.9 us (51%)
  starting transfers between devices  33.7 us (26%)
  Pallas kernels  19.5 us (15%)
  local copies, waits for them, and re-layouts  4.37 us (3%)
  other arithmetic  3.56 us (3%)
    ppermute x38, waiting for transfers between devices, rotate(): return lax.ppermute(x, axis, [(i, (i + shift) % size) for i in range(size)])  65.9 us
    ppermute x38, starting transfers between devices, rotate(): return lax.ppermute(x, axis, [(i, (i + shift) % size) for i in range(size)])  33.7 us
    pallas_call x10, Pallas kernels, call(): pl.pallas_call(kernel, out_shape=[jax.ShapeDtypeStruct(shape, jnp.float32...  19.5 us
    unnamed x26, local copies, waits for them, and re-layouts  4.28 us
    scatter-add x1, other arithmetic, on_device(): weight = jnp.zeros((cells_x * cells_y * cells_z,), jnp.float32).at[local_...  3.46 us
  transfers between devices with their start and end apart: 38, of which 22 were waited for; matrix products, arithmetic and copies ran while one was open for 0% of the time, Pallas kernels for 4%

profile of v1, /device:TPU:0, one launch (start us, length us, event | category | flops | bytes accessed | tf_op | source)
XLA Modules:
  0.0 128.0 jit_solution(4630025775809998495)
XLA Ops:
  1.3 3.5 %scatter_custom_fusion = f32[32768]{0:T(1024)S(1)} fusion(s32[512]{0:T(512)S(1)} %compare_select_fusion, f32[512]{0:T(512)} %param.11, f32[]{:T(128)} %constant.54.clone.1), kind=kCustom, calls=%fused_computation.10 | custom fusion | flops 512 | bytes 131584 | tf_op jit(solution)/shard_map/scatter-add | solution.py:771
  9.0 2.0 %collective-permute-start.1 = (f32[19,16,256]{2,1,0:T(8,128)S(1)}, f32[19,16,256]{2,1,0:T(8,128)S(1)}, u32[]{:S(2)}, u32[]{:S(2)}) collective-permute-start(f32[19,16,256]{2,1,0:T(8,128)S(1)} %constant_dynamic-update-slice_fusion.1), channel_id=1, source_target_pairs={{0,12},{4,0},{8,4},{12,8},{1,13},{5,1},{9,5},{13,9},{2,14},{6,2},{... | collective-permute-start | bytes 933896 | tf_op jit(solution)/shard_map/ppermute | solution.py:21
  11.0 5.1 %collective-permute-done.refs_5_.refs_6_ = f32[19,16,256]{2,1,0:T(8,128)S(1)} collective-permute-done((f32[19,16,256]{2,1,0:T(8,128)S(1)}, f32[19,16,256]{2,1,0:T(8,128)S(1)}, u32[]{:S(2)}, u32[]{:S(2)}) %collective-permute-start) | collective-permute-done | bytes 311328 | tf_op jit(solution)/shard_map/ppermute | solution.py:21
  16.2 2.5 %collective-permute-done.1.refs_6_.refs_7_ = f32[19,16,256]{2,1,0:T(8,128)S(1)} collective-permute-done((f32[19,16,256]{2,1,0:T(8,128)S(1)}, f32[19,16,256]{2,1,0:T(8,128)S(1)}, u32[]{:S(2)}, u32[]{:S(2)}) %collective-permute-start.1) | collective-permute-done | bytes 311328 | tf_op jit(solution)/shard_map/ppermute | solution.py:21
  20.4 2.2 %collective-permute-start.3 = (f32[312,256]{1,0:T(8,128)S(1)}, f32[312,256]{1,0:T(8,128)S(1)}, u32[]{:S(2)}, u32[]{:S(2)}) collective-permute-start(f32[312,256]{1,0:T(8,128)S(1)} %get-tuple-element.46), channel_id=1, source_target_pairs={{0,3},{1,0},{2,1},{3,2},{4,7},{5,4},{6,5},{7,6},{8,11},{9,8},{10,9... | collective-permute-start | bytes 958472 | tf_op jit(solution)/shard_map/ppermute | solution.py:21
  26.0 11.6 %collective-permute-done.12 = f32[4,8,128]{2,1,0:T(8,128)S(1)} collective-permute-done((f32[4,8,128]{2,1,0:T(8,128)S(1)}, f32[4,8,128]{2,1,0:T(8,128)S(1)}, u32[]{:S(2)}, u32[]{:S(2)}) %collective-permute-start.12) | collective-permute-done | bytes 16416 | tf_op jit(solution)/shard_map/ppermute | solution.py:21
  41.1 2.9 %shard_map.78 = (f32[16,24,256]{2,1,0:T(8,128)S(1)}, f32[16,24,256]{2,1,0:T(8,128)S(1)}, f32[16,24,256]{2,1,0:T(8,128)S(1)}, f32[16,24,256]{2,1,0:T(8,128)S(1)},...) custom-call(s32[2]{0:T(128)S(1)} %pad_add_fusion.refs_0_, ...), custom_call_target="tpu_custom_call" | custom-call | tf_op jit(solution)/shard_map/pallas_call | solution.py:261
  46.1 4.9 %collective-permute-done.4 = f32[4,8,128]{2,1,0:T(8,128)S(1)} collective-permute-done((f32[4,8,128]{2,1,0:T(8,128)S(1)}, f32[4,8,128]{2,1,0:T(8,128)S(1)}, u32[]{:S(2)}, u32[]{:S(2)}) %collective-permute-start.4) | collective-permute-done | bytes 16416 | tf_op jit(solution)/shard_map/ppermute | solution.py:21
  51.0 4.6 %collective-permute-done.5 = f32[4,8,128]{2,1,0:T(8,128)S(1)} collective-permute-done((f32[4,8,128]{2,1,0:T(8,128)S(1)}, f32[4,8,128]{2,1,0:T(8,128)S(1)}, u32[]{:S(2)}, u32[]{:S(2)}) %collective-permute-start.5) | collective-permute-done | bytes 16416 | tf_op jit(solution)/shard_map/ppermute | solution.py:21
  58.3 2.4 %collective-permute-done.8.refs_3_ = f32[16,8,128]{2,1,0:T(8,128)S(1)} collective-permute-done((f32[16,8,128]{2,1,0:T(8,128)S(1)}, f32[16,8,128]{2,1,0:T(8,128)S(1)}, u32[]{:S(2)}, u32[]{:S(2)}) %collective-permute-start.8) | collective-permute-done | bytes 65568 | tf_op jit(solution)/shard_map/ppermute | solution.py:21
  61.0 4.1 %shard_map.81 = (f32[6,8,128]{2,1,0:T(8,128)S(1)}, f32[16,24,256]{2,1,0:T(8,128)S(1)}, f32[8,24,256]{2,1,0:T(8,128)S(1)}, f32[16,24,256]{2,1,0:T(8,128)S(1)}, f32[16,24,256]{2,1,0:T(8,128)}, /*index=5*/f32[8,128]{1,0:T(8,128)}) custom-call(s32[2]{0:T(128)S(1)} %pad_add_fusion.refs_0_, f32[16,8,128]{2,1,0:T(8,128)S(1)} %constant_dynamic-update-slice_fusion.2.refs_1_, ...), custom_call_target="tpu_custom_call" | custom-call | tf_op jit(solution)/shard_map/pallas_call | solution.py:261
  67.1 4.4 %collective-permute-done.16 = f32[6,8,128]{2,1,0:T(8,128)S(1)} collective-permute-done((f32[6,8,128]{2,1,0:T(8,128)S(1)}, f32[6,8,128]{2,1,0:T(8,128)S(1)}, u32[]{:S(2)}, u32[]{:S(2)}) %collective-permute-start.16) | collective-permute-done | bytes 24608 | tf_op jit(solution)/shard_map/ppermute | solution.py:21
  74.3 3.6 %collective-permute-done.20.refs_3_ = f32[24,8,128]{2,1,0:T(8,128)S(1)} collective-permute-done((f32[24,8,128]{2,1,0:T(8,128)S(1)}, f32[24,8,128]{2,1,0:T(8,128)S(1)}, u32[]{:S(2)}, u32[]{:S(2)}) %collective-permute-start.20) | collective-permute-done | bytes 98336 | tf_op jit(solution)/shard_map/ppermute | solution.py:21
  78.4 2.7 %shard_map.82 = (f32[4,16,256]{2,1,0:T(8,128)S(1)}, f32[4,16,256]{2,1,0:T(8,128)S(1)}, f32[8,16,256]{2,1,0:T(8,128)S(1)}, f32[1,8,128]{2,1,0:T(8,128)S(1)}, f32[8,128]{1,0:T(8,128)S(1)}, /*index=5*/f32[8,128]{1,0:T(8,128)S(1)}) custom-call(s32[2]{0:T(128)S(1)} %pad_add_fusion.refs_0_, f32[24,8,128]{2,1,0:T(8,128)S(1)} %constant_dynamic-update-slice_fusion.6.refs_1_, ...), custom_call_target="tpu_custom_call" | custom-call | tf_op jit(solution)/shard_map/pallas_call | solution.py:261
  85.2 3.5 %collective-permute-start.25 = (f32[16,4,256]{2,1,0:T(4,128)S(1)}, f32[16,4,256]{2,1,0:T(4,128)S(1)}, u32[]{:S(2)}, u32[]{:S(2)}) collective-permute-start(f32[16,4,256]{2,1,0:T(4,128)S(1)} %get-tuple-element.75), channel_id=1, source_target_pairs={{0,3},{1,0},{2,1},{3,2},{4,7},{5,4},{6,5},{7,6},{8,11},{9,8},{10,9... | collective-permute-start | bytes 196616 | tf_op jit(solution)/shard_map/ppermute | solution.py:21
  88.8 2.8 %collective-permute-done.24.before = f32[16,4,256]{2,1,0:T(4,128)S(1)} collective-permute-done((f32[16,4,256]{2,1,0:T(4,128)S(1)}, f32[16,4,256]{2,1,0:T(4,128)S(1)}, u32[]{:S(2)}, u32[]{:S(2)}) %collective-permute-start.24) | collective-permute-done | bytes 65568 | tf_op jit(solution)/shard_map/ppermute | solution.py:21
  92.4 3.9 %collective-permute-start.28 = (f32[5,8,128]{2,1,0:T(8,128)S(1)}, f32[5,8,128]{2,1,0:T(8,128)S(1)}, u32[]{:S(2)}, u32[]{:S(2)}) collective-permute-start(f32[5,8,128]{2,1,0:T(8,128)S(1)} %get-tuple-element.77), channel_id=1, source_target_pairs={{0,3},{1,0},{2,1},{3,2},{4,7},{5,4},{6,5},{7,6},{8,11},{9,8},{10,9... | collective-permute-start | bytes 61448 | tf_op jit(solution)/shard_map/ppermute | solution.py:21
  96.9 4.9 %collective-permute-done.26 = f32[5,8,128]{2,1,0:T(8,128)S(1)} collective-permute-done((f32[5,8,128]{2,1,0:T(8,128)S(1)}, f32[5,8,128]{2,1,0:T(8,128)S(1)}, u32[]{:S(2)}, u32[]{:S(2)}) %collective-permute-start.26) | collective-permute-done | bytes 20512 | tf_op jit(solution)/shard_map/ppermute | solution.py:21
  104.2 3.3 %collective-permute-done.30.refs_3_ = f32[20,8,128]{2,1,0:T(8,128)S(1)} collective-permute-done((f32[20,8,128]{2,1,0:T(8,128)S(1)}, f32[20,8,128]{2,1,0:T(8,128)S(1)}, u32[]{:S(2)}, u32[]{:S(2)}) %collective-permute-start.30) | collective-permute-done | bytes 81952 | tf_op jit(solution)/shard_map/ppermute | solution.py:21
  108.0 3.7 %shard_map.85 = (f32[5,8,128]{2,1,0:T(8,128)S(1)}, f32[16,24,256]{2,1,0:T(8,128)S(1)}, f32[8,24,256]{2,1,0:T(8,128)S(1)}, f32[8,128]{1,0:T(8,128)}, f32[16,24,256]{2,1,0:T(8,128)S(1)}, /*index=5*/f32[8,128]{1,0:T(8,128)S(1)}) custom-call(s32[2]{0:T(128)S(1)} %pad_add_fusion.refs_0_, f32[20,8,128]{2,1,0:T(8,128)S(1)} %constant_dynamic-update-slice_fusion.10.refs_1_, ...), custom_call_target="tpu_custom_call" | custom-call | tf_op jit(solution)/shard_map/pallas_call | solution.py:261
  112.9 2.0 %collective-permute-start.32 = (f32[5,8,128]{2,1,0:T(8,128)S(1)}, f32[5,8,128]{2,1,0:T(8,128)S(1)}, u32[]{:S(2)}, u32[]{:S(2)}) collective-permute-start(f32[5,8,128]{2,1,0:T(8,128)S(1)} %get-tuple-element.82), channel_id=1, source_target_pairs={{0,1},{1,2},{2,3},{3,0},{4,5},{5,6},{6,7},{7,4},{8,9},{9,10},{10,1... | collective-permute-start | bytes 61448 | tf_op jit(solution)/shard_map/ppermute | solution.py:21
  114.9 3.6 %collective-permute-done.32 = f32[5,8,128]{2,1,0:T(8,128)S(1)} collective-permute-done((f32[5,8,128]{2,1,0:T(8,128)S(1)}, f32[5,8,128]{2,1,0:T(8,128)S(1)}, u32[]{:S(2)}, u32[]{:S(2)}) %collective-permute-start.32) | collective-permute-done | bytes 20512 | tf_op jit(solution)/shard_map/ppermute | solution.py:21
  120.9 3.2 %collective-permute-done.36.refs_3_ = f32[20,8,128]{2,1,0:T(8,128)S(1)} collective-permute-done((f32[20,8,128]{2,1,0:T(8,128)S(1)}, f32[20,8,128]{2,1,0:T(8,128)S(1)}, u32[]{:S(2)}, u32[]{:S(2)}) %collective-permute-start.36) | collective-permute-done | bytes 81952 | tf_op jit(solution)/shard_map/ppermute | solution.py:21
  124.6 3.4 %shard_map.86 = (f32[8,16,256]{2,1,0:T(8,128)}, f32[8,16,256]{2,1,0:T(8,128)}) custom-call(s32[2]{0:T(128)S(1)} %pad_add_fusion.refs_0_, f32[20,8,128]{2,1,0:T(8,128)S(1)} %constant_dynamic-update-slice_fusion.14.refs_1_, f32[20,8,128]{2,1,0:T(8,128)S(1)} %collective-permute-done.35.refs_2_, f32[20,8,128]{2,1,0:T(8,128)S(1)} %collective-permute-done.36.refs_3_, ...), custom_call_target="tpu_custom_call" | custom-call | tf_op jit(solution)/shard_map/pallas_call | solution.py:261
  (102 shorter events, 36.2 us)
Async XLA Ops:
  8.5 7.7 %collective-permute-start = (f32[19,16,256]{2,1,0:T(8,128)S(1)}, f32[19,16,256]{2,1,0:T(8,128)S(1)}, u32[]{:S(2)}, u32[]{:S(2)}) collective-permute-start(f32[19,16,256]{2,1,0:T(8,128)S(1)} %constant_dynamic-update-slice_fusion), channel_id=1, source_target_pairs={{0,4},{4,8},{8,12},{12,0},{1,5},{5,9},{9,13},{13,1},{2,6},{6,10},{... | collective-permute-start | bytes 933896 | tf_op jit(solution)/shard_map/ppermute | solution.py:21
  9.0 9.6 %collective-permute-start.1 = (f32[19,16,256]{2,1,0:T(8,128)S(1)}, f32[19,16,256]{2,1,0:T(8,128)S(1)}, u32[]{:S(2)}, u32[]{:S(2)}) collective-permute-start(f32[19,16,256]{2,1,0:T(8,128)S(1)} %constant_dynamic-update-slice_fusion.1), channel_id=1, source_target_pairs={{0,12},{4,0},{8,4},{12,8},{1,13},{5,1},{9,5},{13,9},{2,14},{6,2},{... | collective-permute-start | bytes 933896 | tf_op jit(solution)/shard_map/ppermute | solution.py:21
  18.8 22.3 %collective-permute-start.2 = (f32[312,256]{1,0:T(8,128)S(1)}, f32[312,256]{1,0:T(8,128)S(1)}, u32[]{:S(2)}, u32[]{:S(2)}) collective-permute-start(f32[312,256]{1,0:T(8,128)S(1)} %get-tuple-element.45), channel_id=1, source_target_pairs={{0,1},{1,2},{2,3},{3,0},{4,5},{5,6},{6,7},{7,4},{8,9},{9,10},{10,1... | collective-permute-start | bytes 958472 | tf_op jit(solution)/shard_map/ppermute | solution.py:21
  20.4 20.7 %collective-permute-start.3 = (f32[312,256]{1,0:T(8,128)S(1)}, f32[312,256]{1,0:T(8,128)S(1)}, u32[]{:S(2)}, u32[]{:S(2)}) collective-permute-start(f32[312,256]{1,0:T(8,128)S(1)} %get-tuple-element.46), channel_id=1, source_target_pairs={{0,3},{1,0},{2,1},{3,2},{4,7},{5,4},{6,5},{7,6},{8,11},{9,8},{10,9... | collective-permute-start | bytes 958472 | tf_op jit(solution)/shard_map/ppermute | solution.py:21
  23.0 14.6 %collective-permute-start.12 = (f32[4,8,128]{2,1,0:T(8,128)S(1)}, f32[4,8,128]{2,1,0:T(8,128)S(1)}, u32[]{:S(2)}, u32[]{:S(2)}) collective-permute-start(f32[4,8,128]{2,1,0:T(8,128)S(1)} %shard_map.79), channel_id=1, source_target_pairs={{0,3},{1,0},{2,1},{3,2},{4,7},{5,4},{6,5},{7,6},{8,11},{9,8},{10,9... | collective-permute-start | bytes 49160 | tf_op jit(solution)/shard_map/ppermute | solution.py:21
  24.9 14.3 %collective-permute-start.11 = (f32[4,8,128]{2,1,0:T(8,128)S(1)}, f32[4,8,128]{2,1,0:T(8,128)S(1)}, u32[]{:S(2)}, u32[]{:S(2)}) collective-permute-start(f32[4,8,128]{2,1,0:T(8,128)S(1)} %shard_map.79), channel_id=1, source_target_pairs={{0,2},{1,3},{2,0},{3,1},{4,6},{5,7},{6,4},{7,5},{8,10},{9,11},{10,... | collective-permute-start | bytes 49160 | tf_op jit(solution)/shard_map/ppermute | solution.py:21
  24.9 14.3 %collective-permute-start.10 = (f32[4,8,128]{2,1,0:T(8,128)S(1)}, f32[4,8,128]{2,1,0:T(8,128)S(1)}, u32[]{:S(2)}, u32[]{:S(2)}) collective-permute-start(f32[4,8,128]{2,1,0:T(8,128)S(1)} %shard_map.79), channel_id=1, source_target_pairs={{0,1},{1,2},{2,3},{3,0},{4,5},{5,6},{6,7},{7,4},{8,9},{9,10},{10,1... | collective-permute-start | bytes 49160 | tf_op jit(solution)/shard_map/ppermute | solution.py:21
  39.2 17.5 %collective-permute-start.15 = (f32[16,8,128]{2,1,0:T(8,128)S(1)}, f32[16,8,128]{2,1,0:T(8,128)S(1)}, u32[]{:S(2)}, u32[]{:S(2)}) collective-permute-start(f32[16,8,128]{2,1,0:T(8,128)S(1)} %pad_maximum_fusion.refs_1_), channel_id=1, source_target_pairs={{0,12},{4,0},{8,4},{12,8},{1,13},{5,1},{9,5},{13,9},{2,14},{6,2},{... | collective-permute-start | bytes 196616 | tf_op jit(solution)/shard_map/ppermute | solution.py:21
  40.5 16.3 %collective-permute-start.14 = (f32[16,8,128]{2,1,0:T(8,128)S(1)}, f32[16,8,128]{2,1,0:T(8,128)S(1)}, u32[]{:S(2)}, u32[]{:S(2)}) collective-permute-start(f32[16,8,128]{2,1,0:T(8,128)S(1)} %pad_maximum_fusion.refs_1_), channel_id=1, source_target_pairs={{0,8},{4,12},{8,0},{12,4},{1,9},{5,13},{9,1},{13,5},{2,10},{6,14},... | collective-permute-start | bytes 196616 | tf_op jit(solution)/shard_map/ppermute | solution.py:21
  41.0 15.9 %collective-permute-start.13 = (f32[16,8,128]{2,1,0:T(8,128)S(1)}, f32[16,8,128]{2,1,0:T(8,128)S(1)}, u32[]{:S(2)}, u32[]{:S(2)}) collective-permute-start(f32[16,8,128]{2,1,0:T(8,128)S(1)} %pad_maximum_fusion.refs_1_), channel_id=1, source_target_pairs={{0,4},{4,8},{8,12},{12,0},{1,5},{5,9},{9,13},{13,1},{2,6},{6,10},{... | collective-permute-start | bytes 196616 | tf_op jit(solution)/shard_map/ppermute | solution.py:21
  44.0 11.6 %collective-permute-start.6 = (f32[4,8,128]{2,1,0:T(8,128)S(1)}, f32[4,8,128]{2,1,0:T(8,128)S(1)}, u32[]{:S(2)}, u32[]{:S(2)}) collective-permute-start(f32[4,8,128]{2,1,0:T(8,128)S(1)} %get-tuple-element.47), channel_id=1, source_target_pairs={{0,3},{1,0},{2,1},{3,2},{4,7},{5,4},{6,5},{7,6},{8,11},{9,8},{10,9... | collective-permute-start | bytes 49160 | tf_op jit(solution)/shard_map/ppermute | solution.py:21
  65.1 6.5 %collective-permute-start.18 = (f32[6,8,128]{2,1,0:T(8,128)S(1)}, f32[6,8,128]{2,1,0:T(8,128)S(1)}, u32[]{:S(2)}, u32[]{:S(2)}) collective-permute-start(f32[6,8,128]{2,1,0:T(8,128)S(1)} %get-tuple-element.63), channel_id=1, source_target_pairs={{0,3},{1,0},{2,1},{3,2},{4,7},{5,4},{6,5},{7,6},{8,11},{9,8},{10,9... | collective-permute-start | bytes 73736 | tf_op jit(solution)/shard_map/ppermute | solution.py:21
  65.1 6.5 %collective-permute-start.17 = (f32[6,8,128]{2,1,0:T(8,128)S(1)}, f32[6,8,128]{2,1,0:T(8,128)S(1)}, u32[]{:S(2)}, u32[]{:S(2)}) collective-permute-start(f32[6,8,128]{2,1,0:T(8,128)S(1)} %get-tuple-element.63), channel_id=1, source_target_pairs={{0,2},{1,3},{2,0},{3,1},{4,6},{5,7},{6,4},{7,5},{8,10},{9,11},{10,... | collective-permute-start | bytes 73736 | tf_op jit(solution)/shard_map/ppermute | solution.py:21
  65.9 5.6 %collective-permute-start.16 = (f32[6,8,128]{2,1,0:T(8,128)S(1)}, f32[6,8,128]{2,1,0:T(8,128)S(1)}, u32[]{:S(2)}, u32[]{:S(2)}) collective-permute-start(f32[6,8,128]{2,1,0:T(8,128)S(1)} %get-tuple-element.63), channel_id=1, source_target_pairs={{0,1},{1,2},{2,3},{3,0},{4,5},{5,6},{6,7},{7,4},{8,9},{9,10},{10,1... | collective-permute-start | bytes 73736 | tf_op jit(solution)/shard_map/ppermute | solution.py:21
  71.6 6.2 %collective-permute-start.20 = (f32[24,8,128]{2,1,0:T(8,128)S(1)}, f32[24,8,128]{2,1,0:T(8,128)S(1)}, u32[]{:S(2)}, u32[]{:S(2)}) collective-permute-start(f32[24,8,128]{2,1,0:T(8,128)S(1)} %constant_dynamic-update-slice_fusion.6.refs_1_), channel_id=1, source_target_pairs={{0,8},{4,12},{8,0},{12,4},{1,9},{5,13},{9,1},{13,5},{2,10},{6,14},... | collective-permute-start | bytes 294920 | tf_op jit(solution)/shard_map/ppermute | solution.py:21
  72.7 5.7 %collective-permute-start.19 = (f32[24,8,128]{2,1,0:T(8,128)S(1)}, f32[24,8,128]{2,1,0:T(8,128)S(1)}, u32[]{:S(2)}, u32[]{:S(2)}) collective-permute-start(f32[24,8,128]{2,1,0:T(8,128)S(1)} %constant_dynamic-update-slice_fusion.6.refs_1_), channel_id=1, source_target_pairs={{0,4},{4,8},{8,12},{12,0},{1,5},{5,9},{9,13},{13,1},{2,6},{6,10},{... | collective-permute-start | bytes 294920 | tf_op jit(solution)/shard_map/ppermute | solution.py:21
  84.9 6.7 %collective-permute-start.24 = (f32[16,4,256]{2,1,0:T(4,128)S(1)}, f32[16,4,256]{2,1,0:T(4,128)S(1)}, u32[]{:S(2)}, u32[]{:S(2)}) collective-permute-start(f32[16,4,256]{2,1,0:T(4,128)S(1)} %get-tuple-element.74), channel_id=1, source_target_pairs={{0,1},{1,2},{2,3},{3,0},{4,5},{5,6},{6,7},{7,4},{8,9},{9,10},{10,1... | collective-permute-start | bytes 196616 | tf_op jit(solution)/shard_map/ppermute | solution.py:21
  85.2 6.3 %collective-permute-start.25 = (f32[16,4,256]{2,1,0:T(4,128)S(1)}, f32[16,4,256]{2,1,0:T(4,128)S(1)}, u32[]{:S(2)}, u32[]{:S(2)}) collective-permute-start(f32[16,4,256]{2,1,0:T(4,128)S(1)} %get-tuple-element.75), channel_id=1, source_target_pairs={{0,3},{1,0},{2,1},{3,2},{4,7},{5,4},{6,5},{7,6},{8,11},{9,8},{10,9... | collective-permute-start | bytes 196616 | tf_op jit(solution)/shard_map/ppermute | solution.py:21
  92.4 9.5 %collective-permute-start.28 = (f32[5,8,128]{2,1,0:T(8,128)S(1)}, f32[5,8,128]{2,1,0:T(8,128)S(1)}, u32[]{:S(2)}, u32[]{:S(2)}) collective-permute-start(f32[5,8,128]{2,1,0:T(8,128)S(1)} %get-tuple-element.77), channel_id=1, source_target_pairs={{0,3},{1,0},{2,1},{3,2},{4,7},{5,4},{6,5},{7,6},{8,11},{9,8},{10,9... | collective-permute-start | bytes 61448 | tf_op jit(solution)/shard_map/ppermute | solution.py:21
  96.3 5.6 %collective-permute-start.27 = (f32[5,8,128]{2,1,0:T(8,128)S(1)}, f32[5,8,128]{2,1,0:T(8,128)S(1)}, u32[]{:S(2)}, u32[]{:S(2)}) collective-permute-start(f32[5,8,128]{2,1,0:T(8,128)S(1)} %get-tuple-element.77), channel_id=1, source_target_pairs={{0,2},{1,3},{2,0},{3,1},{4,6},{5,7},{6,4},{7,5},{8,10},{9,11},{10,... | collective-permute-start | bytes 61448 | tf_op jit(solution)/shard_map/ppermute | solution.py:21
  96.3 5.6 %collective-permute-start.26 = (f32[5,8,128]{2,1,0:T(8,128)S(1)}, f32[5,8,128]{2,1,0:T(8,128)S(1)}, u32[]{:S(2)}, u32[]{:S(2)}) collective-permute-start(f32[5,8,128]{2,1,0:T(8,128)S(1)} %get-tuple-element.77), channel_id=1, source_target_pairs={{0,1},{1,2},{2,3},{3,0},{4,5},{5,6},{6,7},{7,4},{8,9},{9,10},{10,1... | collective-permute-start | bytes 61448 | tf_op jit(solution)/shard_map/ppermute | solution.py:21
  111.8 6.7 %collective-permute-start.34 = (f32[5,8,128]{2,1,0:T(8,128)S(1)}, f32[5,8,128]{2,1,0:T(8,128)S(1)}, u32[]{:S(2)}, u32[]{:S(2)}) collective-permute-start(f32[5,8,128]{2,1,0:T(8,128)S(1)} %get-tuple-element.82), channel_id=1, source_target_pairs={{0,3},{1,0},{2,1},{3,2},{4,7},{5,4},{6,5},{7,6},{8,11},{9,8},{10,9... | collective-permute-start | bytes 61448 | tf_op jit(solution)/shard_map/ppermute | solution.py:21
  112.3 6.2 %collective-permute-start.33 = (f32[5,8,128]{2,1,0:T(8,128)S(1)}, f32[5,8,128]{2,1,0:T(8,128)S(1)}, u32[]{:S(2)}, u32[]{:S(2)}) collective-permute-start(f32[5,8,128]{2,1,0:T(8,128)S(1)} %get-tuple-element.82), channel_id=1, source_target_pairs={{0,2},{1,3},{2,0},{3,1},{4,6},{5,7},{6,4},{7,5},{8,10},{9,11},{10,... | collective-permute-start | bytes 61448 | tf_op jit(solution)/shard_map/ppermute | solution.py:21
  112.9 5.6 %collective-permute-start.32 = (f32[5,8,128]{2,1,0:T(8,128)S(1)}, f32[5,8,128]{2,1,0:T(8,128)S(1)}, u32[]{:S(2)}, u32[]{:S(2)}) collective-permute-start(f32[5,8,128]{2,1,0:T(8,128)S(1)} %get-tuple-element.82), channel_id=1, source_target_pairs={{0,1},{1,2},{2,3},{3,0},{4,5},{5,6},{6,7},{7,4},{8,9},{9,10},{10,1... | collective-permute-start | bytes 61448 | tf_op jit(solution)/shard_map/ppermute | solution.py:21
  (19 other events, 62.2 us)

commit v2 on v1

--- a/solution.py
+++ b/solution.py
@@ -19,6 +19,15 @@
 def rotate(x, axis, shift):
     size = lax.axis_size(axis)
     return lax.ppermute(x, axis, [(i, (i + shift) % size) for i in range(size)])
+
+
+def exchange(even_pairs, odd_pairs, axis):
+    size = lax.axis_size(axis)
+    inner = [(i, i) for i in (0, size - 1)]
+    for i in range(1, size - 1, 2):
+        inner += [(i, i + 1), (i + 1, i)]
+    outer = [(i, i ^ 1) for i in range(size)]
+    return lax.ppermute(even_pairs, axis, outer), lax.ppermute(odd_pairs, axis, inner)
 
 
 def shifted(v, step, dim):
@@ -139,7 +148,13 @@
         for t in range(sizes[1]):
             part = refs[s][t * per + index]
             tile = part if tile is None else tile + part
-    return total(tile)
+    return tile
+
+
+def halved(one, two):
+    lower = iota(one.shape, 1) < one.shape[1] // 2
+    middle = one.shape[1] // 2
+    return jnp.where(lower, one + shifted(one, middle, 1), two + shifted(two, middle, 1))
 
 
 def coarse_correction(source, mid, out, level1, level2):
@@ -268,15 +283,55 @@
     )(*inputs)
 
 
-def own_coarse_conductivity(log_cond):
-    def kernel(log_ref, out_ref):
-        planes = [jnp.exp(log_ref[x]) for x in range(log_ref.shape[0])]
-        coarse = restrict_rows(planes, 0, planes[0].shape[0])
+def prepare(place, sizes, fields, cells, precision):
+    own_x, own_y, lanes = fields[0].shape
+    number = len(fields)
+    all_rows = own_y * sizes[1]
+    depths = FIELD_DEPTHS
+
+    def kernel(*refs):
+        place = refs[0]
+        fields = refs[1 : 1 + number]
+        cells, precision = refs[1 + number : 3 + number]
+        coarse_ref, weight_ref, even_ref, odd_ref = refs[3 + number :]
+        cell = cells[...]
+        column = lax.div(cell, lanes)
+        at_z = cell - column * lanes
+        at_x = lax.div(column, all_rows)
+        at_y = column - at_x * all_rows
+        row = (at_x - place[0] * own_x) * own_y + (at_y - place[1] * own_y)
+        count = cell.shape[1]
+        picks = flag(iota((own_x * own_y, count), 0) == row)
+        values = jnp.where(iota((lanes, count), 0) == at_z, precision[...], 0.0)
+        weight = lax.dot_general(
+            picks, values, (((1,), (1,)), ((), ())),
+            precision=EXACT, preferred_element_type=jnp.float32,
+        )
+        for x in range(own_x):
+            weight_ref[x] = weight[x * own_y : (x + 1) * own_y]
+        even = lax.rem(place[0], 2) == 0
+        at = 0
+        for index, depth in enumerate(depths):
+            ref = weight_ref if index == number else fields[index]
+            start = own_x - depth
+            even_start = jnp.where(even, start, 0)
+            odd_start = jnp.where(even, 0, start)
+            for x in range(depth):
+                even_ref[at + x] = ref[even_start + x]
+                odd_ref[at + x] = ref[odd_start + x]
+            at += depth
+        planes = [jnp.exp(fields[2][x]) for x in range(own_x)]
+        coarse = restrict_rows(planes, 0, own_y)
         for x in range(coarse.shape[0]):
-            out_ref[x] = coarse[x] * 0.125
-
-    x, y, z = log_cond.shape
-    return call(kernel, [(x // 2, y // 2, z // 2)], [], [log_cond], smem_first=False)[0]
+            coarse_ref[x] = coarse[x] * 0.125
+
+    edge = (sum(depths), own_y, lanes)
+    return call(
+        kernel,
+        [(own_x // 2, own_y // 2, lanes // 2), fields[0].shape, edge, edge],
+        [],
+        [place] + list(fields) + [cells, precision],
+    )
 
 
 def gathered(own):
@@ -288,45 +343,59 @@
 FIELD_DEPTHS = (DEEP, HALO, HALO, HALO, WIDE)
 
 
+def reach(depth, own_x, x):
+    return depth - max(0, depth - x, x - depth - own_x + 1)
+
+
 def setup_rows(own_x):
     starts, at = [], 0
     for depth in FIELD_DEPTHS:
-        starts.append(at)
-        at += (own_x + 2 * depth) * depth
+        starts.append([])
+        for x in range(own_x + 2 * depth):
+            starts[-1].append(at)
+            at += reach(depth, own_x, x)
     return starts, -(-at // 8) * 8
 
 
-def field_plane(fields, low, high, index, x):
+def field_plane(fields, even_edge, odd_edge, even, index, x):
     depth = FIELD_DEPTHS[index]
     start = sum(FIELD_DEPTHS[:index])
     own = fields[index].shape[0]
     if x < depth:
-        return low[start + x]
+        return jnp.where(even, odd_edge[start + x], even_edge[start + x])
     if x < depth + own:
         return fields[index][x - depth]
-    return high[start + x - depth - own]
-
-
-def pack_setup_edges(fields, low, high):
+    at = start + x - depth - own
+    return jnp.where(even, even_edge[at], odd_edge[at])
+
+
+def pack_setup_edges(place, fields, even_edge, odd_edge):
     own_x, own_y, lanes = fields[0].shape
     starts, rows = setup_rows(own_x)
     number = len(fields)
 
     def kernel(*refs):
-        fields = refs[:number]
-        low, high, first_ref, last_ref = refs[number:]
+        place = refs[0]
+        fields = refs[1 : 1 + number]
+        even_edge, odd_edge, even_ref, odd_ref = refs[1 + number :]
+        even_x = lax.rem(place[0], 2) == 0
+        even_y = lax.rem(place[1], 2) == 0
         for index, depth in enumerate(FIELD_DEPTHS):
             for x in range(own_x + 2 * depth):
-                plane = field_plane(fields, low, high, index, x)
-                at = starts[index] + x * depth
-                first_ref[at : at + depth, :] = plane[:depth]
-                last_ref[at : at + depth, :] = plane[own_y - depth :]
-
-    inputs = list(fields) + [low, high]
-    return call(kernel, [(rows, lanes)] * 2, [], inputs, smem_first=False)
-
-
-def setup(place, sizes, fields, low, high, before, after):
+                here = reach(depth, own_x, x)
+                if here == 0:
+                    continue
+                plane = field_plane(fields, even_edge, odd_edge, even_x, index, x)
+                at = starts[index][x]
+                first, last = plane[:here], plane[own_y - here :]
+                even_ref[at : at + here, :] = jnp.where(even_y, last, first)
+                odd_ref[at : at + here, :] = jnp.where(even_y, first, last)
+
+    inputs = [place] + list(fields) + [even_edge, odd_edge]
+    return call(kernel, [(rows, lanes)] * 2, [], inputs)
+
+
+def setup(place, sizes, fields, x_edges, y_edges):
     own_x, own_y, lanes = fields[0].shape
     frame = (own_x + 2 * HALO, own_y + 2 * HALO, lanes)
     starts, _ = setup_rows(own_x)
@@ -336,7 +405,9 @@
     def kernel(*refs):
         place = refs[0]
         fields = refs[1 : 1 + number]
-        low, high, before, after = refs[1 + number : 5 + number]
+        even_edge, odd_edge, even_rows, odd_rows = refs[1 + number : 5 + number]
+        even_x = lax.rem(place[0], 2) == 0
+        even_y = lax.rem(place[1], 2) == 0
         outs = refs[5 + number : 18 + number]
         cond, hux, huy, huz, nbu, fx, fy, fz, rd, weight, source, z_out, b1 = outs
         prior = refs[18 + number]
@@ -346,17 +417,27 @@
         def assemble(index, ref, x_skip, first_row):
             depth = FIELD_DEPTHS[index]
             for x in range(own_x + 2 * depth):
-                at = starts[index] + x * depth
-                ref[x + x_skip, first_row : first_row + depth, :] = before[at : at + depth, :]
-                ref[x + x_skip, first_row + depth : first_row + depth + own_y, :] = field_plane(
-                    fields, low, high, index, x
+                here = reach(depth, own_x, x)
+                at = starts[index][x]
+                own_row = first_row + depth
+                if here < depth or x_skip:
+                    ref[x + x_skip] = jnp.zeros(ref.shape[1:], jnp.float32)
+                ref[x + x_skip, own_row : own_row + own_y, :] = field_plane(
+                    fields, even_edge, odd_edge, even_x, index, x
                 )
-                end = first_row + depth + own_y
-                ref[x + x_skip, end : end + depth, :] = after[at : at + depth, :]
+                if here == 0:
+                    continue
+                even_part, odd_part = even_rows[at : at + here, :], odd_rows[at : at + here, :]
+                ref[x + x_skip, own_row - here : own_row, :] = jnp.where(
+                    even_y, odd_part, even_part
+                )
+                end = own_row + own_y
+                ref[x + x_skip, end : end + here, :] = jnp.where(even_y, even_part, odd_part)
 
         zero = jnp.zeros(frame[1:], jnp.float32)
-        for x in range(frame[0]):
+        for x in range(HALO - WIDE):
             weight[x] = zero
+            weight[frame[0] - 1 - x] = zero
         assemble(0, prior, 0, 0)
         assemble(1, grad, 0, 0)
         assemble(2, cond, 0, 0)
@@ -407,7 +488,7 @@
         kernel,
         [frame] * 12 + [coarse],
         [deep, frame, frame],
-        [place] + list(fields) + [low, high, before, after],
+        [place] + list(fields) + list(x_edges) + list(y_edges),
     )
 
 
@@ -463,7 +544,6 @@
     coarse = (own_x // 2, (rows - 2 * HALO) // 2, lanes // 2)
     whole = levels[0].shape
     first_time = earlier is None
-    sums = 2 if first_time else 1
     extra = [] if first_time else [earlier[0], earlier[1], earlier[2]]
     inputs = [place] + list(blocks) + list(levels) + list(fine) + [z, direction, weight] + extra
 
@@ -481,7 +561,12 @@
         fx, fy, fz, rd = take(4)
         z, direction, weight = take(3)
         old = take(len(extra))
-        b1, second, curved, kept, combined, ratio_ref = take(6)
+        b1, second, curved = take(3)
+        if first_time:
+            (kept,) = take(1)
+            combined = direction
+        else:
+            combined, norm_ref = take(2)
         whole_source, whole_mid, whole_out, mid = take(4)
         frame_rows = iota((rows, lanes), 0)
         own_rows = flag((frame_rows >= HALO) & (frame_rows < rows - HALO))
@@ -490,15 +575,12 @@
         correction = prolonged(whole_out, place, planes // 2, rows, HALO)
         if first_time:
             ratio = None
-            for x in range(planes):
-                combined[x] = direction[x]
-            ratio_ref[...] = jnp.zeros((8, 128), jnp.float32)
         else:
-            norm = summed_tiles(blocks, sizes, per, coarse[0])
+            norm = total(summed_tiles(blocks, sizes, per, coarse[0]))
             ratio = norm / old[2][0:1, 0:1]
             for x in range(planes):
                 combined[x] = direction[x] + ratio * old[1][x]
-            ratio_ref[...] = jnp.broadcast_to(norm, (8, 128))
+            norm_ref[...] = jnp.broadcast_to(norm, (8, 128))
         for x in range(1, planes - 1):
             mid[x] = rd[x] * z[x] + correction[x // 2]
         zero = jnp.zeros((rows, lanes), jnp.float32)
@@ -520,8 +602,6 @@
             second[x] = zero
             if first_time:
                 kept[x] = zero
-        if not first_time:
-            kept[...] = jnp.zeros(kept.shape, jnp.float32)
         x_mask, y_mask, z_mask, outside = frame_masks(place, (planes, rows, lanes), HALO, sizes)
         squares = zero
         for x in range(HALO, planes - HALO):
@@ -544,21 +624,21 @@
                 squares = squares + center * center
         iterate = {x: rd[x] * rights[x] for x in range(HALO - 1, planes - HALO + 1)}
         fine_restricted(rights, iterate, fx, fy, fz, b1, HALO, own_x)
-        b1[coarse[0]] = fold(jnp.where(own_rows > 0, forms, 0.0))
+        tile = fold(jnp.where(own_rows > 0, forms, 0.0))
         if first_time:
-            b1[coarse[0] + 1] = fold(jnp.where(own_rows > 0, squares, 0.0))
+            tile = halved(tile, fold(jnp.where(own_rows > 0, squares, 0.0)))
+        b1[coarse[0]] = tile
 
     frame = (planes, rows, lanes)
     return call(
         kernel,
         [
-            (coarse[0] + sums,) + coarse[1:],
+            (coarse[0] + 1,) + coarse[1:],
             frame,
             (own_x, rows, lanes),
-            frame if first_time else (8, 128),
             frame,
-            (8, 128),
-        ],
+        ]
+        + ([] if first_time else [(8, 128)]),
         [whole, whole, whole, frame],
         inputs,
     )
@@ -617,8 +697,10 @@
         image = image_planes(
             levels, fine, place, sizes, blocks, per, second, curved, cond, faces, scratch
         )
-        form = summed_tiles(blocks, sizes, per, coarse)
-        norm = summed_tiles(blocks, sizes, per, coarse + 1)
+        tile = summed_tiles(blocks, sizes, per, coarse)
+        lower = iota(tile.shape, 1) < tile.shape[1] // 2
+        form = total(jnp.where(lower, tile, 0.0))
+        norm = total(jnp.where(lower, 0.0, tile))
         step = norm / form
         norm_ref[...] = jnp.broadcast_to(norm, (8, 128))
         step_ref[...] = jnp.broadcast_to(step, (8, 128))
@@ -671,7 +753,7 @@
         image = image_planes(
             levels, fine, place, sizes, blocks, per, second, curved, cond, faces, scratch
         )
-        form = summed_tiles(blocks, sizes, per, coarse)
+        form = total(summed_tiles(blocks, sizes, per, coarse))
         now = norm[0:1, 0:1] / form
         before = step[0:1, 0:1]
         for x in range(HALO, planes - HALO):
@@ -691,23 +773,35 @@
     )
 
 
+def edge_rows(own_x):
+    starts, at = [], 0
+    for x in range(own_x + 2 * HALO):
+        starts.append(at)
+        at += reach(HALO, own_x, x)
+    return starts, -(-at // 8) * 8
+
+
 def pack_edges(own, low, high):
     own_x, own_y, lanes = own.shape
     planes = own_x + 2 * HALO
+    starts, rows = edge_rows(own_x)
 
     def kernel(own, low, high, first_ref, last_ref):
         for x in range(planes):
+            here = reach(HALO, own_x, x)
+            if here == 0:
+                continue
             if x < HALO:
                 ref, at = low, x
             elif x < HALO + own_x:
                 ref, at = own, x - HALO
             else:
                 ref, at = high, x - HALO - own_x
-            first_ref[x] = ref[at, :HALO, :]
-            last_ref[x] = ref[at, own_y - HALO :, :]
-
-    strip = (planes, HALO, lanes)
-    return call(kernel, [strip] * 2, [], [own, low, high], smem_first=False)
+            row = starts[x]
+            first_ref[row : row + here, :] = ref[at, :here, :]
+            last_ref[row : row + here, :] = ref[at, own_y - here :, :]
+
+    return call(kernel, [(rows, lanes)] * 2, [], [own, low, high], smem_first=False)
 
 
 def begin(own, low, high, before, after, tile, cond, faces, fine):
@@ -715,6 +809,7 @@
     planes, rows = own_x + 2 * HALO, own_y + 2 * HALO
     frame = (planes, rows, lanes)
     coarse = (own_x // 2, own_y // 2, lanes // 2)
+    starts, _ = edge_rows(own_x)
 
     def kernel(
         own, low, high, before, after, tile, cond, hux, huy, huz, nbu, fx, fy, fz, rd,
@@ -727,9 +822,15 @@
                 value = own[x - HALO]
             else:
                 value = high[x - HALO - own_x]
+            here = reach(HALO, own_x, x)
+            if here < HALO:
+                direction[x] = jnp.zeros((rows, lanes), jnp.float32)
             direction[x, HALO : HALO + own_y, :] = value
-            direction[x, :HALO, :] = before[x]
-            direction[x, HALO + own_y :, :] = after[x]
+            if here:
+                row = starts[x]
+                direction[x, HALO - here : HALO, :] = before[row : row + here, :]
+                end = HALO + own_y
+                direction[x, end : end + here, :] = after[row : row + here, :]
         z = sensitivity_planes(
             lambda x: cond[x] * direction[x], hux, huy, huz, nbu, 1, planes - 1
         )
@@ -756,47 +857,33 @@
     cells_x, cells_y, cells_z = log_conductivity.shape
     coarse = (cells_x // 2, cells_y // 2, cells_z // 2)
 
-    cond_blocks = gathered(own_coarse_conductivity(log_conductivity))
-
-    rows_all = cells_y * sizes[1]
-    sensor_row = sensor_cells // (rows_all * cells_z)
-    sensor_column = sensor_cells // cells_z % rows_all
-    sensor_depth = sensor_cells % cells_z
-    local_cell = (
-        (sensor_row - place_x * cells_x) * cells_y + (sensor_column - place_y * cells_y)
-    ) * cells_z + sensor_depth
-    weight = (
-        jnp.zeros((cells_x * cells_y * cells_z,), jnp.float32)
-        .at[local_cell]
-        .add(noise_precision)
-        .reshape(cells_x, cells_y, cells_z)
-    )
-
-    fields = (prior_sample, gradient, log_conductivity, state, weight)
-    first = jnp.concatenate([v[:d] for v, d in zip(fields, FIELD_DEPTHS)], axis=0)
-    last = jnp.concatenate([v[cells_x - d :] for v, d in zip(fields, FIELD_DEPTHS)], axis=0)
-    low, high = rotate(last, "gx", 1), rotate(first, "gx", -1)
-    first, last = pack_setup_edges(fields, low, high)
-    before, after = rotate(last, "gy", 1), rotate(first, "gy", -1)
+    fields = (prior_sample, gradient, log_conductivity, state)
+    own_cond, weight, *x_edges = prepare(
+        place, sizes, fields, sensor_cells[None], noise_precision[None]
+    )
+    fields = fields + (weight,)
+    x_edges = exchange(*x_edges, "gx")
+    cond_blocks = gathered(own_cond)
+    y_edges = exchange(*pack_setup_edges(place, fields, *x_edges), "gy")
     (cond, hux, huy, huz, nbu, fx, fy, fz, rd, weight, source, z, b1) = setup(
-        place, sizes, fields, low, high, before, after
+        place, sizes, fields, x_edges, y_edges
     )
     faces = (hux, huy, huz, nbu)
     fine = (fx, fy, fz, rd)
     levels = coarse_setup(place, sizes, cond_blocks, coarse)
 
-    b1, second, curved, kept, _, _ = middle(
+    b1, second, curved, kept = middle(
         place, sizes, gathered(b1), coarse[0], levels, fine, z, source, weight, None
     )
     first, last, remaining, tile, norm, step = end_first(
-        place, sizes, gathered(b1), coarse[0] + 2, levels, fine, second, curved, cond, faces,
+        place, sizes, gathered(b1), coarse[0] + 1, levels, fine, second, curved, cond, faces,
         source,
     )
     low, high = rotate(last, "gx", 1), rotate(first, "gx", -1)
     first, last = pack_edges(remaining, low, high)
     before, after = rotate(last, "gy", 1), rotate(first, "gy", -1)
     direction, z, b1 = begin(remaining, low, high, before, after, tile, cond, faces, fine)
-    b1, second, curved, _, combined, norm = middle(
+    b1, second, curved, combined, norm = middle(
         place, sizes, gathered(b1), coarse[0] + 1, levels, fine, z, direction, weight,
         (kept, source, norm),
     )

time: 128 us -> 114 us (0.89)
  waiting for transfers between devices: 65.9 us -> 46.1 us
  starting transfers between devices: 33.7 us -> 41.8 us
  other arithmetic: 3.56 us -> 0.08 us
    ppermute x38 -> x34, waiting for transfers between devices: 65.9 us -> 42.6 us  [rotate(): return lax.ppermute(x, axis, [(i, (i + shift) % size) for i in range(size)])]
    ppermute x38 -> x34, starting transfers between devices: 33.7 us -> 39.8 us  [rotate(): return lax.ppermute(x, axis, [(i, (i + shift) % size) for i in range(size)])]
    ppermute x0 -> x4, waiting for transfers between devices: none -> 3.51 us  [the longest x2 3.5 us: exchange(): lax.ppermute(even_pairs, axis, outer)]
    scatter-add x1 -> x0, other arithmetic: 3.46 us -> none  [on_device(): weight = jnp.zeros((cells_x * cells_y * cells_z,), jnp.float32).at[local_...]
    ppermute x0 -> x4, starting transfers between devices: none -> 1.97 us  [the longest x2 1.34 us: exchange(): lax.ppermute(odd_pairs, axis, inner)]
    unnamed x26 -> x27, local copies, waits for them, and re-layouts: 4.28 us -> 4.34 us
  transfers between devices with their start and end apart: 38 -> 38, of which waited for: 22 -> 20; matrix products, arithmetic and copies ran while one was open for 0% -> 0% of each run, Pallas kernels for 4% -> 4%
where the time goes in v2:
time: 114 us; the launch traced here: 113 us
  waiting for transfers between devices  46.1 us (40%)
  starting transfers between devices  41.8 us (37%)
  Pallas kernels  20.2 us (18%)
  local copies, waits for them, and re-layouts  4.35 us (4%)
    ppermute x34, waiting for transfers between devices, rotate(): return lax.ppermute(x, axis, [(i, (i + shift) % size) for i in range(size)])  42.6 us
    ppermute x34, starting transfers between devices, rotate(): return lax.ppermute(x, axis, [(i, (i + shift) % size) for i in range(size)])  39.8 us
    pallas_call x10, Pallas kernels, call(): pl.pallas_call(kernel, out_shape=[jax.ShapeDtypeStruct(shape, jnp.float32...  20.2 us
    unnamed x27, local copies, waits for them, and re-layouts  4.34 us
    ppermute x2, waiting for transfers between devices, exchange(): lax.ppermute(even_pairs, axis, outer)  3.5 us
  transfers between devices with their start and end apart: 38, of which 20 were waited for; matrix products, arithmetic and copies ran while one was open for 0% of the time, Pallas kernels for 4%

profile of v2, /device:TPU:0, one launch (start us, length us, event | category | flops | bytes accessed | tf_op | source)
XLA Modules:
  0.0 113.5 jit_solution(16222816632184609686)
XLA Ops:
  7.7 4.7 %collective-permute-start.12 = (f32[4,8,128]{2,1,0:T(8,128)S(1)}, f32[4,8,128]{2,1,0:T(8,128)S(1)}, u32[]{:S(2)}, u32[]{:S(2)}) collective-permute-start(f32[4,8,128]{2,1,0:T(8,128)S(1)} %get-tuple-element.55), channel_id=1, source_target_pairs={{0,3},{1,0},{2,1},{3,2},{4,7},{5,4},{6,5},{7,6},{8,11},{9,8},{10,9... | collective-permute-start | bytes 49160 | tf_op jit(solution)/shard_map/ppermute | solution.py:21
  13.3 4.5 %collective-permute-done.10 = f32[4,8,128]{2,1,0:T(8,128)S(1)} collective-permute-done((f32[4,8,128]{2,1,0:T(8,128)S(1)}, f32[4,8,128]{2,1,0:T(8,128)S(1)}, u32[]{:S(2)}, u32[]{:S(2)}) %collective-permute-start.10) | collective-permute-done | bytes 16416 | tf_op jit(solution)/shard_map/ppermute | solution.py:21
  19.6 3.3 %collective-permute-start.14 = (f32[16,8,128]{2,1,0:T(8,128)S(1)}, f32[16,8,128]{2,1,0:T(8,128)S(1)}, u32[]{:S(2)}, u32[]{:S(2)}) collective-permute-start(f32[16,8,128]{2,1,0:T(8,128)S(1)} %constant_dynamic-update-slice_fusion.4.refs_1_), channel_id=1, source_target_pairs={{0,8},{4,12},{8,0},{12,4},{1,9},{5,13},{9,1},{13,5},{2,10},{6,14},... | collective-permute-start | bytes 196616 | tf_op jit(solution)/shard_map/ppermute | solution.py:21
  23.0 3.5 %collective-permute-done.2.refs_8_ = f32[216,256]{1,0:T(8,128)S(1)} collective-permute-done((f32[216,256]{1,0:T(8,128)S(1)}, f32[216,256]{1,0:T(8,128)S(1)}, u32[]{:S(2)}, u32[]{:S(2)}) %collective-permute-start.2) | collective-permute-done | bytes 221216 | tf_op jit(solution)/shard_map/ppermute | solution.py:30
  26.5 3.0 %shard_map.79 = (f32[16,24,256]{2,1,0:T(8,128)S(1)}, f32[16,24,256]{2,1,0:T(8,128)S(1)}, f32[16,24,256]{2,1,0:T(8,128)S(1)}, f32[16,24,256]{2,1,0:T(8,128)S(1)},...) custom-call(s32[2]{0:T(128)S(1)} %pad_add_fusion.refs_0_, ...), custom_call_target="tpu_custom_call" | custom-call | tf_op jit(solution)/shard_map/pallas_call | solution.py:276
  30.3 3.5 %collective-permute-start.4 = (f32[4,8,128]{2,1,0:T(8,128)S(1)}, f32[4,8,128]{2,1,0:T(8,128)S(1)}, u32[]{:S(2)}, u32[]{:S(2)}) collective-permute-start(f32[4,8,128]{2,1,0:T(8,128)S(1)} %get-tuple-element.54), channel_id=1, source_target_pairs={{0,1},{1,2},{2,3},{3,0},{4,5},{5,6},{6,7},{7,4},{8,9},{9,10},{10,1... | collective-permute-start | bytes 49160 | tf_op jit(solution)/shard_map/ppermute | solution.py:21
  33.8 2.5 %collective-permute-done.4 = f32[4,8,128]{2,1,0:T(8,128)S(1)} collective-permute-done((f32[4,8,128]{2,1,0:T(8,128)S(1)}, f32[4,8,128]{2,1,0:T(8,128)S(1)}, u32[]{:S(2)}, u32[]{:S(2)}) %collective-permute-start.4) | collective-permute-done | bytes 16416 | tf_op jit(solution)/shard_map/ppermute | solution.py:21
  36.3 2.7 %collective-permute-start.5 = (f32[4,8,128]{2,1,0:T(8,128)S(1)}, f32[4,8,128]{2,1,0:T(8,128)S(1)}, u32[]{:S(2)}, u32[]{:S(2)}) collective-permute-start(f32[4,8,128]{2,1,0:T(8,128)S(1)} %get-tuple-element.54), channel_id=1, source_target_pairs={{0,2},{1,3},{2,0},{3,1},{4,6},{5,7},{6,4},{7,5},{8,10},{9,11},{10,... | collective-permute-start | bytes 49160 | tf_op jit(solution)/shard_map/ppermute | solution.py:21
  39.0 2.0 %collective-permute-done.5 = f32[4,8,128]{2,1,0:T(8,128)S(1)} collective-permute-done((f32[4,8,128]{2,1,0:T(8,128)S(1)}, f32[4,8,128]{2,1,0:T(8,128)S(1)}, u32[]{:S(2)}, u32[]{:S(2)}) %collective-permute-start.5) | collective-permute-done | bytes 16416 | tf_op jit(solution)/shard_map/ppermute | solution.py:21
  44.0 2.6 %collective-permute-done.8.refs_3_ = f32[16,8,128]{2,1,0:T(8,128)S(1)} collective-permute-done((f32[16,8,128]{2,1,0:T(8,128)S(1)}, f32[16,8,128]{2,1,0:T(8,128)S(1)}, u32[]{:S(2)}, u32[]{:S(2)}) %collective-permute-start.8) | collective-permute-done | bytes 65568 | tf_op jit(solution)/shard_map/ppermute | solution.py:21
  46.7 3.4 %shard_map.81 = (f32[5,8,128]{2,1,0:T(8,128)S(1)}, f32[16,24,256]{2,1,0:T(8,128)S(1)}, f32[8,24,256]{2,1,0:T(8,128)S(1)}, f32[16,24,256]{2,1,0:T(8,128)S(1)}) custom-call(s32[2]{0:T(128)S(1)} %pad_add_fusion.refs_0_, f32[16,8,128]{2,1,0:T(8,128)S(1)} %constant_dynamic-update-slice_fusion.refs_1_, f32[16,8,128]{2,1,0:T(8,128)S(1)} %collective-permute-done.7.refs_2_, ...), custom_call_target="tpu_custom_call" | custom-call | tf_op jit(solution)/shard_map/pallas_call | solution.py:276
  52.7 1.9 %collective-permute-start.16 = (f32[5,8,128]{2,1,0:T(8,128)S(1)}, f32[5,8,128]{2,1,0:T(8,128)S(1)}, u32[]{:S(2)}, u32[]{:S(2)}) collective-permute-start(f32[5,8,128]{2,1,0:T(8,128)S(1)} %get-tuple-element.71), channel_id=1, source_target_pairs={{0,1},{1,2},{2,3},{3,0},{4,5},{5,6},{6,7},{7,4},{8,9},{9,10},{10,1... | collective-permute-start | bytes 61448 | tf_op jit(solution)/shard_map/ppermute | solution.py:21
  54.6 3.6 %collective-permute-done.16 = f32[5,8,128]{2,1,0:T(8,128)S(1)} collective-permute-done((f32[5,8,128]{2,1,0:T(8,128)S(1)}, f32[5,8,128]{2,1,0:T(8,128)S(1)}, u32[]{:S(2)}, u32[]{:S(2)}) %collective-permute-start.16) | collective-permute-done | bytes 20512 | tf_op jit(solution)/shard_map/ppermute | solution.py:21
  60.7 3.0 %collective-permute-done.20.refs_3_ = f32[20,8,128]{2,1,0:T(8,128)S(1)} collective-permute-done((f32[20,8,128]{2,1,0:T(8,128)S(1)}, f32[20,8,128]{2,1,0:T(8,128)S(1)}, u32[]{:S(2)}, u32[]{:S(2)}) %collective-permute-start.20) | collective-permute-done | bytes 81952 | tf_op jit(solution)/shard_map/ppermute | solution.py:21
  64.3 2.7 %shard_map.82 = (f32[4,16,256]{2,1,0:T(8,128)S(1)}, f32[4,16,256]{2,1,0:T(8,128)S(1)}, f32[8,16,256]{2,1,0:T(8,128)S(1)}, f32[1,8,128]{2,1,0:T(8,128)S(1)}, f32[8,128]{1,0:T(8,128)S(1)}, /*index=5*/f32[8,128]{1,0:T(8,128)S(1)}) custom-call(s32[2]{0:T(128)S(1)} %pad_add_fusion.refs_0_, f32[20,8,128]{2,1,0:T(8,128)S(1)} %constant_dynamic-update-slice_fusion.8.refs_1_, ...), custom_call_target="tpu_custom_call" | custom-call | tf_op jit(solution)/shard_map/pallas_call | solution.py:276
  71.0 3.7 %collective-permute-start.25 = (f32[48,256]{1,0:T(8,128)S(1)}, f32[48,256]{1,0:T(8,128)S(1)}, u32[]{:S(2)}, u32[]{:S(2)}) collective-permute-start(f32[48,256]{1,0:T(8,128)S(1)} %get-tuple-element.83), channel_id=1, source_target_pairs={{0,3},{1,0},{2,1},{3,2},{4,7},{5,4},{6,5},{7,6},{8,11},{9,8},{10,9... | collective-permute-start | bytes 147464 | tf_op jit(solution)/shard_map/ppermute | solution.py:21
  74.7 2.3 %collective-permute-done.24.before = f32[48,256]{1,0:T(8,128)S(1)} collective-permute-done((f32[48,256]{1,0:T(8,128)S(1)}, f32[48,256]{1,0:T(8,128)S(1)}, u32[]{:S(2)}, u32[]{:S(2)}) %collective-permute-start.24) | collective-permute-done | bytes 49184 | tf_op jit(solution)/shard_map/ppermute | solution.py:21
  77.8 4.1 %collective-permute-start.28 = (f32[5,8,128]{2,1,0:T(8,128)S(1)}, f32[5,8,128]{2,1,0:T(8,128)S(1)}, u32[]{:S(2)}, u32[]{:S(2)}) collective-permute-start(f32[5,8,128]{2,1,0:T(8,128)S(1)} %get-tuple-element.85), channel_id=1, source_target_pairs={{0,3},{1,0},{2,1},{3,2},{4,7},{5,4},{6,5},{7,6},{8,11},{9,8},{10,9... | collective-permute-start | bytes 61448 | tf_op jit(solution)/shard_map/ppermute | solution.py:21
  82.6 4.9 %collective-permute-done.26 = f32[5,8,128]{2,1,0:T(8,128)S(1)} collective-permute-done((f32[5,8,128]{2,1,0:T(8,128)S(1)}, f32[5,8,128]{2,1,0:T(8,128)S(1)}, u32[]{:S(2)}, u32[]{:S(2)}) %collective-permute-start.26) | collective-permute-done | bytes 20512 | tf_op jit(solution)/shard_map/ppermute | solution.py:21
  90.0 3.0 %collective-permute-done.30.refs_3_ = f32[20,8,128]{2,1,0:T(8,128)S(1)} collective-permute-done((f32[20,8,128]{2,1,0:T(8,128)S(1)}, f32[20,8,128]{2,1,0:T(8,128)S(1)}, u32[]{:S(2)}, u32[]{:S(2)}) %collective-permute-start.30) | collective-permute-done | bytes 81952 | tf_op jit(solution)/shard_map/ppermute | solution.py:21
  93.6 3.4 %shard_map.85 = (f32[5,8,128]{2,1,0:T(8,128)S(1)}, f32[16,24,256]{2,1,0:T(8,128)S(1)}, f32[8,24,256]{2,1,0:T(8,128)S(1)}, f32[16,24,256]{2,1,0:T(8,128)S(1)}, f32[8,128]{1,0:T(8,128)S(1)}) custom-call(s32[2]{0:T(128)S(1)} %pad_add_fusion.refs_0_, f32[20,8,128]{2,1,0:T(8,128)S(1)} %constant_dynamic-update-slice_fusion.12.refs_1_, ...), custom_call_target="tpu_custom_call" | custom-call | tf_op jit(solution)/shard_map/pallas_call | solution.py:276
  100.2 3.6 %collective-permute-done.32 = f32[5,8,128]{2,1,0:T(8,128)S(1)} collective-permute-done((f32[5,8,128]{2,1,0:T(8,128)S(1)}, f32[5,8,128]{2,1,0:T(8,128)S(1)}, u32[]{:S(2)}, u32[]{:S(2)}) %collective-permute-start.32) | collective-permute-done | bytes 20512 | tf_op jit(solution)/shard_map/ppermute | solution.py:21
  106.0 3.6 %collective-permute-done.36.refs_3_ = f32[20,8,128]{2,1,0:T(8,128)S(1)} collective-permute-done((f32[20,8,128]{2,1,0:T(8,128)S(1)}, f32[20,8,128]{2,1,0:T(8,128)S(1)}, u32[]{:S(2)}, u32[]{:S(2)}) %collective-permute-start.36) | collective-permute-done | bytes 81952 | tf_op jit(solution)/shard_map/ppermute | solution.py:21
  110.1 3.4 %shard_map.86 = (f32[8,16,256]{2,1,0:T(8,128)}, f32[8,16,256]{2,1,0:T(8,128)}) custom-call(s32[2]{0:T(128)S(1)} %pad_add_fusion.refs_0_, f32[20,8,128]{2,1,0:T(8,128)S(1)} %constant_dynamic-update-slice_fusion.16.refs_1_, f32[20,8,128]{2,1,0:T(8,128)S(1)} %collective-permute-done.35.refs_2_, f32[20,8,128]{2,1,0:T(8,128)S(1)} %collective-permute-done.36.refs_3_, ...), custom_call_target="tpu_custom_call" | custom-call | tf_op jit(solution)/shard_map/pallas_call | solution.py:276
  (95 shorter events, 33.7 us)
Async XLA Ops:
  6.4 11.4 %collective-permute-start = (f32[19,16,256]{2,1,0:T(8,128)S(1)}, f32[19,16,256]{2,1,0:T(8,128)S(1)}, u32[]{:S(2)}, u32[]{:S(2)}) collective-permute-start(f32[19,16,256]{2,1,0:T(8,128)S(1)} %get-tuple-element.50), channel_id=1, source_target_pairs={{0,4},{4,0},{8,12},{12,8},{1,5},{5,1},{9,13},{13,9},{2,6},{6,2},{1... | collective-permute-start | bytes 933896 | tf_op jit(solution)/shard_map/ppermute | solution.py:30
  7.0 10.9 %collective-permute-start.1 = (f32[19,16,256]{2,1,0:T(8,128)S(1)}, f32[19,16,256]{2,1,0:T(8,128)S(1)}, u32[]{:S(2)}, u32[]{:S(2)}) collective-permute-start(f32[19,16,256]{2,1,0:T(8,128)S(1)} %get-tuple-element.51), channel_id=1, source_target_pairs={{0,0},{12,12},{4,8},{8,4},{1,1},{13,13},{5,9},{9,5},{2,2},{14,14},... | collective-permute-start | bytes 933896 | tf_op jit(solution)/shard_map/ppermute | solution.py:30
  7.7 11.7 %collective-permute-start.12 = (f32[4,8,128]{2,1,0:T(8,128)S(1)}, f32[4,8,128]{2,1,0:T(8,128)S(1)}, u32[]{:S(2)}, u32[]{:S(2)}) collective-permute-start(f32[4,8,128]{2,1,0:T(8,128)S(1)} %get-tuple-element.55), channel_id=1, source_target_pairs={{0,3},{1,0},{2,1},{3,2},{4,7},{5,4},{6,5},{7,6},{8,11},{9,8},{10,9... | collective-permute-start | bytes 49160 | tf_op jit(solution)/shard_map/ppermute | solution.py:21
  12.3 7.0 %collective-permute-start.11 = (f32[4,8,128]{2,1,0:T(8,128)S(1)}, f32[4,8,128]{2,1,0:T(8,128)S(1)}, u32[]{:S(2)}, u32[]{:S(2)}) collective-permute-start(f32[4,8,128]{2,1,0:T(8,128)S(1)} %get-tuple-element.55), channel_id=1, source_target_pairs={{0,2},{1,3},{2,0},{3,1},{4,6},{5,7},{6,4},{7,5},{8,10},{9,11},{10,... | collective-permute-start | bytes 49160 | tf_op jit(solution)/shard_map/ppermute | solution.py:21
  18.6 7.9 %collective-permute-start.2 = (f32[216,256]{1,0:T(8,128)S(1)}, f32[216,256]{1,0:T(8,128)S(1)}, u32[]{:S(2)}, u32[]{:S(2)}) collective-permute-start(f32[216,256]{1,0:T(8,128)S(1)} %get-tuple-element.52), channel_id=1, source_target_pairs={{0,1},{1,0},{2,3},{3,2},{4,5},{5,4},{6,7},{7,6},{8,9},{9,8},{10,11... | collective-permute-start | bytes 663560 | tf_op jit(solution)/shard_map/ppermute | solution.py:30
  18.7 7.9 %collective-permute-start.3 = (f32[216,256]{1,0:T(8,128)S(1)}, f32[216,256]{1,0:T(8,128)S(1)}, u32[]{:S(2)}, u32[]{:S(2)}) collective-permute-start(f32[216,256]{1,0:T(8,128)S(1)} %get-tuple-element.53), channel_id=1, source_target_pairs={{0,0},{3,3},{1,2},{2,1},{4,4},{7,7},{5,6},{6,5},{8,8},{11,11},{9,1... | collective-permute-start | bytes 663560 | tf_op jit(solution)/shard_map/ppermute | solution.py:30
  19.4 23.1 %collective-permute-start.15 = (f32[16,8,128]{2,1,0:T(8,128)S(1)}, f32[16,8,128]{2,1,0:T(8,128)S(1)}, u32[]{:S(2)}, u32[]{:S(2)}) collective-permute-start(f32[16,8,128]{2,1,0:T(8,128)S(1)} %constant_dynamic-update-slice_fusion.4.refs_1_), channel_id=1, source_target_pairs={{0,12},{4,0},{8,4},{12,8},{1,13},{5,1},{9,5},{13,9},{2,14},{6,2},{... | collective-permute-start | bytes 196616 | tf_op jit(solution)/shard_map/ppermute | solution.py:21
  19.6 23.0 %collective-permute-start.14 = (f32[16,8,128]{2,1,0:T(8,128)S(1)}, f32[16,8,128]{2,1,0:T(8,128)S(1)}, u32[]{:S(2)}, u32[]{:S(2)}) collective-permute-start(f32[16,8,128]{2,1,0:T(8,128)S(1)} %constant_dynamic-update-slice_fusion.4.refs_1_), channel_id=1, source_target_pairs={{0,8},{4,12},{8,0},{12,4},{1,9},{5,13},{9,1},{13,5},{2,10},{6,14},... | collective-permute-start | bytes 196616 | tf_op jit(solution)/shard_map/ppermute | solution.py:21
  22.9 19.8 %collective-permute-start.13 = (f32[16,8,128]{2,1,0:T(8,128)S(1)}, f32[16,8,128]{2,1,0:T(8,128)S(1)}, u32[]{:S(2)}, u32[]{:S(2)}) collective-permute-start(f32[16,8,128]{2,1,0:T(8,128)S(1)} %constant_dynamic-update-slice_fusion.4.refs_1_), channel_id=1, source_target_pairs={{0,4},{4,8},{8,12},{12,0},{1,5},{5,9},{9,13},{13,1},{2,6},{6,10},{... | collective-permute-start | bytes 196616 | tf_op jit(solution)/shard_map/ppermute | solution.py:21
  29.5 11.4 %collective-permute-start.6 = (f32[4,8,128]{2,1,0:T(8,128)S(1)}, f32[4,8,128]{2,1,0:T(8,128)S(1)}, u32[]{:S(2)}, u32[]{:S(2)}) collective-permute-start(f32[4,8,128]{2,1,0:T(8,128)S(1)} %get-tuple-element.54), channel_id=1, source_target_pairs={{0,3},{1,0},{2,1},{3,2},{4,7},{5,4},{6,5},{7,6},{8,11},{9,8},{10,9... | collective-permute-start | bytes 49160 | tf_op jit(solution)/shard_map/ppermute | solution.py:21
  30.3 6.0 %collective-permute-start.4 = (f32[4,8,128]{2,1,0:T(8,128)S(1)}, f32[4,8,128]{2,1,0:T(8,128)S(1)}, u32[]{:S(2)}, u32[]{:S(2)}) collective-permute-start(f32[4,8,128]{2,1,0:T(8,128)S(1)} %get-tuple-element.54), channel_id=1, source_target_pairs={{0,1},{1,2},{2,3},{3,0},{4,5},{5,6},{6,7},{7,4},{8,9},{9,10},{10,1... | collective-permute-start | bytes 49160 | tf_op jit(solution)/shard_map/ppermute | solution.py:21
  41.0 5.6 %collective-permute-start.8 = (f32[16,8,128]{2,1,0:T(8,128)S(1)}, f32[16,8,128]{2,1,0:T(8,128)S(1)}, u32[]{:S(2)}, u32[]{:S(2)}) collective-permute-start(f32[16,8,128]{2,1,0:T(8,128)S(1)} %constant_dynamic-update-slice_fusion.refs_1_), channel_id=1, source_target_pairs={{0,8},{4,12},{8,0},{12,4},{1,9},{5,13},{9,1},{13,5},{2,10},{6,14},... | collective-permute-start | bytes 196616 | tf_op jit(solution)/shard_map/ppermute | solution.py:21
  50.1 8.1 %collective-permute-start.18 = (f32[5,8,128]{2,1,0:T(8,128)S(1)}, f32[5,8,128]{2,1,0:T(8,128)S(1)}, u32[]{:S(2)}, u32[]{:S(2)}) collective-permute-start(f32[5,8,128]{2,1,0:T(8,128)S(1)} %get-tuple-element.71), channel_id=1, source_target_pairs={{0,3},{1,0},{2,1},{3,2},{4,7},{5,4},{6,5},{7,6},{8,11},{9,8},{10,9... | collective-permute-start | bytes 61448 | tf_op jit(solution)/shard_map/ppermute | solution.py:21
  52.0 6.2 %collective-permute-start.17 = (f32[5,8,128]{2,1,0:T(8,128)S(1)}, f32[5,8,128]{2,1,0:T(8,128)S(1)}, u32[]{:S(2)}, u32[]{:S(2)}) collective-permute-start(f32[5,8,128]{2,1,0:T(8,128)S(1)} %get-tuple-element.71), channel_id=1, source_target_pairs={{0,2},{1,3},{2,0},{3,1},{4,6},{5,7},{6,4},{7,5},{8,10},{9,11},{10,... | collective-permute-start | bytes 61448 | tf_op jit(solution)/shard_map/ppermute | solution.py:21
  52.7 5.6 %collective-permute-start.16 = (f32[5,8,128]{2,1,0:T(8,128)S(1)}, f32[5,8,128]{2,1,0:T(8,128)S(1)}, u32[]{:S(2)}, u32[]{:S(2)}) collective-permute-start(f32[5,8,128]{2,1,0:T(8,128)S(1)} %get-tuple-element.71), channel_id=1, source_target_pairs={{0,1},{1,2},{2,3},{3,0},{4,5},{5,6},{6,7},{7,4},{8,9},{9,10},{10,1... | collective-permute-start | bytes 61448 | tf_op jit(solution)/shard_map/ppermute | solution.py:21
  70.8 6.2 %collective-permute-start.24 = (f32[48,256]{1,0:T(8,128)S(1)}, f32[48,256]{1,0:T(8,128)S(1)}, u32[]{:S(2)}, u32[]{:S(2)}) collective-permute-start(f32[48,256]{1,0:T(8,128)S(1)} %get-tuple-element.82), channel_id=1, source_target_pairs={{0,1},{1,2},{2,3},{3,0},{4,5},{5,6},{6,7},{7,4},{8,9},{9,10},{10,1... | collective-permute-start | bytes 147464 | tf_op jit(solution)/shard_map/ppermute | solution.py:21
  71.0 6.0 %collective-permute-start.25 = (f32[48,256]{1,0:T(8,128)S(1)}, f32[48,256]{1,0:T(8,128)S(1)}, u32[]{:S(2)}, u32[]{:S(2)}) collective-permute-start(f32[48,256]{1,0:T(8,128)S(1)} %get-tuple-element.83), channel_id=1, source_target_pairs={{0,3},{1,0},{2,1},{3,2},{4,7},{5,4},{6,5},{7,6},{8,11},{9,8},{10,9... | collective-permute-start | bytes 147464 | tf_op jit(solution)/shard_map/ppermute | solution.py:21
  77.8 9.7 %collective-permute-start.28 = (f32[5,8,128]{2,1,0:T(8,128)S(1)}, f32[5,8,128]{2,1,0:T(8,128)S(1)}, u32[]{:S(2)}, u32[]{:S(2)}) collective-permute-start(f32[5,8,128]{2,1,0:T(8,128)S(1)} %get-tuple-element.85), channel_id=1, source_target_pairs={{0,3},{1,0},{2,1},{3,2},{4,7},{5,4},{6,5},{7,6},{8,11},{9,8},{10,9... | collective-permute-start | bytes 61448 | tf_op jit(solution)/shard_map/ppermute | solution.py:21
  81.9 5.6 %collective-permute-start.27 = (f32[5,8,128]{2,1,0:T(8,128)S(1)}, f32[5,8,128]{2,1,0:T(8,128)S(1)}, u32[]{:S(2)}, u32[]{:S(2)}) collective-permute-start(f32[5,8,128]{2,1,0:T(8,128)S(1)} %get-tuple-element.85), channel_id=1, source_target_pairs={{0,2},{1,3},{2,0},{3,1},{4,6},{5,7},{6,4},{7,5},{8,10},{9,11},{10,... | collective-permute-start | bytes 61448 | tf_op jit(solution)/shard_map/ppermute | solution.py:21
  81.9 5.6 %collective-permute-start.26 = (f32[5,8,128]{2,1,0:T(8,128)S(1)}, f32[5,8,128]{2,1,0:T(8,128)S(1)}, u32[]{:S(2)}, u32[]{:S(2)}) collective-permute-start(f32[5,8,128]{2,1,0:T(8,128)S(1)} %get-tuple-element.85), channel_id=1, source_target_pairs={{0,1},{1,2},{2,3},{3,0},{4,5},{5,6},{6,7},{7,4},{8,9},{9,10},{10,1... | collective-permute-start | bytes 61448 | tf_op jit(solution)/shard_map/ppermute | solution.py:21
  96.9 6.9 %collective-permute-start.34 = (f32[5,8,128]{2,1,0:T(8,128)S(1)}, f32[5,8,128]{2,1,0:T(8,128)S(1)}, u32[]{:S(2)}, u32[]{:S(2)}) collective-permute-start(f32[5,8,128]{2,1,0:T(8,128)S(1)} %get-tuple-element.90), channel_id=1, source_target_pairs={{0,3},{1,0},{2,1},{3,2},{4,7},{5,4},{6,5},{7,6},{8,11},{9,8},{10,9... | collective-permute-start | bytes 61448 | tf_op jit(solution)/shard_map/ppermute | solution.py:21
  97.6 6.2 %collective-permute-start.33 = (f32[5,8,128]{2,1,0:T(8,128)S(1)}, f32[5,8,128]{2,1,0:T(8,128)S(1)}, u32[]{:S(2)}, u32[]{:S(2)}) collective-permute-start(f32[5,8,128]{2,1,0:T(8,128)S(1)} %get-tuple-element.90), channel_id=1, source_target_pairs={{0,2},{1,3},{2,0},{3,1},{4,6},{5,7},{6,4},{7,5},{8,10},{9,11},{10,... | collective-permute-start | bytes 61448 | tf_op jit(solution)/shard_map/ppermute | solution.py:21
  98.2 5.6 %collective-permute-start.32 = (f32[5,8,128]{2,1,0:T(8,128)S(1)}, f32[5,8,128]{2,1,0:T(8,128)S(1)}, u32[]{:S(2)}, u32[]{:S(2)}) collective-permute-start(f32[5,8,128]{2,1,0:T(8,128)S(1)} %get-tuple-element.90), channel_id=1, source_target_pairs={{0,1},{1,2},{2,3},{3,0},{4,5},{5,6},{6,7},{7,4},{8,9},{9,10},{10,1... | collective-permute-start | bytes 61448 | tf_op jit(solution)/shard_map/ppermute | solution.py:21
  103.9 5.7 %collective-permute-start.36 = (f32[20,8,128]{2,1,0:T(8,128)S(1)}, f32[20,8,128]{2,1,0:T(8,128)S(1)}, u32[]{:S(2)}, u32[]{:S(2)}) collective-permute-start(f32[20,8,128]{2,1,0:T(8,128)S(1)} %constant_dynamic-update-slice_fusion.16.refs_1_), channel_id=1, source_target_pairs={{0,8},{4,12},{8,0},{12,4},{1,9},{5,13},{9,1},{13,5},{2,10},{6,14},... | collective-permute-start | bytes 245768 | tf_op jit(solution)/shard_map/ppermute | solution.py:21
  (20 other events, 62.8 us)

commit v3 on v2

v3 whole, which is shorter than its diff:
```python
import jax
import jax.numpy as jnp
from jax import lax
from jax.experimental import pallas as pl
from jax.experimental.pallas import tpu as pltpu
from jax.sharding import PartitionSpec as P

DAMPING = 0.8
KEPT = 0.2
PRIOR_MASS = 0.5
COARSE_SWEEPS = 6
HALO = 4
DEEP = 5
WIDE = 2
VMEM_LIMIT = 24 * 1024 * 1024
PREPARE_LIMIT = 65_600_000
EXACT = lax.Precision.HIGHEST


def rotate(x, axis, shift):
    size = lax.axis_size(axis)
    return lax.ppermute(x, axis, [(i, (i + shift) % size) for i in range(size)])


def exchange(even_pairs, odd_pairs, axis):
    size = lax.axis_size(axis)
    inner = [(i, i) for i in (0, size - 1)]
    for i in range(1, size - 1, 2):
        inner += [(i, i + 1), (i + 1, i)]
    outer = [(i, i ^ 1) for i in range(size)]
    return lax.ppermute(even_pairs, axis, outer), lax.ppermute(odd_pairs, axis, inner)


def here():
    return lax.axis_index("gx"), lax.axis_index("gy")


def shifted(v, step, dim):
    size = v.shape[dim]
    return pltpu.roll(v, step % size, dim)


def dot(a, b):
    return lax.dot_general(
        a, b, (((1,), (0,)), ((), ())), precision=EXACT, preferred_element_type=jnp.float32
    )


def iota(shape, dim):
    return lax.broadcasted_iota(jnp.int32, shape, dim)


def total(tile):
    return jnp.sum(jnp.sum(tile, axis=1, keepdims=True), axis=0, keepdims=True)


def fold(plane):
    rows, lanes = plane.shape
    parts = [
        plane[r : r + 8, c : c + 128] for r in range(0, rows, 8) for c in range(0, lanes, 128)
    ]
    out = parts[0]
    for part in parts[1:]:
        out = out + part
    return out


def z_pairs(lanes):
    half = lanes // 2
    return (iota((lanes, half), 0) // 2 == iota((lanes, half), 1)).astype(jnp.float32)


def z_copies(lanes):
    return (iota((lanes, 2 * lanes), 0) == iota((lanes, 2 * lanes), 1) // 2).astype(jnp.float32)


def restrict_rows(planes, first_row, rows):
    extent = planes[0].shape[0]
    here = iota(planes[0].shape, 0)
    inside = (here >= first_row) & (here < first_row + rows)
    pick = (
        (iota((rows // 2, extent), 1) - first_row + 2) // 2 - 1 == iota((rows // 2, extent), 0)
    ).astype(jnp.float32)
    halves = []
    for x in range(0, len(planes), 2):
        pair = jnp.where(inside, planes[x] + planes[x + 1], 0.0)
        halves.append(dot(pick, pair))
    packed = dot(jnp.concatenate(halves, axis=0), z_pairs(planes[0].shape[1]))
    return packed.reshape(len(planes) // 2, rows // 2, packed.shape[1])


def swap_sum(v, dim, stride):
    even = (iota(v.shape, dim) // stride) % 2 == 0
    return v + jnp.where(even, shifted(v, -stride, dim), shifted(v, stride, dim))


def off_diagonal(v, low, high, fx, fx_high, fy, fz, step=1):
    out = fy * shifted(v, 1, 0) + shifted(fy * v, -1, 0)
    out = out + (fz * shifted(v, step, 1) + shifted(fz * v, -step, 1))
    if low is not None:
        out = out + fx * low
    if high is not None:
        out = out + fx_high * high
    return out


def coefficients(planes, scale, step, x_mask, y_mask, z_mask, outside):
    count = len(planes)
    faces = [None] * count
    for x in range(count):
        low = planes[x] if x == 0 else planes[x - 1]
        faces[x] = (scale * x_mask(x)) * (0.5 * (planes[x] + low))
    out = []
    for x in range(count):
        k = planes[x]
        fy = (scale * y_mask) * (0.5 * (k + shifted(k, 1, 0)))
        fz = (scale * z_mask) * (0.5 * (k + shifted(k, step, 1)))
        diag = (scale * outside(x)) * k + fy + shifted(fy, -1, 0) + fz + shifted(fz, -step, 1)
        diag = diag + faces[x]
        if x + 1 < count:
            diag = diag + faces[x + 1]
        out.append((faces[x], fy, fz, DAMPING / diag))
    return out


def flag(condition):
    return jnp.where(condition, 1.0, 0.0).astype(jnp.float32)


def placed_whole(refs, place, sizes, shape, per, first, whole_ref):
    planes, block_rows, _ = shape
    for s in range(sizes[0]):
        at_x = lax.rem(place[0] - s + sizes[0], sizes[0]) * planes
        for t in range(sizes[1]):
            at_y = lax.rem(place[1] - t + sizes[1], sizes[1])
            row = pl.multiple_of(at_y * block_rows, block_rows)
            for x in range(planes):
                block = refs[s][t * per + first + x]
                whole_ref[at_x + x, pl.ds(row, block_rows), :] = block


def summed_tiles(refs, sizes, per, index):
    tile = None
    for s in range(sizes[0]):
        for t in range(sizes[1]):
            part = refs[s][t * per + index]
            tile = part if tile is None else tile + part
    return tile


def halved(one, two):
    lower = iota(one.shape, 1) < one.shape[1] // 2
    middle = one.shape[1] // 2
    return jnp.where(lower, one + shifted(one, middle, 1), two + shifted(two, middle, 1))


def row_pairs(ref, x, rows):
    return ref[x, pl.ds(0, rows // 2, stride=2), :] + ref[x, pl.ds(1, rows // 2, stride=2), :]


def coarse_correction(place, own, source, mid, pairs, level1, level2):
    fx1, fy1, fz1, rd1 = level1
    fx2, fy2, fz2, rd2 = level2
    planes, own_rows, lanes = own
    count = source.shape[0]
    rows = source.shape[1] - own_rows
    half = count // 2
    blank = jnp.zeros((own_rows, lanes), jnp.float32)
    for x in range(count):
        source[x, rows:, :] = blank
        mid[x, rows:, :] = blank
        mid[x, :rows, :] = rd1[x, :rows, :] * source[x, :rows, :]

    def off1(x):
        low = mid[x - 1, :rows, :] if x > 0 else None
        high = mid[x + 1, :rows, :] if x + 1 < count else None
        fx_high = fx1[x + 1, :rows, :] if x + 1 < count else None
        return off_diagonal(
            mid[x, :rows, :], low, high, fx1[x, :rows, :], fx_high,
            fy1[x, :rows, :], fz1[x, :rows, :],
        )

    for x in range(half):
        pair = KEPT * (source[2 * x, :rows, :] + source[2 * x + 1, :rows, :])
        pairs[x, :rows, :] = swap_sum(pair + (off1(2 * x) + off1(2 * x + 1)), 1, 1)
    coarse = [row_pairs(pairs, x, rows) for x in range(half)]
    iterate = [rd2[x] * coarse[x] for x in range(half)]
    for sweep in range(COARSE_SWEEPS - 1):
        new = []
        for x in range(half):
            low = iterate[x - 1] if x > 0 else None
            high = iterate[x + 1] if x + 1 < half else None
            fx_high = fx2[x + 1] if x + 1 < half else None
            off = off_diagonal(iterate[x], low, high, fx2[x], fx_high, fy2[x], fz2[x], 2)
            new.append(KEPT * iterate[x] + rd2[x] * (coarse[x] + off))
        iterate = new
    for x in range(half):
        pairs[x, rows:, :] = blank
        pairs[x, pl.ds(0, rows // 2, stride=2), :] = iterate[x]
        pairs[x, pl.ds(1, rows // 2, stride=2), :] = iterate[x]

    start = jnp.clip((place[1] - 1) * own_rows, 0, max(rows - 2 * own_rows, 0))
    window = pl.ds(pl.multiple_of(start, own_rows), min(3 * own_rows, rows + own_rows))
    ends = HALO // 2
    at = [
        jnp.clip(place[0] * planes - ends + x, 0, count - 1) for x in range(-1, planes + 2 * ends + 1)
    ]
    value = [mid[a, window, :] + pairs[lax.div(a, 2), window, :] for a in at]
    first = place[1] * own_rows - ends - start
    frame_rows = 2 * (own_rows + 2 * ends)
    extent = value[0].shape[0]
    pick = flag(
        iota((frame_rows, extent), 1) == first + iota((frame_rows, extent), 0) // 2
    )
    parts = []
    for x in range(1, len(at) - 1):
        a = at[x]
        off = off_diagonal(
            value[x], value[x - 1], value[x + 1], fx1[a, window, :], fx1[a + 1, window, :],
            fy1[a, window, :], fz1[a, window, :],
        )
        smooth = KEPT * value[x] + rd1[a, window, :] * (source[a, window, :] + off)
        parts.append(dot(pick, smooth))
    wide = dot(jnp.concatenate(parts, axis=0), z_copies(lanes))
    return [wide[x * frame_rows : (x + 1) * frame_rows] for x in range(len(parts))]


def coarse_scratch(own, sizes):
    whole = (own[0] * sizes[0], own[1] * (sizes[1] + 1), own[2])
    return [whole, whole, (whole[0] // 2,) + whole[1:]]


def frame_masks(place, shape, pad, sizes):
    planes, rows, lanes = shape
    own_x, own_y = planes - 2 * pad, rows - 2 * pad
    all_x, all_y = own_x * sizes[0], own_y * sizes[1]
    base_x, base_y = place[0] * own_x - pad, place[1] * own_y - pad
    at_y = base_y + iota((rows, lanes), 0)
    at_z = iota((rows, lanes), 1)
    y_mask = flag((at_y >= 1) & (at_y < all_y))
    z_mask = flag(at_z >= 1)
    edges = flag(at_y == 0) + flag(at_y == all_y - 1) + flag(at_z == 0) + flag(at_z == lanes - 1)

    def x_mask(x):
        at = base_x + x
        return flag((at >= 1) & (at < all_x))

    def outside(x):
        at = base_x + x
        return edges + (flag(at == 0) + flag(at == all_x - 1))

    return x_mask, y_mask, z_mask, outside


def prior_rows(center, low, high, up, down, x_low, x_high, y_mask, z_mask, outside):
    rows, lanes = center.shape
    y_next = shifted(y_mask, -1, 0)
    z_next = shifted(z_mask, -1, 1)
    out = (PRIOR_MASS + outside) * center + x_low * (center - low) + x_high * (center - high)
    out = out + y_mask * (center - up) + y_next * (center - down)
    out = out + z_mask * (center - shifted(center, 1, 1))
    return out + z_next * (center - shifted(center, -1, 1))


def fine_restricted(base, fields, fx, fy, fz, out_ref, first, own):
    planes = []
    for x in range(first, first + own):
        off = off_diagonal(
            fields[x], fields[x - 1], fields[x + 1], fx[x], fx[x + 1], fy[x], fz[x]
        )
        planes.append(KEPT * base[x] + off)
    rows = planes[0].shape[0]
    coarse = restrict_rows(planes, first, rows - 2 * first)
    for x in range(coarse.shape[0]):
        out_ref[x] = coarse[x]


def sensitivity_planes(q, hux, huy, huz, nbu, first, last):
    faces = {x: hux[x] * (q(x) + q(x - 1)) for x in range(first, last + 1)}
    out = {}
    for x in range(first, last):
        mid = q(x)
        along_y = huy[x] * (mid + shifted(mid, 1, 0))
        along_z = huz[x] * (mid + shifted(mid, 1, 1))
        z = faces[x] - faces[x + 1] + nbu[x] * mid
        z = z + (along_y - shifted(along_y, -1, 0))
        out[x] = z + (along_z - shifted(along_z, -1, 1))
    return out


def first_residual_stage(z, fx, fy, fz, rd, z_ref, out_ref, planes):
    for x in z:
        z_ref[x] = z[x]
    iterate = {x: rd[x] * z[x] for x in range(HALO - 1, planes - HALO + 1)}
    fine_restricted(z, iterate, fx, fy, fz, out_ref, HALO, planes - 2 * HALO)


def call(kernel, outs, scratch, inputs, limit=VMEM_LIMIT, cost=None):
    vmem = pl.BlockSpec(memory_space=pltpu.VMEM)
    return pl.pallas_call(
        kernel,
        out_shape=[jax.ShapeDtypeStruct(shape, jnp.float32) for shape in outs],
        in_specs=[vmem] * len(inputs),
        out_specs=[vmem] * len(outs),
        scratch_shapes=[pltpu.VMEM(shape, jnp.float32) for shape in scratch],
        compiler_params=pltpu.CompilerParams(vmem_limit_bytes=limit),
        cost_estimate=cost,
    )(*inputs)


def prepare(sizes, fields, cells, precision):
    own_x, own_y, lanes = fields[0].shape
    number = len(fields)
    all_rows = own_y * sizes[1]
    depths = FIELD_DEPTHS

    def kernel(*refs):
        place = here()
        fields = refs[:number]
        cells, precision = refs[number : 2 + number]
        coarse_ref, weight_ref, even_ref, odd_ref = refs[2 + number :]
        cell = cells[...]
        column = lax.div(cell, lanes)
        at_z = cell - column * lanes
        at_x = lax.div(column, all_rows)
        at_y = column - at_x * all_rows
        row = (at_x - place[0] * own_x) * own_y + (at_y - place[1] * own_y)
        count = cell.shape[1]
        picks = flag(iota((own_x * own_y, count), 0) == row)
        values = jnp.where(iota((lanes, count), 0) == at_z, precision[...], 0.0)
        weight = lax.dot_general(
            picks, values, (((1,), (1,)), ((), ())),
            precision=EXACT, preferred_element_type=jnp.float32,
        )
        for x in range(own_x):
            weight_ref[x] = weight[x * own_y : (x + 1) * own_y]
        even = lax.rem(place[0], 2) == 0
        at = 0
        for index, depth in enumerate(depths):
            ref = weight_ref if index == number else fields[index]
            start = own_x - depth
            even_start = jnp.where(even, start, 0)
            odd_start = jnp.where(even, 0, start)
            for x in range(depth):
                even_ref[at + x] = ref[even_start + x]
                odd_ref[at + x] = ref[odd_start + x]
            at += depth
        planes = [jnp.exp(fields[2][x]) for x in range(own_x)]
        coarse = restrict_rows(planes, 0, own_y)
        for x in range(coarse.shape[0]):
            coarse_ref[x] = coarse[x] * 0.125

    edge = (sum(depths), own_y, lanes)
    return call(
        kernel,
        [(own_x // 2, own_y // 2, lanes // 2), fields[0].shape, edge, edge],
        [],
        list(fields) + [cells, precision],
        limit=PREPARE_LIMIT,
    )


def gathered(own):
    size_x, size_y = lax.axis_size("gx"), lax.axis_size("gy")
    row = jnp.concatenate([own] + [rotate(own, "gy", t) for t in range(1, size_y)], axis=0)
    return [row] + [rotate(row, "gx", s) for s in range(1, size_x)]


FIELD_DEPTHS = (DEEP, HALO, HALO, HALO, WIDE)


def reach(depth, own_x, x):
    return depth - max(0, depth - x, x - depth - own_x + 1)


def setup_rows(own_x):
    starts, at = [], 0
    for depth in FIELD_DEPTHS:
        starts.append([])
        for x in range(own_x + 2 * depth):
            starts[-1].append(at)
            at += reach(depth, own_x, x)
    return starts, -(-at // 8) * 8


def field_plane(fields, even_edge, odd_edge, even, index, x):
    depth = FIELD_DEPTHS[index]
    start = sum(FIELD_DEPTHS[:index])
    own = fields[index].shape[0]
    if x < depth:
        return jnp.where(even, odd_edge[start + x], even_edge[start + x])
    if x < depth + own:
        return fields[index][x - depth]
    at = start + x - depth - own
    return jnp.where(even, even_edge[at], odd_edge[at])


def pack_setup_edges(fields, even_edge, odd_edge):
    own_x, own_y, lanes = fields[0].shape
    starts, rows = setup_rows(own_x)
    number = len(fields)

    def kernel(*refs):
        place = here()
        fields = refs[:number]
        even_edge, odd_edge, even_ref, odd_ref = refs[number:]
        even_x = lax.rem(place[0], 2) == 0
        even_y = lax.rem(place[1], 2) == 0
        for index, depth in enumerate(FIELD_DEPTHS):
            for x in range(own_x + 2 * depth):
                near = reach(depth, own_x, x)
                if near == 0:
                    continue
                plane = field_plane(fields, even_edge, odd_edge, even_x, index, x)
                at = starts[index][x]
                first, last = plane[:near], plane[own_y - near :]
                even_ref[at : at + near, :] = jnp.where(even_y, last, first)
                odd_ref[at : at + near, :] = jnp.where(even_y, first, last)

    inputs = list(fields) + [even_edge, odd_edge]
    return call(kernel, [(rows, lanes)] * 2, [], inputs)


def setup(sizes, fields, x_edges, y_edges, own_cond):
    own_x, own_y, lanes = fields[0].shape
    frame = (own_x + 2 * HALO, own_y + 2 * HALO, lanes)
    starts, _ = setup_rows(own_x)
    number = len(fields)
    coarse = (own_x // 2, own_y // 2, lanes // 2)

    def kernel(*refs):
        place = here()
        fields = refs[:number]
        even_edge, odd_edge, even_rows, odd_rows, own_cond = refs[number : 5 + number]
        even_x = lax.rem(place[0], 2) == 0
        even_y = lax.rem(place[1], 2) == 0
        outs = refs[5 + number : 18 + number]
        cond, hux, huy, huz, nbu, fx, fy, fz, rd, weight, source, z_out, b1 = outs
        prior = refs[18 + number]
        state = refs[19 + number]
        grad = refs[20 + number]

        def assemble(index, ref, x_skip, first_row):
            depth = FIELD_DEPTHS[index]
            for x in range(own_x + 2 * depth):
                near = reach(depth, own_x, x)
                at = starts[index][x]
                own_row = first_row + depth
                if near < depth or x_skip:
                    ref[x + x_skip] = jnp.zeros(ref.shape[1:], jnp.float32)
                ref[x + x_skip, own_row : own_row + own_y, :] = field_plane(
                    fields, even_edge, odd_edge, even_x, index, x
                )
                if near == 0:
                    continue
                even_part, odd_part = even_rows[at : at + near, :], odd_rows[at : at + near, :]
                ref[x + x_skip, own_row - near : own_row, :] = jnp.where(
                    even_y, odd_part, even_part
                )
                end = own_row + own_y
                ref[x + x_skip, end : end + near, :] = jnp.where(even_y, even_part, odd_part)

        zero = jnp.zeros(frame[1:], jnp.float32)
        for x in range(HALO - WIDE):
            weight[x] = zero
            weight[frame[0] - 1 - x] = zero
        assemble(0, prior, 0, 0)
        assemble(1, grad, 0, 0)
        assemble(2, cond, 0, 0)
        assemble(3, state, 0, 0)
        assemble(4, weight, HALO - WIDE, HALO - WIDE)
        x_mask, y_mask, z_mask, outside = frame_masks(place, frame, HALO, sizes)
        planes, rows = frame[:2]
        for x in range(planes):
            center = prior[x + 1, 1 : 1 + rows, :]
            value = prior_rows(
                center,
                prior[x, 1 : 1 + rows, :],
                prior[x + 2, 1 : 1 + rows, :],
                prior[x + 1, 0:rows, :],
                prior[x + 1, 2 : 2 + rows, :],
                x_mask(x),
                x_mask(x + 1),
                y_mask,
                z_mask,
                outside(x),
            )
            source[x] = value - grad[x]
        for x in range(planes):
            cond[x] = jnp.exp(cond[x])
        for x in range(planes):
            u = state[x]
            if x > 0:
                hux[x] = (0.5 * x_mask(x)) * (u - state[x - 1])
            else:
                hux[x] = zero
            huy[x] = (0.5 * y_mask) * (u - shifted(u, 1, 0))
            huz[x] = (0.5 * z_mask) * (u - shifted(u, 1, 1))
            nbu[x] = outside(x) * u
        found = coefficients(
            [cond[x] for x in range(planes)], 1.0, 1, x_mask, y_mask, z_mask, outside
        )
        for x in range(planes):
            fx[x], fy[x], fz[x], rd[x] = found[x]
        z = sensitivity_planes(
            lambda x: cond[x] * source[x], hux, huy, huz, nbu, 1, planes - 1
        )
        z_out[0] = zero
        z_out[planes - 1] = zero
        first_residual_stage(z, fx, fy, fz, rd, z_out, b1, planes)
        for x in range(coarse[0]):
            b1[coarse[0] + x] = own_cond[x]

    deep = (own_x + 2 * DEEP, -(-(own_y + 2 * DEEP) // 8) * 8, lanes)
    return call(
        kernel,
        [frame] * 12 + [(2 * coarse[0],) + coarse[1:]],
        [deep, frame, frame],
        list(fields) + list(x_edges) + list(y_edges) + [own_cond],
    )


def coarse_setup(sizes, blocks, shape):
    planes, own_rows, lanes = shape
    count, rows = planes * sizes[0], own_rows * sizes[1]
    half = count // 2

    def kernel(*refs):
        blocks = refs[: sizes[0]]
        outs = refs[sizes[0] : 8 + sizes[0]]
        cond, pairs = refs[8 + sizes[0] :]
        placed_whole(blocks, here(), sizes, shape, 2 * planes, planes, cond)

        def level(values, scale, step, refs):
            number, extent = len(values), values[0].shape[0]
            at_y = iota((extent, lanes), 0)
            at_z = iota((extent, lanes), 1)
            edges = (
                flag(at_y == 0) + flag(at_y == extent - 1)
                + flag(at_z < step) + flag(at_z >= lanes - step)
            )

            def x_mask(x):
                return 1.0 if x > 0 else 0.0

            def outside(x):
                return edges + float((x == 0) + (x == number - 1))

            found = coefficients(
                values, scale, step, x_mask, flag(at_y >= 1), flag(at_z >= step), outside
            )
            for x in range(number):
                for ref, value in zip(refs, found[x]):
                    ref[x, :extent, :] = value

        level([cond[x] for x in range(count)], 2.0, 1, outs[:4])
        blank = jnp.zeros((own_rows, lanes), jnp.float32)
        for x in range(count):
            for ref in outs[:4]:
                ref[x, rows:, :] = blank
        outs[0][count] = jnp.zeros((rows + own_rows, lanes), jnp.float32)
        for x in range(half):
            pairs[x] = swap_sum(cond[2 * x] + cond[2 * x + 1], 1, 1)
        coarse = [0.125 * row_pairs(pairs, x, rows) for x in range(half)]
        level(coarse, 4.0, 2, outs[4:])

    padded = (count, rows + own_rows, lanes)
    return call(
        kernel,
        [(count + 1,) + padded[1:]] + [padded] * 3 + [(half, rows // 2, lanes)] * 4,
        [(count, rows, lanes), (half, rows, lanes)],
        list(blocks),
    )


def prior_part(sizes, direction):
    planes, rows, lanes = direction.shape

    def kernel(direction, out_ref):
        x_mask, y_mask, z_mask, outside = frame_masks(here(), direction.shape, HALO, sizes)
        for x in range(HALO, planes - HALO):
            center = direction[x]
            out_ref[x - HALO] = prior_rows(
                center,
                direction[x - 1],
                direction[x + 1],
                shifted(center, 1, 0),
                shifted(center, -1, 0),
                x_mask(x),
                x_mask(x + 1),
                y_mask,
                z_mask,
                outside(x),
            )

    size = planes * rows * lanes
    return call(
        kernel, [(planes - 2 * HALO, rows, lanes)], [], [direction],
        cost=pl.CostEstimate(flops=20 * size, bytes_accessed=8 * size, transcendentals=0),
    )[0]


def middle(sizes, blocks, per, levels, fine, z, direction, curved, weight, earlier):
    planes, rows, lanes = z.shape
    own_x = planes - 2 * HALO
    coarse = (own_x // 2, (rows - 2 * HALO) // 2, lanes // 2)
    first_time = earlier is None
    extra = [] if first_time else list(earlier)
    inputs = list(blocks) + list(levels) + list(fine) + [z, direction, curved, weight] + extra

    def kernel(*refs):
        at = 0

        def take(number):
            nonlocal at
            at += number
            return refs[at - number : at]

        place = here()
        blocks = take(sizes[0])
        levels = take(8)
        fx, fy, fz, rd = take(4)
        z, direction, curved, weight = take(4)
        old = take(len(extra))
        b1, second = take(2)
        if first_time:
            (kept,) = take(1)
        else:
            combined, curved_out, norm_ref = take(3)
        source, whole_mid, pairs, mid = take(4)
        frame_rows = iota((rows, lanes), 0)
        own_rows = (frame_rows >= HALO) & (frame_rows < rows - HALO)
        placed_whole(blocks, place, sizes, coarse, per, 0, source)
        correction = coarse_correction(
            place, coarse, source, whole_mid, pairs, levels[:4], levels[4:]
        )
        zero = jnp.zeros((rows, lanes), jnp.float32)
        forms = zero
        squares = zero
        if first_time:
            for x in range(own_x):
                d = direction[x + HALO]
                forms = forms + d * curved[x]
                squares = squares + d * d
        else:
            norm = total(summed_tiles(blocks, sizes, per, coarse[0]))
            ratio = norm / old[2][0:1, 0:1]
            for x in range(own_x):
                d = direction[x + HALO] + ratio * old[1][x + HALO]
                image = curved[x] + ratio * old[3][x]
                combined[x] = d
                curved_out[x] = image
                forms = forms + d * image
            norm_ref[...] = jnp.broadcast_to(norm, (8, 128))
        for x in range(1, planes - 1):
            mid[x] = rd[x] * z[x] + correction[x // 2]
        rights = {}
        for x in range(2, planes - 2):
            off = off_diagonal(mid[x], mid[x - 1], mid[x + 1], fx[x], fx[x + 1], fy[x], fz[x])
            change = KEPT * mid[x] + rd[x] * (z[x] + off)
            if first_time:
                kept[x] = change
            else:
                change = change + ratio * old[0][x]
            right = weight[x] * change
            second[x] = right
            rights[x] = right
            if HALO <= x < planes - HALO:
                forms = forms + right * change
        for x in (0, 1, planes - 2, planes - 1):
            second[x] = zero
            if first_time:
                kept[x] = zero
        iterate = {x: rd[x] * rights[x] for x in range(HALO - 1, planes - HALO + 1)}
        fine_restricted(rights, iterate, fx, fy, fz, b1, HALO, own_x)
        tile = fold(jnp.where(own_rows, forms, 0.0))
        if first_time:
            tile = halved(tile, fold(jnp.where(own_rows, squares, 0.0)))
        b1[coarse[0]] = tile

    frame = (planes, rows, lanes)
    own = (own_x, rows, lanes)
    return call(
        kernel,
        [(coarse[0] + 1,) + coarse[1:], frame] + ([frame] if first_time else [own, own, (8, 128)]),
        coarse_scratch(coarse, sizes) + [frame],
        inputs,
    )


def image_planes(levels, fine, sizes, blocks, per, second, curved, cond, faces, scratch):
    fx, fy, fz, rd = fine
    hux, huy, huz, nbu = faces
    source, whole_mid, pairs, mid = scratch
    place = here()
    planes, rows, lanes = second.shape
    own = ((planes - 2 * HALO) // 2, (rows - 2 * HALO) // 2, lanes // 2)
    placed_whole(blocks, place, sizes, own, per, 0, source)
    correction = coarse_correction(
        place, own, source, whole_mid, pairs, levels[:4], levels[4:]
    )
    for x in range(2, planes - 2):
        mid[x] = rd[x] * second[x] + correction[x // 2]
    adjoint = {}
    for x in range(3, planes - 3):
        off = off_diagonal(mid[x], mid[x - 1], mid[x + 1], fx[x], fx[x + 1], fy[x], fz[x])
        adjoint[x] = KEPT * mid[x] + rd[x] * (second[x] + off)
    out = {}
    along_x = {
        x: hux[x] * (adjoint[x] - adjoint[x - 1]) for x in range(HALO, planes - HALO + 1)
    }
    for x in range(HALO, planes - HALO):
        p = adjoint[x]
        along_y = huy[x] * (p - shifted(p, 1, 0))
        along_z = huz[x] * (p - shifted(p, 1, 1))
        value = along_x[x] + along_x[x + 1] + nbu[x] * p
        value = value + (along_y + shifted(along_y, -1, 0))
        value = value + (along_z + shifted(along_z, -1, 1))
        out[x] = cond[x] * value + curved[x - HALO]
    return out


def end_first(sizes, blocks, per, levels, fine, second, curved, cond, faces, source):
    planes, rows, lanes = second.shape
    own_x, own_y = planes - 2 * HALO, rows - 2 * HALO
    coarse = own_x // 2
    scratch_shapes = coarse_scratch((coarse, own_y // 2, lanes // 2), sizes)
    inputs = (
        list(blocks) + list(levels) + list(fine)
        + [second, curved, cond] + list(faces) + [source]
    )

    def kernel(*refs):
        n = sizes[0]
        blocks = refs[:n]
        levels = refs[n : 8 + n]
        fine = refs[8 + n : 12 + n]
        second, curved, cond = refs[12 + n : 15 + n]
        faces = refs[15 + n : 19 + n]
        source = refs[19 + n]
        first_ref, last_ref, own_ref, tile_ref, norm_ref, step_ref = refs[20 + n : 26 + n]
        *scratch, hold = refs[26 + n :]
        image = image_planes(
            levels, fine, sizes, blocks, per, second, curved, cond, faces, scratch
        )
        tile = summed_tiles(blocks, sizes, per, coarse)
        lower = iota(tile.shape, 1) < tile.shape[1] // 2
        form = total(jnp.where(lower, tile, 0.0))
        norm = total(jnp.where(lower, 0.0, tile))
        step = norm / form
        norm_ref[...] = jnp.broadcast_to(norm, (8, 128))
        step_ref[...] = jnp.broadcast_to(step, (8, 128))
        squares = jnp.zeros((own_y, lanes), jnp.float32)
        for x in range(HALO, planes - HALO):
            hold[x - HALO] = source[x] - step * image[x]
        for x in range(own_x):
            value = hold[x, HALO : HALO + own_y, :]
            squares = squares + value * value
            own_ref[x] = value
            if x < HALO:
                first_ref[x] = value
            if x >= own_x - HALO:
                last_ref[x - own_x + HALO] = value
        tile_ref[0] = fold(squares)

    strip = (HALO, own_y, lanes)
    return call(
        kernel,
        [strip, strip, (own_x, own_y, lanes), (1, 8, 128), (8, 128), (8, 128)],
        scratch_shapes + [(planes, rows, lanes), (own_x, rows, lanes)],
        inputs,
    )


def end_second(
    sizes, blocks, per, levels, fine, second, curved, cond, faces,
    source, remaining, combined, norm, step
):
    planes, rows, lanes = second.shape
    own_x, own_y = planes - 2 * HALO, rows - 2 * HALO
    coarse = own_x // 2
    scratch_shapes = coarse_scratch((coarse, own_y // 2, lanes // 2), sizes)
    inputs = (
        list(blocks) + list(levels) + list(fine)
        + [second, curved, cond] + list(faces) + [source, remaining, combined, norm, step]
    )

    def kernel(*refs):
        n = sizes[0]
        blocks = refs[:n]
        levels = refs[n : 8 + n]
        fine = refs[8 + n : 12 + n]
        second, curved, cond = refs[12 + n : 15 + n]
        faces = refs[15 + n : 19 + n]
        source, remaining, combined, norm, step = refs[19 + n : 24 + n]
        step_out, residual_out = refs[24 + n : 26 + n]
        *scratch, hold, hold_step = refs[26 + n :]
        image = image_planes(
            levels, fine, sizes, blocks, per, second, curved, cond, faces, scratch
        )
        form = total(summed_tiles(blocks, sizes, per, coarse))
        now = norm[0:1, 0:1] / form
        before = step[0:1, 0:1]
        for x in range(HALO, planes - HALO):
            hold[x - HALO] = now * image[x]
            hold_step[x - HALO] = before * source[x] + now * combined[x - HALO]
        for x in range(own_x):
            residual_out[x] = remaining[x] - hold[x, HALO : HALO + own_y, :]
            step_out[x] = hold_step[x, HALO : HALO + own_y, :]

    own = (own_x, own_y, lanes)
    hold = (own_x, rows, lanes)
    return call(
        kernel,
        [own, own],
        scratch_shapes + [(planes, rows, lanes), hold, hold],
        inputs,
    )


def edge_rows(own_x):
    starts, at = [], 0
    for x in range(own_x + 2 * HALO):
        starts.append(at)
        at += reach(HALO, own_x, x)
    return starts, -(-at // 8) * 8


def pack_edges(own, low, high):
    own_x, own_y, lanes = own.shape
    planes = own_x + 2 * HALO
    starts, rows = edge_rows(own_x)

    def kernel(own, low, high, first_ref, last_ref):
        for x in range(planes):
            near = reach(HALO, own_x, x)
            if near == 0:
                continue
            if x < HALO:
                ref, at = low, x
            elif x < HALO + own_x:
                ref, at = own, x - HALO
            else:
                ref, at = high, x - HALO - own_x
            row = starts[x]
            first_ref[row : row + near, :] = ref[at, :near, :]
            last_ref[row : row + near, :] = ref[at, own_y - near :, :]

    return call(kernel, [(rows, lanes)] * 2, [], [own, low, high])


def begin(own, low, high, before, after, tile, cond, faces, fine):
    own_x, own_y, lanes = own.shape
    planes, rows = own_x + 2 * HALO, own_y + 2 * HALO
    frame = (planes, rows, lanes)
    coarse = (own_x // 2, own_y // 2, lanes // 2)
    starts, _ = edge_rows(own_x)

    def kernel(
        own, low, high, before, after, tile, cond, hux, huy, huz, nbu, fx, fy, fz, rd,
        direction, z_out, b1,
    ):
        for x in range(planes):
            if x < HALO:
                value = low[x]
            elif x < HALO + own_x:
                value = own[x - HALO]
            else:
                value = high[x - HALO - own_x]
            near = reach(HALO, own_x, x)
            if near < HALO:
                direction[x] = jnp.zeros((rows, lanes), jnp.float32)
            direction[x, HALO : HALO + own_y, :] = value
            if near:
                row = starts[x]
                direction[x, HALO - near : HALO, :] = before[row : row + near, :]
                end = HALO + own_y
                direction[x, end : end + near, :] = after[row : row + near, :]
        z = sensitivity_planes(
            lambda x: cond[x] * direction[x], hux, huy, huz, nbu, 1, planes - 1
        )
        zero = jnp.zeros((rows, lanes), jnp.float32)
        z_out[0] = zero
        z_out[planes - 1] = zero
        first_residual_stage(z, fx, fy, fz, rd, z_out, b1, planes)
        b1[coarse[0]] = tile[0]

    return call(
        kernel,
        [frame, frame, (coarse[0] + 1,) + coarse[1:]],
        [],
        [own, low, high, before, after, tile, cond] + list(faces) + list(fine),
    )


def on_device(log_conductivity, state, gradient, prior_sample, sensor_cells, noise_precision):
    sizes = (lax.axis_size("gx"), lax.axis_size("gy"))
    cells_x, cells_y, cells_z = log_conductivity.shape
    coarse = (cells_x // 2, cells_y // 2, cells_z // 2)
    per = coarse[0] + 1

    fields = (prior_sample, gradient, log_conductivity, state)
    own_cond, weight, *x_edges = prepare(
        sizes, fields, sensor_cells[None], noise_precision[None]
    )
    fields = fields + (weight,)
    x_edges = exchange(*x_edges, "gx")
    y_edges = exchange(*pack_setup_edges(fields, *x_edges), "gy")
    (cond, hux, huy, huz, nbu, fx, fy, fz, rd, weight, source, z, b1) = setup(
        sizes, fields, x_edges, y_edges, own_cond
    )
    faces = (hux, huy, huz, nbu)
    fine = (fx, fy, fz, rd)

    blocks = gathered(b1)
    curved = prior_part(sizes, source)
    levels = coarse_setup(sizes, blocks, coarse)
    b1, second, kept = middle(
        sizes, blocks, 2 * coarse[0], levels, fine, z, source, curved, weight, None
    )
    first, last, remaining, tile, norm, step = end_first(
        sizes, gathered(b1), per, levels, fine, second, curved, cond, faces, source
    )
    low, high = rotate(last, "gx", 1), rotate(first, "gx", -1)
    first, last = pack_edges(remaining, low, high)
    before, after = rotate(last, "gy", 1), rotate(first, "gy", -1)
    direction, z, b1 = begin(remaining, low, high, before, after, tile, cond, faces, fine)
    blocks = gathered(b1)
    b1, second, combined, curved, norm = middle(
        sizes, blocks, per, levels, fine, z, direction, prior_part(sizes, direction), weight,
        (kept, source, norm, curved),
    )
    return tuple(
        end_second(
            sizes, gathered(b1), per, levels, fine, second, curved, cond,
            faces, source, remaining, combined, norm, step,
        )
    )


def solution(mesh):
    field = P(("ens", "gx"), "gy", None)
    sensors = P(("ens", "gx", "gy"))
    return jax.shard_map(
        on_device,
        mesh=mesh,
        in_specs=(field, field, field, field, sensors, sensors),
        out_specs=(field, field),
        check_vma=False,
    )
```

time: 114 us -> 107 us (0.939)
  Pallas kernels: 20.2 us -> 16.5 us
  local copies, waits for them, and re-layouts: 4.35 us -> 0.97 us
    pallas_call x10 -> x12, Pallas kernels: 20.2 us -> 16.5 us  [call(): pl.pallas_call(kernel, out_shape=[jax.ShapeDtypeStruct(shape, jnp.float32...]
    unnamed x27 -> x24, local copies, waits for them, and re-layouts: 4.34 us -> 0.95 us
    ppermute x34 -> x28, starting transfers between devices: 39.8 us -> 36.9 us  [rotate(): return lax.ppermute(x, axis, [(i, (i + shift) % size) for i in range(size)])]
    ppermute x2, starting transfers between devices: 0.63 us -> 3.31 us  [exchange(): lax.ppermute(even_pairs, axis, outer)]
    ppermute x34 -> x28, waiting for transfers between devices: 42.6 us -> 42.8 us  [rotate(): return lax.ppermute(x, axis, [(i, (i + shift) % size) for i in range(size)])]
  transfers between devices with their start and end apart: 38 -> 32, of which waited for: 20 -> 17; matrix products, arithmetic and copies ran while one was open for 0% -> 0% of each run, Pallas kernels for 4% -> 0%
where the time goes in v3:
time: 107 us
  waiting for transfers between devices  46 us (43%)
  starting transfers between devices  42.5 us (40%)
  Pallas kernels  16.5 us (15%)
    ppermute x28, waiting for transfers between devices, rotate(): return lax.ppermute(x, axis, [(i, (i + shift) % size) for i in range(size)])  42.8 us
    ppermute x28, starting transfers between devices, rotate(): return lax.ppermute(x, axis, [(i, (i + shift) % size) for i in range(size)])  36.9 us
    pallas_call x12, Pallas kernels, call(): pl.pallas_call(kernel, out_shape=[jax.ShapeDtypeStruct(shape, jnp.float32...  16.5 us
    ppermute x2, starting transfers between devices, exchange(): lax.ppermute(even_pairs, axis, outer)  3.31 us
    ppermute x2, waiting for transfers between devices, exchange(): lax.ppermute(even_pairs, axis, outer)  3.24 us
    ppermute x2, starting transfers between devices, exchange(): lax.ppermute(odd_pairs, axis, inner)  2.28 us
  transfers between devices with their start and end apart: 32, of which 17 were waited for; matrix products, arithmetic and copies ran while one was open for 0% of the time, Pallas kernels for 0%

profile of v3, /device:TPU:0, one launch (start us, length us, event | category | flops | bytes accessed | tf_op | source)
XLA Modules:
  0.0 107.0 jit_solution(6303167639080164246)
XLA Ops:
  0.7 2.8 %shard_map.77 = (f32[4,8,128]{2,1,0:T(8,128)}, f32[8,16,256]{2,1,0:T(8,128)}, f32[19,16,256]{2,1,0:T(8,128)}, f32[19,16,256]{2,1,0:T(8,128)}) custom-call(f32[8,16,256]{2,1,0:T(8,128)} %refs_0_.5, f32[8,16,256]{2,1,0:T(8,128)} %refs_1_.5, f32[8,16,256]{2,1,0:T(8,128)} %refs_2_.5, f32[8,16,256]{2,1,0:T(8,128)} %refs_3_.5, s32[1,512]{1,0:T(1,128)} %bitcast.2, ...), custom_call_target="tpu_custom_call" | custom-call | tf_op jit(solution)/shard_map/pallas_call | solution.py:300
  6.7 2.8 %collective-permute-start.2 = (f32[216,256]{1,0:T(8,128)S(1)}, f32[216,256]{1,0:T(8,128)S(1)}, u32[]{:S(2)}, u32[]{:S(2)}) collective-permute-start(f32[216,256]{1,0:T(8,128)S(1)} %get-tuple-element.51), channel_id=1, source_target_pairs={{0,1},{1,0},{2,3},{3,2},{4,5},{5,4},{6,7},{7,6},{8,9},{9,8},{10,11... | collective-permute-start | bytes 663560 | tf_op jit(solution)/shard_map/ppermute | solution.py:31
  10.1 3.2 %collective-permute-done.2.refs_7_ = f32[216,256]{1,0:T(8,128)S(1)} collective-permute-done((f32[216,256]{1,0:T(8,128)S(1)}, f32[216,256]{1,0:T(8,128)S(1)}, u32[]{:S(2)}, u32[]{:S(2)}) %collective-permute-start.2) | collective-permute-done | bytes 221216 | tf_op jit(solution)/shard_map/ppermute | solution.py:31
  13.4 2.4 %shard_map.79 = (f32[16,24,256]{2,1,0:T(8,128)S(1)}, f32[16,24,256]{2,1,0:T(8,128)S(1)}, f32[16,24,256]{2,1,0:T(8,128)S(1)}, f32[16,24,256]{2,1,0:T(8,128)S(1)},...) custom-call(f32[8,16,256]{2,1,0:T(8,128)S(1)} %copy-done, ...), custom_call_target="tpu_custom_call" | custom-call | tf_op jit(solution)/shard_map/pallas_call | solution.py:300
  15.8 4.1 %collective-permute-start.6 = (f32[8,8,128]{2,1,0:T(8,128)S(1)}, f32[8,8,128]{2,1,0:T(8,128)S(1)}, u32[]{:S(2)}, u32[]{:S(2)}) collective-permute-start(f32[8,8,128]{2,1,0:T(8,128)S(1)} %get-tuple-element.54), channel_id=1, source_target_pairs={{0,3},{1,0},{2,1},{3,2},{4,7},{5,4},{6,5},{7,6},{8,11},{9,8},{10,9... | collective-permute-start | bytes 98312 | tf_op jit(solution)/shard_map/ppermute | solution.py:22
  19.9 2.5 %collective-permute-start.5 = (f32[8,8,128]{2,1,0:T(8,128)S(1)}, f32[8,8,128]{2,1,0:T(8,128)S(1)}, u32[]{:S(2)}, u32[]{:S(2)}) collective-permute-start(f32[8,8,128]{2,1,0:T(8,128)S(1)} %get-tuple-element.54), channel_id=1, source_target_pairs={{0,2},{1,3},{2,0},{3,1},{4,6},{5,7},{6,4},{7,5},{8,10},{9,11},{10,... | collective-permute-start | bytes 98312 | tf_op jit(solution)/shard_map/ppermute | solution.py:22
  22.4 1.9 %collective-permute-start.4 = (f32[8,8,128]{2,1,0:T(8,128)S(1)}, f32[8,8,128]{2,1,0:T(8,128)S(1)}, u32[]{:S(2)}, u32[]{:S(2)}) collective-permute-start(f32[8,8,128]{2,1,0:T(8,128)S(1)} %get-tuple-element.54), channel_id=1, source_target_pairs={{0,1},{1,2},{2,3},{3,0},{4,5},{5,6},{6,7},{7,4},{8,9},{9,10},{10,1... | collective-permute-start | bytes 98312 | tf_op jit(solution)/shard_map/ppermute | solution.py:22
  24.4 3.8 %collective-permute-done.4 = f32[8,8,128]{2,1,0:T(8,128)S(1)} collective-permute-done((f32[8,8,128]{2,1,0:T(8,128)S(1)}, f32[8,8,128]{2,1,0:T(8,128)S(1)}, u32[]{:S(2)}, u32[]{:S(2)}) %collective-permute-start.4) | collective-permute-done | bytes 32800 | tf_op jit(solution)/shard_map/ppermute | solution.py:22
  28.2 9.2 %collective-permute-start.8 = (f32[32,8,128]{2,1,0:T(8,128)S(1)}, f32[32,8,128]{2,1,0:T(8,128)S(1)}, u32[]{:S(2)}, u32[]{:S(2)}) collective-permute-start(f32[32,8,128]{2,1,0:T(8,128)S(1)} %constant_dynamic-update-slice_fusion.refs_0_), channel_id=1, source_target_pairs={{0,8},{4,12},{8,0},{12,4},{1,9},{5,13},{9,1},{13,5},{2,10},{6,14},... | collective-permute-start | bytes 393224 | tf_op jit(solution)/shard_map/ppermute | solution.py:22
  37.8 6.5 %collective-permute-done.8.refs_2_ = f32[32,8,128]{2,1,0:T(8,128)S(1)} collective-permute-done((f32[32,8,128]{2,1,0:T(8,128)S(1)}, f32[32,8,128]{2,1,0:T(8,128)S(1)}, u32[]{:S(2)}, u32[]{:S(2)}) %collective-permute-start.8) | collective-permute-done | bytes 131104 | tf_op jit(solution)/shard_map/ppermute | solution.py:22
  44.9 2.5 %shard_map.82 = (f32[5,8,128]{2,1,0:T(8,128)S(1)}, f32[16,24,256]{2,1,0:T(8,128)S(1)}, f32[16,24,256]{2,1,0:T(8,128)S(1)}) custom-call(f32[32,8,128]{2,1,0:T(8,128)S(1)} %constant_dynamic-update-slice_fusion.refs_0_, f32[32,8,128]{2,1,0:T(8,128)S(1)} %collective-permute-done.7.refs_1_, f32[32,8,128]{2,1,0:T(8,128)S(1)} %collective-permute-done.8.refs_2_, ...), custom_call_target="tpu_custom_call" | custom-call | tf_op jit(solution)/shard_map/pallas_call | solution.py:300
  49.5 5.2 %collective-permute-done.10 = f32[5,8,128]{2,1,0:T(8,128)S(1)} collective-permute-done((f32[5,8,128]{2,1,0:T(8,128)S(1)}, f32[5,8,128]{2,1,0:T(8,128)S(1)}, u32[]{:S(2)}, u32[]{:S(2)}) %collective-permute-start.10) | collective-permute-done | bytes 20512 | tf_op jit(solution)/shard_map/ppermute | solution.py:22
  55.3 2.3 %collective-permute-done.15.refs_3_ = f32[20,8,128]{2,1,0:T(8,128)S(1)} collective-permute-done((f32[20,8,128]{2,1,0:T(8,128)S(1)}, f32[20,8,128]{2,1,0:T(8,128)S(1)}, u32[]{:S(2)}, u32[]{:S(2)}) %collective-permute-start.15) | collective-permute-done | bytes 81952 | tf_op jit(solution)/shard_map/ppermute | solution.py:22
  57.5 2.6 %collective-permute-done.14.refs_2_ = f32[20,8,128]{2,1,0:T(8,128)S(1)} collective-permute-done((f32[20,8,128]{2,1,0:T(8,128)S(1)}, f32[20,8,128]{2,1,0:T(8,128)S(1)}, u32[]{:S(2)}, u32[]{:S(2)}) %collective-permute-start.14) | collective-permute-done | bytes 81952 | tf_op jit(solution)/shard_map/ppermute | solution.py:22
  66.2 3.8 %collective-permute-start.19 = (f32[48,256]{1,0:T(8,128)S(1)}, f32[48,256]{1,0:T(8,128)S(1)}, u32[]{:S(2)}, u32[]{:S(2)}) collective-permute-start(f32[48,256]{1,0:T(8,128)S(1)} %get-tuple-element.81), channel_id=1, source_target_pairs={{0,3},{1,0},{2,1},{3,2},{4,7},{5,4},{6,5},{7,6},{8,11},{9,8},{10,9... | collective-permute-start | bytes 147464 | tf_op jit(solution)/shard_map/ppermute | solution.py:22
  70.0 2.2 %collective-permute-done.18.before = f32[48,256]{1,0:T(8,128)S(1)} collective-permute-done((f32[48,256]{1,0:T(8,128)S(1)}, f32[48,256]{1,0:T(8,128)S(1)}, u32[]{:S(2)}, u32[]{:S(2)}) %collective-permute-start.18) | collective-permute-done | bytes 49184 | tf_op jit(solution)/shard_map/ppermute | solution.py:22
  73.0 4.2 %collective-permute-start.22 = (f32[5,8,128]{2,1,0:T(8,128)S(1)}, f32[5,8,128]{2,1,0:T(8,128)S(1)}, u32[]{:S(2)}, u32[]{:S(2)}) collective-permute-start(f32[5,8,128]{2,1,0:T(8,128)S(1)} %get-tuple-element.83), channel_id=1, source_target_pairs={{0,3},{1,0},{2,1},{3,2},{4,7},{5,4},{6,5},{7,6},{8,11},{9,8},{10,9... | collective-permute-start | bytes 61448 | tf_op jit(solution)/shard_map/ppermute | solution.py:22
  77.8 4.9 %collective-permute-done.20 = f32[5,8,128]{2,1,0:T(8,128)S(1)} collective-permute-done((f32[5,8,128]{2,1,0:T(8,128)S(1)}, f32[5,8,128]{2,1,0:T(8,128)S(1)}, u32[]{:S(2)}, u32[]{:S(2)}) %collective-permute-start.20) | collective-permute-done | bytes 20512 | tf_op jit(solution)/shard_map/ppermute | solution.py:22
  85.2 3.2 %collective-permute-done.24.refs_2_ = f32[20,8,128]{2,1,0:T(8,128)S(1)} collective-permute-done((f32[20,8,128]{2,1,0:T(8,128)S(1)}, f32[20,8,128]{2,1,0:T(8,128)S(1)}, u32[]{:S(2)}, u32[]{:S(2)}) %collective-permute-start.24) | collective-permute-done | bytes 81952 | tf_op jit(solution)/shard_map/ppermute | solution.py:22
  88.9 2.5 %shard_map.87 = (f32[5,8,128]{2,1,0:T(8,128)S(1)}, f32[16,24,256]{2,1,0:T(8,128)S(1)}, f32[8,24,256]{2,1,0:T(8,128)S(1)}, f32[8,24,256]{2,1,0:T(8,128)S(1)}, f32[8,128]{1,0:T(8,128)S(1)}) custom-call(f32[20,8,128]{2,1,0:T(8,128)S(1)} %constant_dynamic-update-slice_fusion.8.refs_0_, f32[20,8,128]{2,1,0:T(8,128)S(1)} %collective-permute-done.23.refs_1_, ...), custom_call_target="tpu_custom_call" | custom-call | tf_op jit(solution)/shard_map/pallas_call | solution.py:300
  92.6 1.9 %collective-permute-start.26 = (f32[5,8,128]{2,1,0:T(8,128)S(1)}, f32[5,8,128]{2,1,0:T(8,128)S(1)}, u32[]{:S(2)}, u32[]{:S(2)}) collective-permute-start(f32[5,8,128]{2,1,0:T(8,128)S(1)} %get-tuple-element.88), channel_id=1, source_target_pairs={{0,1},{1,2},{2,3},{3,0},{4,5},{5,6},{6,7},{7,4},{8,9},{9,10},{10,1... | collective-permute-start | bytes 61448 | tf_op jit(solution)/shard_map/ppermute | solution.py:22
  94.6 3.6 %collective-permute-done.26 = f32[5,8,128]{2,1,0:T(8,128)S(1)} collective-permute-done((f32[5,8,128]{2,1,0:T(8,128)S(1)}, f32[5,8,128]{2,1,0:T(8,128)S(1)}, u32[]{:S(2)}, u32[]{:S(2)}) %collective-permute-start.26) | collective-permute-done | bytes 20512 | tf_op jit(solution)/shard_map/ppermute | solution.py:22
  100.5 3.3 %collective-permute-done.30.refs_2_ = f32[20,8,128]{2,1,0:T(8,128)S(1)} collective-permute-done((f32[20,8,128]{2,1,0:T(8,128)S(1)}, f32[20,8,128]{2,1,0:T(8,128)S(1)}, u32[]{:S(2)}, u32[]{:S(2)}) %collective-permute-start.30) | collective-permute-done | bytes 81952 | tf_op jit(solution)/shard_map/ppermute | solution.py:22
  104.4 2.6 %shard_map.88 = (f32[8,16,256]{2,1,0:T(8,128)}, f32[8,16,256]{2,1,0:T(8,128)}) custom-call(f32[20,8,128]{2,1,0:T(8,128)S(1)} %constant_dynamic-update-slice_fusion.12.refs_0_, f32[20,8,128]{2,1,0:T(8,128)S(1)} %collective-permute-done.29.refs_1_, f32[20,8,128]{2,1,0:T(8,128)S(1)} %collective-permute-done.30.refs_2_, ...), custom_call_target="tpu_custom_call" | custom-call | tf_op jit(solution)/shard_map/pallas_call | solution.py:300
  (80 shorter events, 22.1 us)
Async XLA Ops:
  6.7 6.7 %collective-permute-start.2 = (f32[216,256]{1,0:T(8,128)S(1)}, f32[216,256]{1,0:T(8,128)S(1)}, u32[]{:S(2)}, u32[]{:S(2)}) collective-permute-start(f32[216,256]{1,0:T(8,128)S(1)} %get-tuple-element.51), channel_id=1, source_target_pairs={{0,1},{1,0},{2,3},{3,2},{4,5},{5,4},{6,7},{7,6},{8,9},{9,8},{10,11... | collective-permute-start | bytes 663560 | tf_op jit(solution)/shard_map/ppermute | solution.py:31
  15.8 12.4 %collective-permute-start.6 = (f32[8,8,128]{2,1,0:T(8,128)S(1)}, f32[8,8,128]{2,1,0:T(8,128)S(1)}, u32[]{:S(2)}, u32[]{:S(2)}) collective-permute-start(f32[8,8,128]{2,1,0:T(8,128)S(1)} %get-tuple-element.54), channel_id=1, source_target_pairs={{0,3},{1,0},{2,1},{3,2},{4,7},{5,4},{6,5},{7,6},{8,11},{9,8},{10,9... | collective-permute-start | bytes 98312 | tf_op jit(solution)/shard_map/ppermute | solution.py:22
  19.9 8.2 %collective-permute-start.5 = (f32[8,8,128]{2,1,0:T(8,128)S(1)}, f32[8,8,128]{2,1,0:T(8,128)S(1)}, u32[]{:S(2)}, u32[]{:S(2)}) collective-permute-start(f32[8,8,128]{2,1,0:T(8,128)S(1)} %get-tuple-element.54), channel_id=1, source_target_pairs={{0,2},{1,3},{2,0},{3,1},{4,6},{5,7},{6,4},{7,5},{8,10},{9,11},{10,... | collective-permute-start | bytes 98312 | tf_op jit(solution)/shard_map/ppermute | solution.py:22
  22.4 5.7 %collective-permute-start.4 = (f32[8,8,128]{2,1,0:T(8,128)S(1)}, f32[8,8,128]{2,1,0:T(8,128)S(1)}, u32[]{:S(2)}, u32[]{:S(2)}) collective-permute-start(f32[8,8,128]{2,1,0:T(8,128)S(1)} %get-tuple-element.54), channel_id=1, source_target_pairs={{0,1},{1,2},{2,3},{3,0},{4,5},{5,6},{6,7},{7,4},{8,9},{9,10},{10,1... | collective-permute-start | bytes 98312 | tf_op jit(solution)/shard_map/ppermute | solution.py:22
  28.2 9.6 %collective-permute-start.9 = (f32[32,8,128]{2,1,0:T(8,128)S(1)}, f32[32,8,128]{2,1,0:T(8,128)S(1)}, u32[]{:S(2)}, u32[]{:S(2)}) collective-permute-start(f32[32,8,128]{2,1,0:T(8,128)S(1)} %constant_dynamic-update-slice_fusion.refs_0_), channel_id=1, source_target_pairs={{0,12},{4,0},{8,4},{12,8},{1,13},{5,1},{9,5},{13,9},{2,14},{6,2},{... | collective-permute-start | bytes 393224 | tf_op jit(solution)/shard_map/ppermute | solution.py:22
  28.2 16.1 %collective-permute-start.8 = (f32[32,8,128]{2,1,0:T(8,128)S(1)}, f32[32,8,128]{2,1,0:T(8,128)S(1)}, u32[]{:S(2)}, u32[]{:S(2)}) collective-permute-start(f32[32,8,128]{2,1,0:T(8,128)S(1)} %constant_dynamic-update-slice_fusion.refs_0_), channel_id=1, source_target_pairs={{0,8},{4,12},{8,0},{12,4},{1,9},{5,13},{9,1},{13,5},{2,10},{6,14},... | collective-permute-start | bytes 393224 | tf_op jit(solution)/shard_map/ppermute | solution.py:22
  37.4 6.9 %collective-permute-start.7 = (f32[32,8,128]{2,1,0:T(8,128)S(1)}, f32[32,8,128]{2,1,0:T(8,128)S(1)}, u32[]{:S(2)}, u32[]{:S(2)}) collective-permute-start(f32[32,8,128]{2,1,0:T(8,128)S(1)} %constant_dynamic-update-slice_fusion.refs_0_), channel_id=1, source_target_pairs={{0,4},{4,8},{8,12},{12,0},{1,5},{5,9},{9,13},{13,1},{2,6},{6,10},{... | collective-permute-start | bytes 393224 | tf_op jit(solution)/shard_map/ppermute | solution.py:22
  47.4 7.3 %collective-permute-start.12 = (f32[5,8,128]{2,1,0:T(8,128)S(1)}, f32[5,8,128]{2,1,0:T(8,128)S(1)}, u32[]{:S(2)}, u32[]{:S(2)}) collective-permute-start(f32[5,8,128]{2,1,0:T(8,128)S(1)} %get-tuple-element.70), channel_id=1, source_target_pairs={{0,3},{1,0},{2,1},{3,2},{4,7},{5,4},{6,5},{7,6},{8,11},{9,8},{10,9... | collective-permute-start | bytes 61448 | tf_op jit(solution)/shard_map/ppermute | solution.py:22
  47.9 6.7 %collective-permute-start.11 = (f32[5,8,128]{2,1,0:T(8,128)S(1)}, f32[5,8,128]{2,1,0:T(8,128)S(1)}, u32[]{:S(2)}, u32[]{:S(2)}) collective-permute-start(f32[5,8,128]{2,1,0:T(8,128)S(1)} %get-tuple-element.70), channel_id=1, source_target_pairs={{0,2},{1,3},{2,0},{3,1},{4,6},{5,7},{6,4},{7,5},{8,10},{9,11},{10,... | collective-permute-start | bytes 61448 | tf_op jit(solution)/shard_map/ppermute | solution.py:22
  49.0 5.6 %collective-permute-start.10 = (f32[5,8,128]{2,1,0:T(8,128)S(1)}, f32[5,8,128]{2,1,0:T(8,128)S(1)}, u32[]{:S(2)}, u32[]{:S(2)}) collective-permute-start(f32[5,8,128]{2,1,0:T(8,128)S(1)} %get-tuple-element.70), channel_id=1, source_target_pairs={{0,1},{1,2},{2,3},{3,0},{4,5},{5,6},{6,7},{7,4},{8,9},{9,10},{10,1... | collective-permute-start | bytes 61448 | tf_op jit(solution)/shard_map/ppermute | solution.py:22
  54.7 5.4 %collective-permute-start.14 = (f32[20,8,128]{2,1,0:T(8,128)S(1)}, f32[20,8,128]{2,1,0:T(8,128)S(1)}, u32[]{:S(2)}, u32[]{:S(2)}) collective-permute-start(f32[20,8,128]{2,1,0:T(8,128)S(1)} %constant_dynamic-update-slice_fusion.4.refs_0_), channel_id=1, source_target_pairs={{0,8},{4,12},{8,0},{12,4},{1,9},{5,13},{9,1},{13,5},{2,10},{6,14},... | collective-permute-start | bytes 245768 | tf_op jit(solution)/shard_map/ppermute | solution.py:22
  55.1 5.3 %collective-permute-start.13 = (f32[20,8,128]{2,1,0:T(8,128)S(1)}, f32[20,8,128]{2,1,0:T(8,128)S(1)}, u32[]{:S(2)}, u32[]{:S(2)}) collective-permute-start(f32[20,8,128]{2,1,0:T(8,128)S(1)} %constant_dynamic-update-slice_fusion.4.refs_0_), channel_id=1, source_target_pairs={{0,4},{4,8},{8,12},{12,0},{1,5},{5,9},{9,13},{13,1},{2,6},{6,10},{... | collective-permute-start | bytes 245768 | tf_op jit(solution)/shard_map/ppermute | solution.py:22
  66.1 6.1 %collective-permute-start.18 = (f32[48,256]{1,0:T(8,128)S(1)}, f32[48,256]{1,0:T(8,128)S(1)}, u32[]{:S(2)}, u32[]{:S(2)}) collective-permute-start(f32[48,256]{1,0:T(8,128)S(1)} %get-tuple-element.80), channel_id=1, source_target_pairs={{0,1},{1,2},{2,3},{3,0},{4,5},{5,6},{6,7},{7,4},{8,9},{9,10},{10,1... | collective-permute-start | bytes 147464 | tf_op jit(solution)/shard_map/ppermute | solution.py:22
  66.2 6.0 %collective-permute-start.19 = (f32[48,256]{1,0:T(8,128)S(1)}, f32[48,256]{1,0:T(8,128)S(1)}, u32[]{:S(2)}, u32[]{:S(2)}) collective-permute-start(f32[48,256]{1,0:T(8,128)S(1)} %get-tuple-element.81), channel_id=1, source_target_pairs={{0,3},{1,0},{2,1},{3,2},{4,7},{5,4},{6,5},{7,6},{8,11},{9,8},{10,9... | collective-permute-start | bytes 147464 | tf_op jit(solution)/shard_map/ppermute | solution.py:22
  73.0 9.8 %collective-permute-start.22 = (f32[5,8,128]{2,1,0:T(8,128)S(1)}, f32[5,8,128]{2,1,0:T(8,128)S(1)}, u32[]{:S(2)}, u32[]{:S(2)}) collective-permute-start(f32[5,8,128]{2,1,0:T(8,128)S(1)} %get-tuple-element.83), channel_id=1, source_target_pairs={{0,3},{1,0},{2,1},{3,2},{4,7},{5,4},{6,5},{7,6},{8,11},{9,8},{10,9... | collective-permute-start | bytes 61448 | tf_op jit(solution)/shard_map/ppermute | solution.py:22
  77.2 5.6 %collective-permute-start.21 = (f32[5,8,128]{2,1,0:T(8,128)S(1)}, f32[5,8,128]{2,1,0:T(8,128)S(1)}, u32[]{:S(2)}, u32[]{:S(2)}) collective-permute-start(f32[5,8,128]{2,1,0:T(8,128)S(1)} %get-tuple-element.83), channel_id=1, source_target_pairs={{0,2},{1,3},{2,0},{3,1},{4,6},{5,7},{6,4},{7,5},{8,10},{9,11},{10,... | collective-permute-start | bytes 61448 | tf_op jit(solution)/shard_map/ppermute | solution.py:22
  77.2 5.6 %collective-permute-start.20 = (f32[5,8,128]{2,1,0:T(8,128)S(1)}, f32[5,8,128]{2,1,0:T(8,128)S(1)}, u32[]{:S(2)}, u32[]{:S(2)}) collective-permute-start(f32[5,8,128]{2,1,0:T(8,128)S(1)} %get-tuple-element.83), channel_id=1, source_target_pairs={{0,1},{1,2},{2,3},{3,0},{4,5},{5,6},{6,7},{7,4},{8,9},{9,10},{10,1... | collective-permute-start | bytes 61448 | tf_op jit(solution)/shard_map/ppermute | solution.py:22
  82.9 5.5 %collective-permute-start.24 = (f32[20,8,128]{2,1,0:T(8,128)S(1)}, f32[20,8,128]{2,1,0:T(8,128)S(1)}, u32[]{:S(2)}, u32[]{:S(2)}) collective-permute-start(f32[20,8,128]{2,1,0:T(8,128)S(1)} %constant_dynamic-update-slice_fusion.8.refs_0_), channel_id=1, source_target_pairs={{0,8},{4,12},{8,0},{12,4},{1,9},{5,13},{9,1},{13,5},{2,10},{6,14},... | collective-permute-start | bytes 245768 | tf_op jit(solution)/shard_map/ppermute | solution.py:22
  83.9 5.0 %collective-permute-start.23 = (f32[20,8,128]{2,1,0:T(8,128)S(1)}, f32[20,8,128]{2,1,0:T(8,128)S(1)}, u32[]{:S(2)}, u32[]{:S(2)}) collective-permute-start(f32[20,8,128]{2,1,0:T(8,128)S(1)} %constant_dynamic-update-slice_fusion.8.refs_0_), channel_id=1, source_target_pairs={{0,4},{4,8},{8,12},{12,0},{1,5},{5,9},{9,13},{13,1},{2,6},{6,10},{... | collective-permute-start | bytes 245768 | tf_op jit(solution)/shard_map/ppermute | solution.py:22
  91.4 6.8 %collective-permute-start.28 = (f32[5,8,128]{2,1,0:T(8,128)S(1)}, f32[5,8,128]{2,1,0:T(8,128)S(1)}, u32[]{:S(2)}, u32[]{:S(2)}) collective-permute-start(f32[5,8,128]{2,1,0:T(8,128)S(1)} %get-tuple-element.88), channel_id=1, source_target_pairs={{0,3},{1,0},{2,1},{3,2},{4,7},{5,4},{6,5},{7,6},{8,11},{9,8},{10,9... | collective-permute-start | bytes 61448 | tf_op jit(solution)/shard_map/ppermute | solution.py:22
  92.0 6.2 %collective-permute-start.27 = (f32[5,8,128]{2,1,0:T(8,128)S(1)}, f32[5,8,128]{2,1,0:T(8,128)S(1)}, u32[]{:S(2)}, u32[]{:S(2)}) collective-permute-start(f32[5,8,128]{2,1,0:T(8,128)S(1)} %get-tuple-element.88), channel_id=1, source_target_pairs={{0,2},{1,3},{2,0},{3,1},{4,6},{5,7},{6,4},{7,5},{8,10},{9,11},{10,... | collective-permute-start | bytes 61448 | tf_op jit(solution)/shard_map/ppermute | solution.py:22
  92.6 5.6 %collective-permute-start.26 = (f32[5,8,128]{2,1,0:T(8,128)S(1)}, f32[5,8,128]{2,1,0:T(8,128)S(1)}, u32[]{:S(2)}, u32[]{:S(2)}) collective-permute-start(f32[5,8,128]{2,1,0:T(8,128)S(1)} %get-tuple-element.88), channel_id=1, source_target_pairs={{0,1},{1,2},{2,3},{3,0},{4,5},{5,6},{6,7},{7,4},{8,9},{9,10},{10,1... | collective-permute-start | bytes 61448 | tf_op jit(solution)/shard_map/ppermute | solution.py:22
  98.3 5.6 %collective-permute-start.30 = (f32[20,8,128]{2,1,0:T(8,128)S(1)}, f32[20,8,128]{2,1,0:T(8,128)S(1)}, u32[]{:S(2)}, u32[]{:S(2)}) collective-permute-start(f32[20,8,128]{2,1,0:T(8,128)S(1)} %constant_dynamic-update-slice_fusion.12.refs_0_), channel_id=1, source_target_pairs={{0,8},{4,12},{8,0},{12,4},{1,9},{5,13},{9,1},{13,5},{2,10},{6,14},... | collective-permute-start | bytes 245768 | tf_op jit(solution)/shard_map/ppermute | solution.py:22
  99.4 5.0 %collective-permute-start.29 = (f32[20,8,128]{2,1,0:T(8,128)S(1)}, f32[20,8,128]{2,1,0:T(8,128)S(1)}, u32[]{:S(2)}, u32[]{:S(2)}) collective-permute-start(f32[20,8,128]{2,1,0:T(8,128)S(1)} %constant_dynamic-update-slice_fusion.12.refs_0_), channel_id=1, source_target_pairs={{0,4},{4,8},{8,12},{12,0},{1,5},{5,9},{9,13},{13,1},{2,6},{6,10},{... | collective-permute-start | bytes 245768 | tf_op jit(solution)/shard_map/ppermute | solution.py:22
  (14 other events, 50.1 us)

commit v4 on v3

--- a/solution.py
+++ b/solution.py
@@ -137,6 +137,42 @@
             for x in range(planes):
                 block = refs[s][t * per + first + x]
                 whole_ref[at_x + x, pl.ds(row, block_rows), :] = block
+
+
+def placed_overlapping(refs, place, sizes, shape, per, room, whole_ref):
+    planes, block_rows, lanes = shape
+    sub = iota((block_rows, lanes), 0)
+    last, first = sub == block_rows - 1, sub == 0
+
+    def spots():
+        for s in range(sizes[0]):
+            at_x = lax.rem(place[0] - s + sizes[0], sizes[0]) * planes
+            for t in range(sizes[1]):
+                at_y = lax.rem(place[1] - t + sizes[1], sizes[1])
+                row = pl.multiple_of(at_y * block_rows, block_rows)
+                yield refs[s], t * per, at_x, row
+
+    for ref, tile, at_x, row in spots():
+        for x in range(planes):
+            room[at_x + x + 1, pl.ds(row + block_rows, block_rows), :] = ref[tile + x]
+    for ref, tile, at_x, row in spots():
+        adds = [(0, 1, ref[tile + planes]), (planes + 1, 1, ref[tile + planes + 1])]
+        pairs = [(x + 1, ref[tile + planes + 2], 2 * x) for x in range(planes)]
+        pairs += [(0, ref[tile + planes + 3], 0), (planes + 1, ref[tile + planes + 3], 2)]
+        for x, borders, at in pairs:
+            before = shifted(borders, block_rows - 1 - at, 0)
+            after = shifted(borders, -(at + 1), 0)
+            adds.append((x, 0, jnp.where(last, before, 0.0)))
+            adds.append((x, 2, jnp.where(first, after, 0.0)))
+        spans = [
+            (at_x + x, pl.ds(row + step * block_rows, block_rows)) for x, step, _ in adds
+        ]
+        values = [room[x, span, :] + add for (x, span), (_, _, add) in zip(spans, adds)]
+        for (x, span), value in zip(spans, values):
+            room[x, span, :] = value
+    rows = block_rows * sizes[1]
+    for x in range(planes * sizes[0]):
+        whole_ref[x, :rows, :] = room[x + 1, block_rows : block_rows + rows, :]
 
 
 def summed_tiles(refs, sizes, per, index):
@@ -360,10 +396,17 @@
     )
 
 
+def gathered_row(own):
+    size = lax.axis_size("gy")
+    return jnp.concatenate([own] + [rotate(own, "gy", t) for t in range(1, size)], axis=0)
+
+
+def gathered_rows(row):
+    return [row] + [rotate(row, "gx", s) for s in range(1, lax.axis_size("gx"))]
+
+
 def gathered(own):
-    size_x, size_y = lax.axis_size("gx"), lax.axis_size("gy")
-    row = jnp.concatenate([own] + [rotate(own, "gy", t) for t in range(1, size_y)], axis=0)
-    return [row] + [rotate(row, "gx", s) for s in range(1, size_x)]
+    return gathered_rows(gathered_row(own))
 
 
 FIELD_DEPTHS = (DEEP, HALO, HALO, HALO, WIDE)
@@ -627,10 +670,13 @@
             (kept,) = take(1)
         else:
             combined, curved_out, norm_ref = take(3)
-        source, whole_mid, pairs, mid = take(4)
+        source, whole_mid, pairs, mid, *room = refs[at:]
         frame_rows = iota((rows, lanes), 0)
         own_rows = (frame_rows >= HALO) & (frame_rows < rows - HALO)
-        placed_whole(blocks, place, sizes, coarse, per, 0, source)
+        if first_time:
+            placed_whole(blocks, place, sizes, coarse, per, 0, source)
+        else:
+            placed_overlapping(blocks, place, sizes, coarse, per, room[0], source)
         correction = coarse_correction(
             place, coarse, source, whole_mid, pairs, levels[:4], levels[4:]
         )
@@ -643,7 +689,8 @@
                 forms = forms + d * curved[x]
                 squares = squares + d * d
         else:
-            norm = total(summed_tiles(blocks, sizes, per, coarse[0]))
+            tile = summed_tiles(blocks, sizes, per, per - 1)
+            norm = total(jnp.where(iota(tile.shape, 0) >= 4, tile, 0.0))
             ratio = norm / old[2][0:1, 0:1]
             for x in range(own_x):
                 d = direction[x + HALO] + ratio * old[1][x + HALO]
@@ -680,10 +727,11 @@
 
     frame = (planes, rows, lanes)
     own = (own_x, rows, lanes)
+    margin = (coarse[0] * sizes[0] + 2, coarse[1] * (sizes[1] + 2), coarse[2])
     return call(
         kernel,
         [(coarse[0] + 1,) + coarse[1:], frame] + ([frame] if first_time else [own, own, (8, 128)]),
-        coarse_scratch(coarse, sizes) + [frame],
+        coarse_scratch(coarse, sizes) + [frame] + ([] if first_time else [margin]),
         inputs,
     )
 
@@ -720,6 +768,68 @@
     return out
 
 
+def own_restricted(direction, cond, faces, fine, squares, out_ref):
+    fx, fy, fz, rd = fine
+    hux, huy, huz, nbu = faces
+    first, last = min(direction), max(direction)
+    own_x = last - first + 1
+    rows, lanes = direction[first].shape
+    q = {x: cond[x] * direction[x] for x in direction}
+    along_x = {first: hux[first] * q[first], last + 1: hux[last + 1] * q[last]}
+    for x in range(first + 1, last + 1):
+        along_x[x] = hux[x] * (q[x] + q[x - 1])
+    z = {first - 1: -along_x[first], last + 1: along_x[last + 1]}
+    for x in direction:
+        mid = q[x]
+        along_y = huy[x] * (mid + shifted(mid, 1, 0))
+        along_z = huz[x] * (mid + shifted(mid, 1, 1))
+        value = along_x[x] - along_x[x + 1] + nbu[x] * mid
+        value = value + (along_y - shifted(along_y, -1, 0))
+        z[x] = value + (along_z - shifted(along_z, -1, 1))
+    iterate = {x: rd[x] * z[x] for x in z}
+    planes = [fx[first - 1] * iterate[first - 1]]
+    for x in range(first - 1, last + 2):
+        off = off_diagonal(
+            iterate[x], iterate.get(x - 1), iterate.get(x + 1),
+            fx[x], fx[x + 1], fy[x], fz[x],
+        )
+        planes.append(KEPT * z[x] + off)
+    planes[0] = fx[first - 1] * iterate[first - 1]
+    planes.append(fx[last + 2] * iterate[last + 1])
+    margin = HALO - 2
+    block_rows = (rows - 2 * HALO) // 2
+    target = iota((2 * block_rows, rows), 0)
+    home = jnp.where(target < block_rows, target + 1, jnp.where(target == block_rows, 0, -9))
+    home = jnp.where(target == block_rows + 1, block_rows + 1, home)
+    here_row = iota((2 * block_rows, rows), 1)
+    pick = flag((here_row >= margin + 2 * home) & (here_row < margin + 2 * home + 2))
+    frame_rows = iota((rows, lanes), 0)
+    inside = (frame_rows >= margin) & (frame_rows < rows - margin)
+    halves = [
+        dot(pick, jnp.where(inside, planes[x] + planes[x + 1], 0.0))
+        for x in range(0, len(planes), 2)
+    ]
+    packed = dot(jnp.concatenate(halves, axis=0), z_pairs(lanes))
+    tops, borders = [], []
+    for x in range(len(halves)):
+        at = 2 * block_rows * x
+        tops.append(packed[at : at + block_rows])
+        borders.append(packed[at + block_rows : at + 2 * block_rows])
+    number = own_x // 2
+    for x in range(number):
+        out_ref[x] = tops[x + 1]
+    out_ref[number] = tops[0]
+    out_ref[number + 1] = tops[-1]
+    pairs = borders[1]
+    for x in range(1, number):
+        pairs = pairs + shifted(borders[x + 1], 2 * x, 0)
+    out_ref[number + 2] = pairs
+    tile = fold(squares)
+    tile = tile + shifted(tile, 4, 0)
+    corners = borders[0] + shifted(borders[-1], 2, 0)
+    out_ref[number + 3] = jnp.where(iota(tile.shape, 0) >= 4, tile, corners)
+
+
 def end_first(sizes, blocks, per, levels, fine, second, curved, cond, faces, source):
     planes, rows, lanes = second.shape
     own_x, own_y = planes - 2 * HALO, rows - 2 * HALO
@@ -738,7 +848,7 @@
         second, curved, cond = refs[12 + n : 15 + n]
         faces = refs[15 + n : 19 + n]
         source = refs[19 + n]
-        first_ref, last_ref, own_ref, tile_ref, norm_ref, step_ref = refs[20 + n : 26 + n]
+        first_ref, last_ref, own_ref, b1, norm_ref, step_ref = refs[20 + n : 26 + n]
         *scratch, hold = refs[26 + n :]
         image = image_planes(
             levels, fine, sizes, blocks, per, second, curved, cond, faces, scratch
@@ -750,23 +860,29 @@
         step = norm / form
         norm_ref[...] = jnp.broadcast_to(norm, (8, 128))
         step_ref[...] = jnp.broadcast_to(step, (8, 128))
-        squares = jnp.zeros((own_y, lanes), jnp.float32)
+        frame_rows = iota((rows, lanes), 0)
+        own_rows = (frame_rows >= HALO) & (frame_rows < rows - HALO)
+        squares = jnp.zeros((rows, lanes), jnp.float32)
+        remaining = {}
         for x in range(HALO, planes - HALO):
-            hold[x - HALO] = source[x] - step * image[x]
+            value = jnp.where(own_rows, source[x] - step * image[x], 0.0)
+            hold[x - HALO] = value
+            remaining[x] = value
+            squares = squares + value * value
+        own_restricted(remaining, cond, faces, fine, squares, b1)
         for x in range(own_x):
             value = hold[x, HALO : HALO + own_y, :]
-            squares = squares + value * value
             own_ref[x] = value
             if x < HALO:
                 first_ref[x] = value
             if x >= own_x - HALO:
                 last_ref[x - own_x + HALO] = value
-        tile_ref[0] = fold(squares)
 
     strip = (HALO, own_y, lanes)
     return call(
         kernel,
-        [strip, strip, (own_x, own_y, lanes), (1, 8, 128), (8, 128), (8, 128)],
+        [strip, strip, (own_x, own_y, lanes), (coarse + 4, own_y // 2, lanes // 2)]
+        + [(8, 128), (8, 128)],
         scratch_shapes + [(planes, rows, lanes), (own_x, rows, lanes)],
         inputs,
     )
@@ -849,16 +965,14 @@
     return call(kernel, [(rows, lanes)] * 2, [], [own, low, high])
 
 
-def begin(own, low, high, before, after, tile, cond, faces, fine):
+def begin(own, low, high, before, after, cond, faces):
     own_x, own_y, lanes = own.shape
     planes, rows = own_x + 2 * HALO, own_y + 2 * HALO
     frame = (planes, rows, lanes)
-    coarse = (own_x // 2, own_y // 2, lanes // 2)
     starts, _ = edge_rows(own_x)
 
     def kernel(
-        own, low, high, before, after, tile, cond, hux, huy, huz, nbu, fx, fy, fz, rd,
-        direction, z_out, b1,
+        own, low, high, before, after, cond, hux, huy, huz, nbu, direction, z_out
     ):
         for x in range(planes):
             if x < HALO:
@@ -882,14 +996,16 @@
         zero = jnp.zeros((rows, lanes), jnp.float32)
         z_out[0] = zero
         z_out[planes - 1] = zero
-        first_residual_stage(z, fx, fy, fz, rd, z_out, b1, planes)
-        b1[coarse[0]] = tile[0]
-
+        for x in z:
+            z_out[x] = z[x]
+
+    size = planes * rows * lanes
     return call(
         kernel,
-        [frame, frame, (coarse[0] + 1,) + coarse[1:]],
+        [frame, frame],
         [],
-        [own, low, high, before, after, tile, cond] + list(faces) + list(fine),
+        [own, low, high, before, after, cond] + list(faces),
+        cost=pl.CostEstimate(flops=20 * size, bytes_accessed=28 * size, transcendentals=0),
     )
 
 
@@ -918,16 +1034,18 @@
     b1, second, kept = middle(
         sizes, blocks, 2 * coarse[0], levels, fine, z, source, curved, weight, None
     )
-    first, last, remaining, tile, norm, step = end_first(
+    first, last, remaining, b1, norm, step = end_first(
         sizes, gathered(b1), per, levels, fine, second, curved, cond, faces, source
     )
+    row = gathered_row(b1)
     low, high = rotate(last, "gx", 1), rotate(first, "gx", -1)
     first, last = pack_edges(remaining, low, high)
+    row, first, last = lax.optimization_barrier((row, first, last))
+    blocks = gathered_rows(row)
     before, after = rotate(last, "gy", 1), rotate(first, "gy", -1)
-    direction, z, b1 = begin(remaining, low, high, before, after, tile, cond, faces, fine)
-    blocks = gathered(b1)
+    direction, z = begin(remaining, low, high, before, after, cond, faces)
     b1, second, combined, curved, norm = middle(
-        sizes, blocks, per, levels, fine, z, direction, prior_part(sizes, direction), weight,
+        sizes, blocks, per + 3, levels, fine, z, direction, prior_part(sizes, direction), weight,
         (kept, source, norm, curved),
     )
     return tuple(

time: 107 us -> 100 us (0.935)
  waiting for transfers between devices: 46 us -> 40.1 us
  starting transfers between devices: 42.5 us -> 40.7 us
    ppermute x28, waiting for transfers between devices: 42.8 us -> 36.9 us  [rotate(): return lax.ppermute(x, axis, [(i, (i + shift) % size) for i in range(size)])]
    ppermute x28, starting transfers between devices: 36.9 us -> 35.1 us  [rotate(): return lax.ppermute(x, axis, [(i, (i + shift) % size) for i in range(size)])]
  transfers between devices with their start and end apart: 32 -> 32, of which waited for: 17 -> 16; matrix products, arithmetic and copies ran while one was open for 0% -> 0% of each run, Pallas kernels for 0% -> 1%
where the time goes in v4:
time: 100 us; the launch traced here: 99.9 us
  starting transfers between devices  40.7 us (41%)
  waiting for transfers between devices  40.1 us (40%)
  Pallas kernels  17.2 us (17%)
    ppermute x28, waiting for transfers between devices, rotate(): return lax.ppermute(x, axis, [(i, (i + shift) % size) for i in range(size)])  36.9 us
    ppermute x28, starting transfers between devices, rotate(): return lax.ppermute(x, axis, [(i, (i + shift) % size) for i in range(size)])  35.1 us
    pallas_call x12, Pallas kernels, call(): pl.pallas_call(kernel, out_shape=[jax.ShapeDtypeStruct(shape, jnp.float32...  17.2 us
    ppermute x2, starting transfers between devices, exchange(): lax.ppermute(even_pairs, axis, outer)  3.31 us
    ppermute x2, waiting for transfers between devices, exchange(): lax.ppermute(even_pairs, axis, outer)  3.24 us
    ppermute x2, starting transfers between devices, exchange(): lax.ppermute(odd_pairs, axis, inner)  2.28 us
  transfers between devices with their start and end apart: 32, of which 16 were waited for; matrix products, arithmetic and copies ran while one was open for 0% of the time, Pallas kernels for 1%

profile of v4, /device:TPU:0, one launch (start us, length us, event | category | flops | bytes accessed | tf_op | source)
XLA Modules:
  0.0 99.9 jit_solution(9857313569038261106)
XLA Ops:
  0.7 2.8 %shard_map.77 = (f32[4,8,128]{2,1,0:T(8,128)}, f32[8,16,256]{2,1,0:T(8,128)}, f32[19,16,256]{2,1,0:T(8,128)}, f32[19,16,256]{2,1,0:T(8,128)}) custom-call(f32[8,16,256]{2,1,0:T(8,128)} %refs_0_.5, f32[8,16,256]{2,1,0:T(8,128)} %refs_1_.5, f32[8,16,256]{2,1,0:T(8,128)} %refs_2_.5, f32[8,16,256]{2,1,0:T(8,128)} %refs_3_.5, s32[1,512]{1,0:T(1,128)} %bitcast.2, ...), custom_call_target="tpu_custom_call" | custom-call | tf_op jit(solution)/shard_map/pallas_call | solution.py:336
  6.7 2.8 %collective-permute-start.2 = (f32[216,256]{1,0:T(8,128)S(1)}, f32[216,256]{1,0:T(8,128)S(1)}, u32[]{:S(2)}, u32[]{:S(2)}) collective-permute-start(f32[216,256]{1,0:T(8,128)S(1)} %get-tuple-element.53), channel_id=1, source_target_pairs={{0,1},{1,0},{2,3},{3,2},{4,5},{5,4},{6,7},{7,6},{8,9},{9,8},{10,11... | collective-permute-start | bytes 663560 | tf_op jit(solution)/shard_map/ppermute | solution.py:31
  10.1 3.2 %collective-permute-done.2.refs_7_ = f32[216,256]{1,0:T(8,128)S(1)} collective-permute-done((f32[216,256]{1,0:T(8,128)S(1)}, f32[216,256]{1,0:T(8,128)S(1)}, u32[]{:S(2)}, u32[]{:S(2)}) %collective-permute-start.2) | collective-permute-done | bytes 221216 | tf_op jit(solution)/shard_map/ppermute | solution.py:31
  13.4 2.4 %shard_map.79 = (f32[16,24,256]{2,1,0:T(8,128)S(1)}, f32[16,24,256]{2,1,0:T(8,128)S(1)}, f32[16,24,256]{2,1,0:T(8,128)S(1)}, f32[16,24,256]{2,1,0:T(8,128)S(1)},...) custom-call(f32[8,16,256]{2,1,0:T(8,128)S(1)} %copy-done, ...), custom_call_target="tpu_custom_call" | custom-call | tf_op jit(solution)/shard_map/pallas_call | solution.py:336
  15.8 4.1 %collective-permute-start.6 = (f32[8,8,128]{2,1,0:T(8,128)S(1)}, f32[8,8,128]{2,1,0:T(8,128)S(1)}, u32[]{:S(2)}, u32[]{:S(2)}) collective-permute-start(f32[8,8,128]{2,1,0:T(8,128)S(1)} %get-tuple-element.56), channel_id=1, source_target_pairs={{0,3},{1,0},{2,1},{3,2},{4,7},{5,4},{6,5},{7,6},{8,11},{9,8},{10,9... | collective-permute-start | bytes 98312 | tf_op jit(solution)/shard_map/ppermute | solution.py:22
  19.9 2.5 %collective-permute-start.5 = (f32[8,8,128]{2,1,0:T(8,128)S(1)}, f32[8,8,128]{2,1,0:T(8,128)S(1)}, u32[]{:S(2)}, u32[]{:S(2)}) collective-permute-start(f32[8,8,128]{2,1,0:T(8,128)S(1)} %get-tuple-element.56), channel_id=1, source_target_pairs={{0,2},{1,3},{2,0},{3,1},{4,6},{5,7},{6,4},{7,5},{8,10},{9,11},{10,... | collective-permute-start | bytes 98312 | tf_op jit(solution)/shard_map/ppermute | solution.py:22
  22.4 1.9 %collective-permute-start.4 = (f32[8,8,128]{2,1,0:T(8,128)S(1)}, f32[8,8,128]{2,1,0:T(8,128)S(1)}, u32[]{:S(2)}, u32[]{:S(2)}) collective-permute-start(f32[8,8,128]{2,1,0:T(8,128)S(1)} %get-tuple-element.56), channel_id=1, source_target_pairs={{0,1},{1,2},{2,3},{3,0},{4,5},{5,6},{6,7},{7,4},{8,9},{9,10},{10,1... | collective-permute-start | bytes 98312 | tf_op jit(solution)/shard_map/ppermute | solution.py:22
  24.4 3.8 %collective-permute-done.4 = f32[8,8,128]{2,1,0:T(8,128)S(1)} collective-permute-done((f32[8,8,128]{2,1,0:T(8,128)S(1)}, f32[8,8,128]{2,1,0:T(8,128)S(1)}, u32[]{:S(2)}, u32[]{:S(2)}) %collective-permute-start.4) | collective-permute-done | bytes 32800 | tf_op jit(solution)/shard_map/ppermute | solution.py:22
  28.2 9.2 %collective-permute-start.8 = (f32[32,8,128]{2,1,0:T(8,128)S(1)}, f32[32,8,128]{2,1,0:T(8,128)S(1)}, u32[]{:S(2)}, u32[]{:S(2)}) collective-permute-start(f32[32,8,128]{2,1,0:T(8,128)S(1)} %constant_dynamic-update-slice_fusion.refs_0_), channel_id=1, source_target_pairs={{0,8},{4,12},{8,0},{12,4},{1,9},{5,13},{9,1},{13,5},{2,10},{6,14},... | collective-permute-start | bytes 393224 | tf_op jit(solution)/shard_map/ppermute | solution.py:22
  37.8 6.5 %collective-permute-done.8.refs_2_ = f32[32,8,128]{2,1,0:T(8,128)S(1)} collective-permute-done((f32[32,8,128]{2,1,0:T(8,128)S(1)}, f32[32,8,128]{2,1,0:T(8,128)S(1)}, u32[]{:S(2)}, u32[]{:S(2)}) %collective-permute-start.8) | collective-permute-done | bytes 131104 | tf_op jit(solution)/shard_map/ppermute | solution.py:22
  44.9 2.4 %shard_map.82 = (f32[5,8,128]{2,1,0:T(8,128)S(1)}, f32[16,24,256]{2,1,0:T(8,128)S(1)}, f32[16,24,256]{2,1,0:T(8,128)S(1)}) custom-call(f32[32,8,128]{2,1,0:T(8,128)S(1)} %constant_dynamic-update-slice_fusion.refs_0_, f32[32,8,128]{2,1,0:T(8,128)S(1)} %collective-permute-done.7.refs_1_, f32[32,8,128]{2,1,0:T(8,128)S(1)} %collective-permute-done.8.refs_2_, ...), custom_call_target="tpu_custom_call" | custom-call | tf_op jit(solution)/shard_map/pallas_call | solution.py:336
  49.4 5.1 %collective-permute-done.10 = f32[5,8,128]{2,1,0:T(8,128)S(1)} collective-permute-done((f32[5,8,128]{2,1,0:T(8,128)S(1)}, f32[5,8,128]{2,1,0:T(8,128)S(1)}, u32[]{:S(2)}, u32[]{:S(2)}) %collective-permute-start.10) | collective-permute-done | bytes 20512 | tf_op jit(solution)/shard_map/ppermute | solution.py:22
  55.2 2.2 %collective-permute-done.15.refs_3_ = f32[20,8,128]{2,1,0:T(8,128)S(1)} collective-permute-done((f32[20,8,128]{2,1,0:T(8,128)S(1)}, f32[20,8,128]{2,1,0:T(8,128)S(1)}, u32[]{:S(2)}, u32[]{:S(2)}) %collective-permute-start.15) | collective-permute-done | bytes 81952 | tf_op jit(solution)/shard_map/ppermute | solution.py:22
  57.4 2.6 %collective-permute-done.14.refs_2_ = f32[20,8,128]{2,1,0:T(8,128)S(1)} collective-permute-done((f32[20,8,128]{2,1,0:T(8,128)S(1)}, f32[20,8,128]{2,1,0:T(8,128)S(1)}, u32[]{:S(2)}, u32[]{:S(2)}) %collective-permute-start.14) | collective-permute-done | bytes 81952 | tf_op jit(solution)/shard_map/ppermute | solution.py:22
  60.4 2.9 %shard_map.83 = (f32[4,16,256]{2,1,0:T(8,128)S(1)}, f32[4,16,256]{2,1,0:T(8,128)S(1)}, f32[8,16,256]{2,1,0:T(8,128)S(1)}, f32[8,8,128]{2,1,0:T(8,128)S(1)}, f32[8,128]{1,0:T(8,128)S(1)}, /*index=5*/f32[8,128]{1,0:T(8,128)S(1)}) custom-call(f32[20,8,128]{2,1,0:T(8,128)S(1)} %constant_dynamic-update-slice_fusion.4.refs_0_, ...), custom_call_target="tpu_custom_call" | custom-call | tf_op jit(solution)/shard_map/pallas_call | solution.py:336
  65.3 1.7 %collective-permute-start.20 = (f32[4,16,256]{2,1,0:T(8,128)S(1)}, f32[4,16,256]{2,1,0:T(8,128)S(1)}, u32[]{:S(2)}, u32[]{:S(2)}) collective-permute-start(f32[4,16,256]{2,1,0:T(8,128)S(1)} %get-tuple-element.82), channel_id=1, source_target_pairs={{0,12},{4,0},{8,4},{12,8},{1,13},{5,1},{9,5},{13,9},{2,14},{6,2},{... | collective-permute-start | bytes 196616 | tf_op jit(solution)/shard_map/ppermute | solution.py:22
  67.2 1.9 %collective-permute-done.17 = f32[8,8,128]{2,1,0:T(8,128)S(1)} collective-permute-done((f32[8,8,128]{2,1,0:T(8,128)S(1)}, f32[8,8,128]{2,1,0:T(8,128)S(1)}, u32[]{:S(2)}, u32[]{:S(2)}) %collective-permute-start.17) | collective-permute-done | bytes 32800 | tf_op jit(solution)/shard_map/ppermute | solution.py:22
  72.1 2.4 %collective-permute-start.24 = (f32[48,256]{1,0:T(8,128)S(1)}, f32[48,256]{1,0:T(8,128)S(1)}, u32[]{:S(2)}, u32[]{:S(2)}) collective-permute-start(f32[48,256]{1,0:T(8,128)S(1)} %get-tuple-element.86), channel_id=1, source_target_pairs={{0,1},{1,2},{2,3},{3,0},{4,5},{5,6},{6,7},{7,4},{8,9},{9,10},{10,1... | collective-permute-start | bytes 147464 | tf_op jit(solution)/shard_map/ppermute | solution.py:22
  75.9 2.5 %collective-permute-done.24.before = f32[48,256]{1,0:T(8,128)S(1)} collective-permute-done((f32[48,256]{1,0:T(8,128)S(1)}, f32[48,256]{1,0:T(8,128)S(1)}, u32[]{:S(2)}, u32[]{:S(2)}) %collective-permute-start.24) | collective-permute-done | bytes 49184 | tf_op jit(solution)/shard_map/ppermute | solution.py:22
  80.3 2.6 %shard_map.87 = (f32[5,8,128]{2,1,0:T(8,128)S(1)}, f32[16,24,256]{2,1,0:T(8,128)S(1)}, f32[8,24,256]{2,1,0:T(8,128)S(1)}, f32[8,24,256]{2,1,0:T(8,128)S(1)}, f32[8,128]{1,0:T(8,128)S(1)}) custom-call(f32[32,8,128]{2,1,0:T(8,128)S(1)} %pad_maximum_fusion.refs_0_, f32[32,8,128]{2,1,0:T(8,128)S(1)} %collective-permute-done.21.refs_1_, ...), custom_call_target="tpu_custom_call" | custom-call | tf_op jit(solution)/shard_map/pallas_call | solution.py:336
  82.9 2.7 %collective-permute-start.28 = (f32[5,8,128]{2,1,0:T(8,128)S(1)}, f32[5,8,128]{2,1,0:T(8,128)S(1)}, u32[]{:S(2)}, u32[]{:S(2)}) collective-permute-start(f32[5,8,128]{2,1,0:T(8,128)S(1)} %get-tuple-element.92), channel_id=1, source_target_pairs={{0,3},{1,0},{2,1},{3,2},{4,7},{5,4},{6,5},{7,6},{8,11},{9,8},{10,9... | collective-permute-start | bytes 61448 | tf_op jit(solution)/shard_map/ppermute | solution.py:22
  86.3 4.8 %collective-permute-done.26 = f32[5,8,128]{2,1,0:T(8,128)S(1)} collective-permute-done((f32[5,8,128]{2,1,0:T(8,128)S(1)}, f32[5,8,128]{2,1,0:T(8,128)S(1)}, u32[]{:S(2)}, u32[]{:S(2)}) %collective-permute-start.26) | collective-permute-done | bytes 20512 | tf_op jit(solution)/shard_map/ppermute | solution.py:22
  93.5 3.3 %collective-permute-done.30.refs_2_ = f32[20,8,128]{2,1,0:T(8,128)S(1)} collective-permute-done((f32[20,8,128]{2,1,0:T(8,128)S(1)}, f32[20,8,128]{2,1,0:T(8,128)S(1)}, u32[]{:S(2)}, u32[]{:S(2)}) %collective-permute-start.30) | collective-permute-done | bytes 81952 | tf_op jit(solution)/shard_map/ppermute | solution.py:22
  97.3 2.6 %shard_map.88 = (f32[8,16,256]{2,1,0:T(8,128)}, f32[8,16,256]{2,1,0:T(8,128)}) custom-call(f32[20,8,128]{2,1,0:T(8,128)S(1)} %constant_dynamic-update-slice_fusion.8.refs_0_, f32[20,8,128]{2,1,0:T(8,128)S(1)} %collective-permute-done.29.refs_1_, f32[20,8,128]{2,1,0:T(8,128)S(1)} %collective-permute-done.30.refs_2_, ...), custom_call_target="tpu_custom_call" | custom-call | tf_op jit(solution)/shard_map/pallas_call | solution.py:336
  (77 shorter events, 19.8 us)
Async XLA Ops:
  6.7 6.7 %collective-permute-start.2 = (f32[216,256]{1,0:T(8,128)S(1)}, f32[216,256]{1,0:T(8,128)S(1)}, u32[]{:S(2)}, u32[]{:S(2)}) collective-permute-start(f32[216,256]{1,0:T(8,128)S(1)} %get-tuple-element.53), channel_id=1, source_target_pairs={{0,1},{1,0},{2,3},{3,2},{4,5},{5,4},{6,7},{7,6},{8,9},{9,8},{10,11... | collective-permute-start | bytes 663560 | tf_op jit(solution)/shard_map/ppermute | solution.py:31
  15.8 12.4 %collective-permute-start.6 = (f32[8,8,128]{2,1,0:T(8,128)S(1)}, f32[8,8,128]{2,1,0:T(8,128)S(1)}, u32[]{:S(2)}, u32[]{:S(2)}) collective-permute-start(f32[8,8,128]{2,1,0:T(8,128)S(1)} %get-tuple-element.56), channel_id=1, source_target_pairs={{0,3},{1,0},{2,1},{3,2},{4,7},{5,4},{6,5},{7,6},{8,11},{9,8},{10,9... | collective-permute-start | bytes 98312 | tf_op jit(solution)/shard_map/ppermute | solution.py:22
  19.9 8.2 %collective-permute-start.5 = (f32[8,8,128]{2,1,0:T(8,128)S(1)}, f32[8,8,128]{2,1,0:T(8,128)S(1)}, u32[]{:S(2)}, u32[]{:S(2)}) collective-permute-start(f32[8,8,128]{2,1,0:T(8,128)S(1)} %get-tuple-element.56), channel_id=1, source_target_pairs={{0,2},{1,3},{2,0},{3,1},{4,6},{5,7},{6,4},{7,5},{8,10},{9,11},{10,... | collective-permute-start | bytes 98312 | tf_op jit(solution)/shard_map/ppermute | solution.py:22
  22.4 5.7 %collective-permute-start.4 = (f32[8,8,128]{2,1,0:T(8,128)S(1)}, f32[8,8,128]{2,1,0:T(8,128)S(1)}, u32[]{:S(2)}, u32[]{:S(2)}) collective-permute-start(f32[8,8,128]{2,1,0:T(8,128)S(1)} %get-tuple-element.56), channel_id=1, source_target_pairs={{0,1},{1,2},{2,3},{3,0},{4,5},{5,6},{6,7},{7,4},{8,9},{9,10},{10,1... | collective-permute-start | bytes 98312 | tf_op jit(solution)/shard_map/ppermute | solution.py:22
  28.2 9.6 %collective-permute-start.9 = (f32[32,8,128]{2,1,0:T(8,128)S(1)}, f32[32,8,128]{2,1,0:T(8,128)S(1)}, u32[]{:S(2)}, u32[]{:S(2)}) collective-permute-start(f32[32,8,128]{2,1,0:T(8,128)S(1)} %constant_dynamic-update-slice_fusion.refs_0_), channel_id=1, source_target_pairs={{0,12},{4,0},{8,4},{12,8},{1,13},{5,1},{9,5},{13,9},{2,14},{6,2},{... | collective-permute-start | bytes 393224 | tf_op jit(solution)/shard_map/ppermute | solution.py:22
  28.2 16.1 %collective-permute-start.8 = (f32[32,8,128]{2,1,0:T(8,128)S(1)}, f32[32,8,128]{2,1,0:T(8,128)S(1)}, u32[]{:S(2)}, u32[]{:S(2)}) collective-permute-start(f32[32,8,128]{2,1,0:T(8,128)S(1)} %constant_dynamic-update-slice_fusion.refs_0_), channel_id=1, source_target_pairs={{0,8},{4,12},{8,0},{12,4},{1,9},{5,13},{9,1},{13,5},{2,10},{6,14},... | collective-permute-start | bytes 393224 | tf_op jit(solution)/shard_map/ppermute | solution.py:22
  37.4 6.9 %collective-permute-start.7 = (f32[32,8,128]{2,1,0:T(8,128)S(1)}, f32[32,8,128]{2,1,0:T(8,128)S(1)}, u32[]{:S(2)}, u32[]{:S(2)}) collective-permute-start(f32[32,8,128]{2,1,0:T(8,128)S(1)} %constant_dynamic-update-slice_fusion.refs_0_), channel_id=1, source_target_pairs={{0,4},{4,8},{8,12},{12,0},{1,5},{5,9},{9,13},{13,1},{2,6},{6,10},{... | collective-permute-start | bytes 393224 | tf_op jit(solution)/shard_map/ppermute | solution.py:22
  47.3 7.2 %collective-permute-start.12 = (f32[5,8,128]{2,1,0:T(8,128)S(1)}, f32[5,8,128]{2,1,0:T(8,128)S(1)}, u32[]{:S(2)}, u32[]{:S(2)}) collective-permute-start(f32[5,8,128]{2,1,0:T(8,128)S(1)} %get-tuple-element.72), channel_id=1, source_target_pairs={{0,3},{1,0},{2,1},{3,2},{4,7},{5,4},{6,5},{7,6},{8,11},{9,8},{10,9... | collective-permute-start | bytes 61448 | tf_op jit(solution)/shard_map/ppermute | solution.py:22
  47.8 6.7 %collective-permute-start.11 = (f32[5,8,128]{2,1,0:T(8,128)S(1)}, f32[5,8,128]{2,1,0:T(8,128)S(1)}, u32[]{:S(2)}, u32[]{:S(2)}) collective-permute-start(f32[5,8,128]{2,1,0:T(8,128)S(1)} %get-tuple-element.72), channel_id=1, source_target_pairs={{0,2},{1,3},{2,0},{3,1},{4,6},{5,7},{6,4},{7,5},{8,10},{9,11},{10,... | collective-permute-start | bytes 61448 | tf_op jit(solution)/shard_map/ppermute | solution.py:22
  48.9 5.6 %collective-permute-start.10 = (f32[5,8,128]{2,1,0:T(8,128)S(1)}, f32[5,8,128]{2,1,0:T(8,128)S(1)}, u32[]{:S(2)}, u32[]{:S(2)}) collective-permute-start(f32[5,8,128]{2,1,0:T(8,128)S(1)} %get-tuple-element.72), channel_id=1, source_target_pairs={{0,1},{1,2},{2,3},{3,0},{4,5},{5,6},{6,7},{7,4},{8,9},{9,10},{10,1... | collective-permute-start | bytes 61448 | tf_op jit(solution)/shard_map/ppermute | solution.py:22
  54.6 5.4 %collective-permute-start.14 = (f32[20,8,128]{2,1,0:T(8,128)S(1)}, f32[20,8,128]{2,1,0:T(8,128)S(1)}, u32[]{:S(2)}, u32[]{:S(2)}) collective-permute-start(f32[20,8,128]{2,1,0:T(8,128)S(1)} %constant_dynamic-update-slice_fusion.4.refs_0_), channel_id=1, source_target_pairs={{0,8},{4,12},{8,0},{12,4},{1,9},{5,13},{9,1},{13,5},{2,10},{6,14},... | collective-permute-start | bytes 245768 | tf_op jit(solution)/shard_map/ppermute | solution.py:22
  55.0 5.3 %collective-permute-start.13 = (f32[20,8,128]{2,1,0:T(8,128)S(1)}, f32[20,8,128]{2,1,0:T(8,128)S(1)}, u32[]{:S(2)}, u32[]{:S(2)}) collective-permute-start(f32[20,8,128]{2,1,0:T(8,128)S(1)} %constant_dynamic-update-slice_fusion.4.refs_0_), channel_id=1, source_target_pairs={{0,4},{4,8},{8,12},{12,0},{1,5},{5,9},{9,13},{13,1},{2,6},{6,10},{... | collective-permute-start | bytes 245768 | tf_op jit(solution)/shard_map/ppermute | solution.py:22
  64.3 4.8 %collective-permute-start.17 = (f32[8,8,128]{2,1,0:T(8,128)S(1)}, f32[8,8,128]{2,1,0:T(8,128)S(1)}, u32[]{:S(2)}, u32[]{:S(2)}) collective-permute-start(f32[8,8,128]{2,1,0:T(8,128)S(1)} %get-tuple-element.79), channel_id=1, source_target_pairs={{0,2},{1,3},{2,0},{3,1},{4,6},{5,7},{6,4},{7,5},{8,10},{9,11},{10,... | collective-permute-start | bytes 98312 | tf_op jit(solution)/shard_map/ppermute | solution.py:22
  64.3 5.7 %collective-permute-start.16 = (f32[8,8,128]{2,1,0:T(8,128)S(1)}, f32[8,8,128]{2,1,0:T(8,128)S(1)}, u32[]{:S(2)}, u32[]{:S(2)}) collective-permute-start(f32[8,8,128]{2,1,0:T(8,128)S(1)} %get-tuple-element.79), channel_id=1, source_target_pairs={{0,1},{1,2},{2,3},{3,0},{4,5},{5,6},{6,7},{7,4},{8,9},{9,10},{10,1... | collective-permute-start | bytes 98312 | tf_op jit(solution)/shard_map/ppermute | solution.py:22
  70.1 10.2 %collective-permute-start.23 = (f32[32,8,128]{2,1,0:T(8,128)S(1)}, f32[32,8,128]{2,1,0:T(8,128)S(1)}, u32[]{:S(2)}, u32[]{:S(2)}) collective-permute-start(f32[32,8,128]{2,1,0:T(8,128)S(1)} %pad_maximum_fusion.refs_0_), channel_id=1, source_target_pairs={{0,12},{4,0},{8,4},{12,8},{1,13},{5,1},{9,5},{13,9},{2,14},{6,2},{... | collective-permute-start | bytes 393224 | tf_op jit(solution)/shard_map/ppermute | solution.py:22
  71.0 9.2 %collective-permute-start.22 = (f32[32,8,128]{2,1,0:T(8,128)S(1)}, f32[32,8,128]{2,1,0:T(8,128)S(1)}, u32[]{:S(2)}, u32[]{:S(2)}) collective-permute-start(f32[32,8,128]{2,1,0:T(8,128)S(1)} %pad_maximum_fusion.refs_0_), channel_id=1, source_target_pairs={{0,8},{4,12},{8,0},{12,4},{1,9},{5,13},{9,1},{13,5},{2,10},{6,14},... | collective-permute-start | bytes 393224 | tf_op jit(solution)/shard_map/ppermute | solution.py:22
  72.1 8.2 %collective-permute-start.21 = (f32[32,8,128]{2,1,0:T(8,128)S(1)}, f32[32,8,128]{2,1,0:T(8,128)S(1)}, u32[]{:S(2)}, u32[]{:S(2)}) collective-permute-start(f32[32,8,128]{2,1,0:T(8,128)S(1)} %pad_maximum_fusion.refs_0_), channel_id=1, source_target_pairs={{0,4},{4,8},{8,12},{12,0},{1,5},{5,9},{9,13},{13,1},{2,6},{6,10},{... | collective-permute-start | bytes 393224 | tf_op jit(solution)/shard_map/ppermute | solution.py:22
  72.1 6.4 %collective-permute-start.24 = (f32[48,256]{1,0:T(8,128)S(1)}, f32[48,256]{1,0:T(8,128)S(1)}, u32[]{:S(2)}, u32[]{:S(2)}) collective-permute-start(f32[48,256]{1,0:T(8,128)S(1)} %get-tuple-element.86), channel_id=1, source_target_pairs={{0,1},{1,2},{2,3},{3,0},{4,5},{5,6},{6,7},{7,4},{8,9},{9,10},{10,1... | collective-permute-start | bytes 147464 | tf_op jit(solution)/shard_map/ppermute | solution.py:22
  74.5 5.0 %collective-permute-start.25 = (f32[48,256]{1,0:T(8,128)S(1)}, f32[48,256]{1,0:T(8,128)S(1)}, u32[]{:S(2)}, u32[]{:S(2)}) collective-permute-start(f32[48,256]{1,0:T(8,128)S(1)} %get-tuple-element.87), channel_id=1, source_target_pairs={{0,3},{1,0},{2,1},{3,2},{4,7},{5,4},{6,5},{7,6},{8,11},{9,8},{10,9... | collective-permute-start | bytes 147464 | tf_op jit(solution)/shard_map/ppermute | solution.py:22
  82.9 8.3 %collective-permute-start.28 = (f32[5,8,128]{2,1,0:T(8,128)S(1)}, f32[5,8,128]{2,1,0:T(8,128)S(1)}, u32[]{:S(2)}, u32[]{:S(2)}) collective-permute-start(f32[5,8,128]{2,1,0:T(8,128)S(1)} %get-tuple-element.92), channel_id=1, source_target_pairs={{0,3},{1,0},{2,1},{3,2},{4,7},{5,4},{6,5},{7,6},{8,11},{9,8},{10,9... | collective-permute-start | bytes 61448 | tf_op jit(solution)/shard_map/ppermute | solution.py:22
  85.6 5.6 %collective-permute-start.27 = (f32[5,8,128]{2,1,0:T(8,128)S(1)}, f32[5,8,128]{2,1,0:T(8,128)S(1)}, u32[]{:S(2)}, u32[]{:S(2)}) collective-permute-start(f32[5,8,128]{2,1,0:T(8,128)S(1)} %get-tuple-element.92), channel_id=1, source_target_pairs={{0,2},{1,3},{2,0},{3,1},{4,6},{5,7},{6,4},{7,5},{8,10},{9,11},{10,... | collective-permute-start | bytes 61448 | tf_op jit(solution)/shard_map/ppermute | solution.py:22
  85.6 5.6 %collective-permute-start.26 = (f32[5,8,128]{2,1,0:T(8,128)S(1)}, f32[5,8,128]{2,1,0:T(8,128)S(1)}, u32[]{:S(2)}, u32[]{:S(2)}) collective-permute-start(f32[5,8,128]{2,1,0:T(8,128)S(1)} %get-tuple-element.92), channel_id=1, source_target_pairs={{0,1},{1,2},{2,3},{3,0},{4,5},{5,6},{6,7},{7,4},{8,9},{9,10},{10,1... | collective-permute-start | bytes 61448 | tf_op jit(solution)/shard_map/ppermute | solution.py:22
  91.2 5.6 %collective-permute-start.30 = (f32[20,8,128]{2,1,0:T(8,128)S(1)}, f32[20,8,128]{2,1,0:T(8,128)S(1)}, u32[]{:S(2)}, u32[]{:S(2)}) collective-permute-start(f32[20,8,128]{2,1,0:T(8,128)S(1)} %constant_dynamic-update-slice_fusion.8.refs_0_), channel_id=1, source_target_pairs={{0,8},{4,12},{8,0},{12,4},{1,9},{5,13},{9,1},{13,5},{2,10},{6,14},... | collective-permute-start | bytes 245768 | tf_op jit(solution)/shard_map/ppermute | solution.py:22
  92.4 5.0 %collective-permute-start.29 = (f32[20,8,128]{2,1,0:T(8,128)S(1)}, f32[20,8,128]{2,1,0:T(8,128)S(1)}, u32[]{:S(2)}, u32[]{:S(2)}) collective-permute-start(f32[20,8,128]{2,1,0:T(8,128)S(1)} %constant_dynamic-update-slice_fusion.8.refs_0_), channel_id=1, source_target_pairs={{0,4},{4,8},{8,12},{12,0},{1,5},{5,9},{9,13},{13,1},{2,6},{6,10},{... | collective-permute-start | bytes 245768 | tf_op jit(solution)/shard_map/ppermute | solution.py:22
  (14 other events, 53.7 us)

commit v5 on v4

--- a/solution.py
+++ b/solution.py
@@ -13,7 +13,6 @@
 DEEP = 5
 WIDE = 2
 VMEM_LIMIT = 24 * 1024 * 1024
-PREPARE_LIMIT = 65_600_000
 EXACT = lax.Precision.HIGHEST
 
 
@@ -344,17 +343,12 @@
     )(*inputs)
 
 
-def prepare(sizes, fields, cells, precision):
-    own_x, own_y, lanes = fields[0].shape
-    number = len(fields)
+def scattered(sizes, shape, cells, precision):
+    own_x, own_y, lanes = shape
     all_rows = own_y * sizes[1]
-    depths = FIELD_DEPTHS
-
-    def kernel(*refs):
+
+    def kernel(cells, precision, out_ref):
         place = here()
-        fields = refs[:number]
-        cells, precision = refs[number : 2 + number]
-        coarse_ref, weight_ref, even_ref, odd_ref = refs[2 + number :]
         cell = cells[...]
         column = lax.div(cell, lanes)
         at_z = cell - column * lanes
@@ -369,30 +363,49 @@
             precision=EXACT, preferred_element_type=jnp.float32,
         )
         for x in range(own_x):
-            weight_ref[x] = weight[x * own_y : (x + 1) * own_y]
-        even = lax.rem(place[0], 2) == 0
+            out_ref[x] = weight[x * own_y : (x + 1) * own_y]
+
+    cost = pl.CostEstimate(flops=10**9, bytes_accessed=4096, transcendentals=0)
+    return call(kernel, [shape], [], [cells, precision], cost=cost)[0]
+
+
+def prepare(fields):
+    own_x, own_y, lanes = fields[0].shape
+    number = len(fields)
+    starts, rows = setup_rows(own_x, True)
+
+    def kernel(*refs):
+        place = here()
+        fields = refs[:number]
+        coarse_ref, even_edge, odd_edge, even_rows, odd_rows = refs[number:]
+        even_x = lax.rem(place[0], 2) == 0
+        even_y = lax.rem(place[1], 2) == 0
         at = 0
-        for index, depth in enumerate(depths):
-            ref = weight_ref if index == number else fields[index]
+        for index, depth in enumerate(FIELD_DEPTHS):
+            ref = fields[index]
             start = own_x - depth
-            even_start = jnp.where(even, start, 0)
-            odd_start = jnp.where(even, 0, start)
+            even_start = jnp.where(even_x, start, 0)
+            odd_start = jnp.where(even_x, 0, start)
             for x in range(depth):
-                even_ref[at + x] = ref[even_start + x]
-                odd_ref[at + x] = ref[odd_start + x]
+                even_edge[at + x] = ref[even_start + x]
+                odd_edge[at + x] = ref[odd_start + x]
             at += depth
+            for x in range(own_x):
+                first, last = ref[x, :depth, :], ref[x, own_y - depth :, :]
+                row = starts[index, x + depth]
+                even_rows[row : row + depth, :] = jnp.where(even_y, last, first)
+                odd_rows[row : row + depth, :] = jnp.where(even_y, first, last)
         planes = [jnp.exp(fields[2][x]) for x in range(own_x)]
         coarse = restrict_rows(planes, 0, own_y)
         for x in range(coarse.shape[0]):
             coarse_ref[x] = coarse[x] * 0.125
 
-    edge = (sum(depths), own_y, lanes)
+    edge = (sum(FIELD_DEPTHS), own_y, lanes)
     return call(
         kernel,
-        [(own_x // 2, own_y // 2, lanes // 2), fields[0].shape, edge, edge],
+        [(own_x // 2, own_y // 2, lanes // 2), edge, edge, (rows, lanes), (rows, lanes)],
         [],
-        list(fields) + [cells, precision],
-        limit=PREPARE_LIMIT,
+        list(fields),
     )
 
 
@@ -416,13 +429,14 @@
     return depth - max(0, depth - x, x - depth - own_x + 1)
 
 
-def setup_rows(own_x):
-    starts, at = [], 0
-    for depth in FIELD_DEPTHS:
-        starts.append([])
+def setup_rows(own_x, own):
+    starts, at = {}, 0
+    for index, depth in enumerate(FIELD_DEPTHS):
         for x in range(own_x + 2 * depth):
-            starts[-1].append(at)
-            at += reach(depth, own_x, x)
+            near = reach(depth, own_x, x)
+            if near and own == (near == depth):
+                starts[index, x] = at
+                at += near
     return starts, -(-at // 8) * 8
 
 
@@ -438,56 +452,47 @@
     return jnp.where(even, even_edge[at], odd_edge[at])
 
 
-def pack_setup_edges(fields, even_edge, odd_edge):
+def pack_corners(fields, even_edge, odd_edge):
     own_x, own_y, lanes = fields[0].shape
-    starts, rows = setup_rows(own_x)
+    starts, rows = setup_rows(own_x, False)
+
+    def kernel(even_edge, odd_edge, even_ref, odd_ref):
+        place = here()
+        even_x = lax.rem(place[0], 2) == 0
+        even_y = lax.rem(place[1], 2) == 0
+        for (index, x), at in starts.items():
+            near = reach(FIELD_DEPTHS[index], own_x, x)
+            plane = field_plane(fields, even_edge, odd_edge, even_x, index, x)
+            first, last = plane[:near], plane[own_y - near :]
+            even_ref[at : at + near, :] = jnp.where(even_y, last, first)
+            odd_ref[at : at + near, :] = jnp.where(even_y, first, last)
+
+    return call(kernel, [(rows, lanes)] * 2, [], [even_edge, odd_edge])
+
+
+def setup(sizes, fields, x_edges, y_edges, corners, own_cond):
+    own_x, own_y, lanes = fields[0].shape
+    frame = (own_x + 2 * HALO, own_y + 2 * HALO, lanes)
+    own_starts, _ = setup_rows(own_x, True)
+    corner_starts, _ = setup_rows(own_x, False)
     number = len(fields)
+    coarse = (own_x // 2, own_y // 2, lanes // 2)
 
     def kernel(*refs):
         place = here()
         fields = refs[:number]
-        even_edge, odd_edge, even_ref, odd_ref = refs[number:]
+        even_edge, odd_edge, *y_rows = refs[number : 6 + number]
+        own_cond = refs[6 + number]
         even_x = lax.rem(place[0], 2) == 0
         even_y = lax.rem(place[1], 2) == 0
-        for index, depth in enumerate(FIELD_DEPTHS):
-            for x in range(own_x + 2 * depth):
-                near = reach(depth, own_x, x)
-                if near == 0:
-                    continue
-                plane = field_plane(fields, even_edge, odd_edge, even_x, index, x)
-                at = starts[index][x]
-                first, last = plane[:near], plane[own_y - near :]
-                even_ref[at : at + near, :] = jnp.where(even_y, last, first)
-                odd_ref[at : at + near, :] = jnp.where(even_y, first, last)
-
-    inputs = list(fields) + [even_edge, odd_edge]
-    return call(kernel, [(rows, lanes)] * 2, [], inputs)
-
-
-def setup(sizes, fields, x_edges, y_edges, own_cond):
-    own_x, own_y, lanes = fields[0].shape
-    frame = (own_x + 2 * HALO, own_y + 2 * HALO, lanes)
-    starts, _ = setup_rows(own_x)
-    number = len(fields)
-    coarse = (own_x // 2, own_y // 2, lanes // 2)
-
-    def kernel(*refs):
-        place = here()
-        fields = refs[:number]
-        even_edge, odd_edge, even_rows, odd_rows, own_cond = refs[number : 5 + number]
-        even_x = lax.rem(place[0], 2) == 0
-        even_y = lax.rem(place[1], 2) == 0
-        outs = refs[5 + number : 18 + number]
+        outs = refs[7 + number : 20 + number]
         cond, hux, huy, huz, nbu, fx, fy, fz, rd, weight, source, z_out, b1 = outs
-        prior = refs[18 + number]
-        state = refs[19 + number]
-        grad = refs[20 + number]
+        prior, state, grad = refs[20 + number :]
 
         def assemble(index, ref, x_skip, first_row):
             depth = FIELD_DEPTHS[index]
             for x in range(own_x + 2 * depth):
                 near = reach(depth, own_x, x)
-                at = starts[index][x]
                 own_row = first_row + depth
                 if near < depth or x_skip:
                     ref[x + x_skip] = jnp.zeros(ref.shape[1:], jnp.float32)
@@ -496,6 +501,10 @@
                 )
                 if near == 0:
                     continue
+                if near == depth:
+                    at, (even_rows, odd_rows) = own_starts[index, x], y_rows[:2]
+                else:
+                    at, (even_rows, odd_rows) = corner_starts[index, x], y_rows[2:]
                 even_part, odd_part = even_rows[at : at + near, :], odd_rows[at : at + near, :]
                 ref[x + x_skip, own_row - near : own_row, :] = jnp.where(
                     even_y, odd_part, even_part
@@ -559,7 +568,7 @@
         kernel,
         [frame] * 12 + [(2 * coarse[0],) + coarse[1:]],
         [deep, frame, frame],
-        list(fields) + list(x_edges) + list(y_edges) + [own_cond],
+        list(fields) + list(x_edges) + list(y_edges) + list(corners) + [own_cond],
     )
 
 
@@ -1015,15 +1024,16 @@
     coarse = (cells_x // 2, cells_y // 2, cells_z // 2)
     per = coarse[0] + 1
 
-    fields = (prior_sample, gradient, log_conductivity, state)
-    own_cond, weight, *x_edges = prepare(
-        sizes, fields, sensor_cells[None], noise_precision[None]
-    )
-    fields = fields + (weight,)
-    x_edges = exchange(*x_edges, "gx")
-    y_edges = exchange(*pack_setup_edges(fields, *x_edges), "gy")
+    weight = scattered(
+        sizes, log_conductivity.shape, sensor_cells[None], noise_precision[None]
+    )
+    fields = (prior_sample, gradient, log_conductivity, state, weight)
+    own_cond, even_edge, odd_edge, even_rows, odd_rows = prepare(fields)
+    x_edges = exchange(even_edge, odd_edge, "gx")
+    y_edges = exchange(even_rows, odd_rows, "gy")
+    corners = exchange(*pack_corners(fields, *x_edges), "gy")
     (cond, hux, huy, huz, nbu, fx, fy, fz, rd, weight, source, z, b1) = setup(
-        sizes, fields, x_edges, y_edges, own_cond
+        sizes, fields, x_edges, y_edges, corners, own_cond
     )
     faces = (hux, huy, huz, nbu)
     fine = (fx, fy, fz, rd)

time: 100 us -> 96.4 us (0.964)
  starting transfers between devices: 40.7 us -> 38.2 us
  Pallas kernels: 17.2 us -> 15.5 us
    ppermute x28, starting transfers between devices: 35.1 us -> 28.6 us  [rotate(): return lax.ppermute(x, axis, [(i, (i + shift) % size) for i in range(size)])]
    ppermute x2 -> x3, starting transfers between devices: 3.31 us -> 7.66 us  [exchange(): lax.ppermute(even_pairs, axis, outer)]
    pallas_call x12 -> x13, Pallas kernels: 17.2 us -> 15.5 us  [call(): pl.pallas_call(kernel, out_shape=[jax.ShapeDtypeStruct(shape, jnp.float32...]
    ppermute x2 -> x3, waiting for transfers between devices: 3.24 us -> 1.57 us  [exchange(): lax.ppermute(even_pairs, axis, outer)]
    ppermute x28, waiting for transfers between devices: 36.9 us -> 38.1 us  [rotate(): return lax.ppermute(x, axis, [(i, (i + shift) % size) for i in range(size)])]
    ppermute x2 -> x3, starting transfers between devices: 2.28 us -> 1.98 us  [exchange(): lax.ppermute(odd_pairs, axis, inner)]
  transfers between devices with their start and end apart: 32 -> 34, of which waited for: 16 -> 16; matrix products, arithmetic and copies ran while one was open for 0% -> 0% of each run, Pallas kernels for 1% -> 1%
where the time goes in v5:
time: 96.4 us; the launch traced here: 96.1 us
  waiting for transfers between devices  39.7 us (41%)
  starting transfers between devices  38.2 us (40%)
  Pallas kernels  15.5 us (16%)
  local copies, waits for them, and re-layouts  1.75 us (2%)
    ppermute x28, waiting for transfers between devices, rotate(): return lax.ppermute(x, axis, [(i, (i + shift) % size) for i in range(size)])  38.1 us
    ppermute x28, starting transfers between devices, rotate(): return lax.ppermute(x, axis, [(i, (i + shift) % size) for i in range(size)])  28.6 us
    pallas_call x13, Pallas kernels, call(): pl.pallas_call(kernel, out_shape=[jax.ShapeDtypeStruct(shape, jnp.float32...  15.5 us
    ppermute x3, starting transfers between devices, exchange(): lax.ppermute(even_pairs, axis, outer)  7.66 us
    ppermute x3, starting transfers between devices, exchange(): lax.ppermute(odd_pairs, axis, inner)  1.98 us
  transfers between devices with their start and end apart: 34, of which 16 were waited for; matrix products, arithmetic and copies ran while one was open for 0% of the time, Pallas kernels for 1%

profile of v5, /device:TPU:0, one launch (start us, length us, event | category | flops | bytes accessed | tf_op | source)
XLA Modules:
  0.0 96.1 jit_solution(16206144871898787603)
XLA Ops:
  4.8 2.6 %collective-permute-start.2 = (f32[152,256]{1,0:T(8,128)S(1)}, f32[152,256]{1,0:T(8,128)S(1)}, u32[]{:S(2)}, u32[]{:S(2)}) collective-permute-start(f32[152,256]{1,0:T(8,128)S(1)} %get-tuple-element.53), channel_id=1, source_target_pairs={{0,1},{1,0},{2,3},{3,2},{4,5},{5,4},{6,7},{7,6},{8,9},{9,8},{10,11... | collective-permute-start | bytes 466952 | tf_op jit(solution)/shard_map/ppermute | solution.py:30
  8.2 4.5 %collective-permute-start.4 = (f32[64,256]{1,0:T(8,128)S(1)}, f32[64,256]{1,0:T(8,128)S(1)}, u32[]{:S(2)}, u32[]{:S(2)}) collective-permute-start(f32[64,256]{1,0:T(8,128)S(1)} %get-tuple-element.55), channel_id=1, source_target_pairs={{0,1},{1,0},{2,3},{3,2},{4,5},{5,4},{6,7},{7,6},{8,9},{9,8},{10,11... | collective-permute-start | bytes 196616 | tf_op jit(solution)/shard_map/ppermute | solution.py:30
  13.4 1.6 %collective-permute-done.4.refs_9_ = f32[64,256]{1,0:T(8,128)S(1)} collective-permute-done((f32[64,256]{1,0:T(8,128)S(1)}, f32[64,256]{1,0:T(8,128)S(1)}, u32[]{:S(2)}, u32[]{:S(2)}) %collective-permute-start.4) | collective-permute-done | bytes 65568 | tf_op jit(solution)/shard_map/ppermute | solution.py:30
  14.9 2.3 %shard_map.80 = (f32[16,24,256]{2,1,0:T(8,128)S(1)}, f32[16,24,256]{2,1,0:T(8,128)S(1)}, f32[16,24,256]{2,1,0:T(8,128)S(1)}, f32[16,24,256]{2,1,0:T(8,128)S(1)},...) custom-call(f32[8,16,256]{2,1,0:T(8,128)S(1)} %copy-done, ...), custom_call_target="tpu_custom_call" | custom-call | tf_op jit(solution)/shard_map/pallas_call | solution.py:335
  17.3 1.7 %collective-permute-start.8 = (f32[8,8,128]{2,1,0:T(8,128)S(1)}, f32[8,8,128]{2,1,0:T(8,128)S(1)}, u32[]{:S(2)}, u32[]{:S(2)}) collective-permute-start(f32[8,8,128]{2,1,0:T(8,128)S(1)} %get-tuple-element.58), channel_id=1, source_target_pairs={{0,3},{1,0},{2,1},{3,2},{4,7},{5,4},{6,5},{7,6},{8,11},{9,8},{10,9... | collective-permute-start | bytes 98312 | tf_op jit(solution)/shard_map/ppermute | solution.py:21
  18.9 3.8 %collective-permute-start.7 = (f32[8,8,128]{2,1,0:T(8,128)S(1)}, f32[8,8,128]{2,1,0:T(8,128)S(1)}, u32[]{:S(2)}, u32[]{:S(2)}) collective-permute-start(f32[8,8,128]{2,1,0:T(8,128)S(1)} %get-tuple-element.58), channel_id=1, source_target_pairs={{0,2},{1,3},{2,0},{3,1},{4,6},{5,7},{6,4},{7,5},{8,10},{9,11},{10,... | collective-permute-start | bytes 98312 | tf_op jit(solution)/shard_map/ppermute | solution.py:21
  23.4 5.0 %collective-permute-done.6 = f32[8,8,128]{2,1,0:T(8,128)S(1)} collective-permute-done((f32[8,8,128]{2,1,0:T(8,128)S(1)}, f32[8,8,128]{2,1,0:T(8,128)S(1)}, u32[]{:S(2)}, u32[]{:S(2)}) %collective-permute-start.6) | collective-permute-done | bytes 32800 | tf_op jit(solution)/shard_map/ppermute | solution.py:21
  28.5 5.1 %collective-permute-start.10 = (f32[32,8,128]{2,1,0:T(8,128)S(1)}, f32[32,8,128]{2,1,0:T(8,128)S(1)}, u32[]{:S(2)}, u32[]{:S(2)}) collective-permute-start(f32[32,8,128]{2,1,0:T(8,128)S(1)} %constant_dynamic-update-slice_fusion.refs_0_), channel_id=1, source_target_pairs={{0,8},{4,12},{8,0},{12,4},{1,9},{5,13},{9,1},{13,5},{2,10},{6,14},... | collective-permute-start | bytes 393224 | tf_op jit(solution)/shard_map/ppermute | solution.py:21
  34.0 6.5 %collective-permute-done.10.refs_2_ = f32[32,8,128]{2,1,0:T(8,128)S(1)} collective-permute-done((f32[32,8,128]{2,1,0:T(8,128)S(1)}, f32[32,8,128]{2,1,0:T(8,128)S(1)}, u32[]{:S(2)}, u32[]{:S(2)}) %collective-permute-start.10) | collective-permute-done | bytes 131104 | tf_op jit(solution)/shard_map/ppermute | solution.py:21
  41.1 2.4 %shard_map.83 = (f32[5,8,128]{2,1,0:T(8,128)S(1)}, f32[16,24,256]{2,1,0:T(8,128)S(1)}, f32[16,24,256]{2,1,0:T(8,128)S(1)}) custom-call(f32[32,8,128]{2,1,0:T(8,128)S(1)} %constant_dynamic-update-slice_fusion.refs_0_, f32[32,8,128]{2,1,0:T(8,128)S(1)} %collective-permute-done.9.refs_1_, f32[32,8,128]{2,1,0:T(8,128)S(1)} %collective-permute-done.10.refs_2_, ...), custom_call_target="tpu_custom_call" | custom-call | tf_op jit(solution)/shard_map/pallas_call | solution.py:335
  45.6 5.2 %collective-permute-done.12 = f32[5,8,128]{2,1,0:T(8,128)S(1)} collective-permute-done((f32[5,8,128]{2,1,0:T(8,128)S(1)}, f32[5,8,128]{2,1,0:T(8,128)S(1)}, u32[]{:S(2)}, u32[]{:S(2)}) %collective-permute-start.12) | collective-permute-done | bytes 20512 | tf_op jit(solution)/shard_map/ppermute | solution.py:21
  51.4 2.2 %collective-permute-done.17.refs_3_ = f32[20,8,128]{2,1,0:T(8,128)S(1)} collective-permute-done((f32[20,8,128]{2,1,0:T(8,128)S(1)}, f32[20,8,128]{2,1,0:T(8,128)S(1)}, u32[]{:S(2)}, u32[]{:S(2)}) %collective-permute-start.17) | collective-permute-done | bytes 81952 | tf_op jit(solution)/shard_map/ppermute | solution.py:21
  53.6 2.6 %collective-permute-done.16.refs_2_ = f32[20,8,128]{2,1,0:T(8,128)S(1)} collective-permute-done((f32[20,8,128]{2,1,0:T(8,128)S(1)}, f32[20,8,128]{2,1,0:T(8,128)S(1)}, u32[]{:S(2)}, u32[]{:S(2)}) %collective-permute-start.16) | collective-permute-done | bytes 81952 | tf_op jit(solution)/shard_map/ppermute | solution.py:21
  56.6 2.9 %shard_map.84 = (f32[4,16,256]{2,1,0:T(8,128)S(1)}, f32[4,16,256]{2,1,0:T(8,128)S(1)}, f32[8,16,256]{2,1,0:T(8,128)S(1)}, f32[8,8,128]{2,1,0:T(8,128)S(1)}, f32[8,128]{1,0:T(8,128)S(1)}, /*index=5*/f32[8,128]{1,0:T(8,128)S(1)}) custom-call(f32[20,8,128]{2,1,0:T(8,128)S(1)} %constant_dynamic-update-slice_fusion.4.refs_0_, ...), custom_call_target="tpu_custom_call" | custom-call | tf_op jit(solution)/shard_map/pallas_call | solution.py:335
  61.5 1.7 %collective-permute-start.22 = (f32[4,16,256]{2,1,0:T(8,128)S(1)}, f32[4,16,256]{2,1,0:T(8,128)S(1)}, u32[]{:S(2)}, u32[]{:S(2)}) collective-permute-start(f32[4,16,256]{2,1,0:T(8,128)S(1)} %get-tuple-element.84), channel_id=1, source_target_pairs={{0,12},{4,0},{8,4},{12,8},{1,13},{5,1},{9,5},{13,9},{2,14},{6,2},{... | collective-permute-start | bytes 196616 | tf_op jit(solution)/shard_map/ppermute | solution.py:21
  63.4 1.9 %collective-permute-done.19 = f32[8,8,128]{2,1,0:T(8,128)S(1)} collective-permute-done((f32[8,8,128]{2,1,0:T(8,128)S(1)}, f32[8,8,128]{2,1,0:T(8,128)S(1)}, u32[]{:S(2)}, u32[]{:S(2)}) %collective-permute-start.19) | collective-permute-done | bytes 32800 | tf_op jit(solution)/shard_map/ppermute | solution.py:21
  68.3 2.4 %collective-permute-start.26 = (f32[48,256]{1,0:T(8,128)S(1)}, f32[48,256]{1,0:T(8,128)S(1)}, u32[]{:S(2)}, u32[]{:S(2)}) collective-permute-start(f32[48,256]{1,0:T(8,128)S(1)} %get-tuple-element.88), channel_id=1, source_target_pairs={{0,1},{1,2},{2,3},{3,0},{4,5},{5,6},{6,7},{7,4},{8,9},{9,10},{10,1... | collective-permute-start | bytes 147464 | tf_op jit(solution)/shard_map/ppermute | solution.py:21
  70.7 1.4 %collective-permute-start.27 = (f32[48,256]{1,0:T(8,128)S(1)}, f32[48,256]{1,0:T(8,128)S(1)}, u32[]{:S(2)}, u32[]{:S(2)}) collective-permute-start(f32[48,256]{1,0:T(8,128)S(1)} %get-tuple-element.89), channel_id=1, source_target_pairs={{0,3},{1,0},{2,1},{3,2},{4,7},{5,4},{6,5},{7,6},{8,11},{9,8},{10,9... | collective-permute-start | bytes 147464 | tf_op jit(solution)/shard_map/ppermute | solution.py:21
  72.1 2.5 %collective-permute-done.26.before = f32[48,256]{1,0:T(8,128)S(1)} collective-permute-done((f32[48,256]{1,0:T(8,128)S(1)}, f32[48,256]{1,0:T(8,128)S(1)}, u32[]{:S(2)}, u32[]{:S(2)}) %collective-permute-start.26) | collective-permute-done | bytes 49184 | tf_op jit(solution)/shard_map/ppermute | solution.py:21
  76.5 2.6 %shard_map.88 = (f32[5,8,128]{2,1,0:T(8,128)S(1)}, f32[16,24,256]{2,1,0:T(8,128)S(1)}, f32[8,24,256]{2,1,0:T(8,128)S(1)}, f32[8,24,256]{2,1,0:T(8,128)S(1)}, f32[8,128]{1,0:T(8,128)S(1)}) custom-call(f32[32,8,128]{2,1,0:T(8,128)S(1)} %pad_maximum_fusion.refs_0_, f32[32,8,128]{2,1,0:T(8,128)S(1)} %collective-permute-done.23.refs_1_, ...), custom_call_target="tpu_custom_call" | custom-call | tf_op jit(solution)/shard_map/pallas_call | solution.py:335
  79.1 2.7 %collective-permute-start.30 = (f32[5,8,128]{2,1,0:T(8,128)S(1)}, f32[5,8,128]{2,1,0:T(8,128)S(1)}, u32[]{:S(2)}, u32[]{:S(2)}) collective-permute-start(f32[5,8,128]{2,1,0:T(8,128)S(1)} %get-tuple-element.94), channel_id=1, source_target_pairs={{0,3},{1,0},{2,1},{3,2},{4,7},{5,4},{6,5},{7,6},{8,11},{9,8},{10,9... | collective-permute-start | bytes 61448 | tf_op jit(solution)/shard_map/ppermute | solution.py:21
  82.6 4.8 %collective-permute-done.28 = f32[5,8,128]{2,1,0:T(8,128)S(1)} collective-permute-done((f32[5,8,128]{2,1,0:T(8,128)S(1)}, f32[5,8,128]{2,1,0:T(8,128)S(1)}, u32[]{:S(2)}, u32[]{:S(2)}) %collective-permute-start.28) | collective-permute-done | bytes 20512 | tf_op jit(solution)/shard_map/ppermute | solution.py:21
  89.7 3.3 %collective-permute-done.32.refs_2_ = f32[20,8,128]{2,1,0:T(8,128)S(1)} collective-permute-done((f32[20,8,128]{2,1,0:T(8,128)S(1)}, f32[20,8,128]{2,1,0:T(8,128)S(1)}, u32[]{:S(2)}, u32[]{:S(2)}) %collective-permute-start.32) | collective-permute-done | bytes 81952 | tf_op jit(solution)/shard_map/ppermute | solution.py:21
  93.6 2.6 %shard_map.89 = (f32[8,16,256]{2,1,0:T(8,128)}, f32[8,16,256]{2,1,0:T(8,128)}) custom-call(f32[20,8,128]{2,1,0:T(8,128)S(1)} %constant_dynamic-update-slice_fusion.8.refs_0_, f32[20,8,128]{2,1,0:T(8,128)S(1)} %collective-permute-done.31.refs_1_, f32[20,8,128]{2,1,0:T(8,128)S(1)} %collective-permute-done.32.refs_2_, ...), custom_call_target="tpu_custom_call" | custom-call | tf_op jit(solution)/shard_map/pallas_call | solution.py:335
  (82 shorter events, 20.9 us)
Async XLA Ops:
  4.8 8.5 %collective-permute-start.2 = (f32[152,256]{1,0:T(8,128)S(1)}, f32[152,256]{1,0:T(8,128)S(1)}, u32[]{:S(2)}, u32[]{:S(2)}) collective-permute-start(f32[152,256]{1,0:T(8,128)S(1)} %get-tuple-element.53), channel_id=1, source_target_pairs={{0,1},{1,0},{2,3},{3,2},{4,5},{5,4},{6,7},{7,6},{8,9},{9,8},{10,11... | collective-permute-start | bytes 466952 | tf_op jit(solution)/shard_map/ppermute | solution.py:30
  7.4 5.9 %collective-permute-start.3 = (f32[152,256]{1,0:T(8,128)S(1)}, f32[152,256]{1,0:T(8,128)S(1)}, u32[]{:S(2)}, u32[]{:S(2)}) collective-permute-start(f32[152,256]{1,0:T(8,128)S(1)} %get-tuple-element.54), channel_id=1, source_target_pairs={{0,0},{3,3},{1,2},{2,1},{4,4},{7,7},{5,6},{6,5},{8,8},{11,11},{9,1... | collective-permute-start | bytes 466952 | tf_op jit(solution)/shard_map/ppermute | solution.py:30
  8.2 6.7 %collective-permute-start.4 = (f32[64,256]{1,0:T(8,128)S(1)}, f32[64,256]{1,0:T(8,128)S(1)}, u32[]{:S(2)}, u32[]{:S(2)}) collective-permute-start(f32[64,256]{1,0:T(8,128)S(1)} %get-tuple-element.55), channel_id=1, source_target_pairs={{0,1},{1,0},{2,3},{3,2},{4,5},{5,4},{6,7},{7,6},{8,9},{9,8},{10,11... | collective-permute-start | bytes 196616 | tf_op jit(solution)/shard_map/ppermute | solution.py:30
  17.3 11.2 %collective-permute-start.8 = (f32[8,8,128]{2,1,0:T(8,128)S(1)}, f32[8,8,128]{2,1,0:T(8,128)S(1)}, u32[]{:S(2)}, u32[]{:S(2)}) collective-permute-start(f32[8,8,128]{2,1,0:T(8,128)S(1)} %get-tuple-element.58), channel_id=1, source_target_pairs={{0,3},{1,0},{2,1},{3,2},{4,7},{5,4},{6,5},{7,6},{8,11},{9,8},{10,9... | collective-permute-start | bytes 98312 | tf_op jit(solution)/shard_map/ppermute | solution.py:21
  18.9 9.5 %collective-permute-start.7 = (f32[8,8,128]{2,1,0:T(8,128)S(1)}, f32[8,8,128]{2,1,0:T(8,128)S(1)}, u32[]{:S(2)}, u32[]{:S(2)}) collective-permute-start(f32[8,8,128]{2,1,0:T(8,128)S(1)} %get-tuple-element.58), channel_id=1, source_target_pairs={{0,2},{1,3},{2,0},{3,1},{4,6},{5,7},{6,4},{7,5},{8,10},{9,11},{10,... | collective-permute-start | bytes 98312 | tf_op jit(solution)/shard_map/ppermute | solution.py:21
  22.7 5.7 %collective-permute-start.6 = (f32[8,8,128]{2,1,0:T(8,128)S(1)}, f32[8,8,128]{2,1,0:T(8,128)S(1)}, u32[]{:S(2)}, u32[]{:S(2)}) collective-permute-start(f32[8,8,128]{2,1,0:T(8,128)S(1)} %get-tuple-element.58), channel_id=1, source_target_pairs={{0,1},{1,2},{2,3},{3,0},{4,5},{5,6},{6,7},{7,4},{8,9},{9,10},{10,1... | collective-permute-start | bytes 98312 | tf_op jit(solution)/shard_map/ppermute | solution.py:21
  28.5 5.5 %collective-permute-start.11 = (f32[32,8,128]{2,1,0:T(8,128)S(1)}, f32[32,8,128]{2,1,0:T(8,128)S(1)}, u32[]{:S(2)}, u32[]{:S(2)}) collective-permute-start(f32[32,8,128]{2,1,0:T(8,128)S(1)} %constant_dynamic-update-slice_fusion.refs_0_), channel_id=1, source_target_pairs={{0,12},{4,0},{8,4},{12,8},{1,13},{5,1},{9,5},{13,9},{2,14},{6,2},{... | collective-permute-start | bytes 393224 | tf_op jit(solution)/shard_map/ppermute | solution.py:21
  28.5 12.0 %collective-permute-start.10 = (f32[32,8,128]{2,1,0:T(8,128)S(1)}, f32[32,8,128]{2,1,0:T(8,128)S(1)}, u32[]{:S(2)}, u32[]{:S(2)}) collective-permute-start(f32[32,8,128]{2,1,0:T(8,128)S(1)} %constant_dynamic-update-slice_fusion.refs_0_), channel_id=1, source_target_pairs={{0,8},{4,12},{8,0},{12,4},{1,9},{5,13},{9,1},{13,5},{2,10},{6,14},... | collective-permute-start | bytes 393224 | tf_op jit(solution)/shard_map/ppermute | solution.py:21
  33.6 6.9 %collective-permute-start.9 = (f32[32,8,128]{2,1,0:T(8,128)S(1)}, f32[32,8,128]{2,1,0:T(8,128)S(1)}, u32[]{:S(2)}, u32[]{:S(2)}) collective-permute-start(f32[32,8,128]{2,1,0:T(8,128)S(1)} %constant_dynamic-update-slice_fusion.refs_0_), channel_id=1, source_target_pairs={{0,4},{4,8},{8,12},{12,0},{1,5},{5,9},{9,13},{13,1},{2,6},{6,10},{... | collective-permute-start | bytes 393224 | tf_op jit(solution)/shard_map/ppermute | solution.py:21
  43.5 7.3 %collective-permute-start.14 = (f32[5,8,128]{2,1,0:T(8,128)S(1)}, f32[5,8,128]{2,1,0:T(8,128)S(1)}, u32[]{:S(2)}, u32[]{:S(2)}) collective-permute-start(f32[5,8,128]{2,1,0:T(8,128)S(1)} %get-tuple-element.74), channel_id=1, source_target_pairs={{0,3},{1,0},{2,1},{3,2},{4,7},{5,4},{6,5},{7,6},{8,11},{9,8},{10,9... | collective-permute-start | bytes 61448 | tf_op jit(solution)/shard_map/ppermute | solution.py:21
  44.0 6.7 %collective-permute-start.13 = (f32[5,8,128]{2,1,0:T(8,128)S(1)}, f32[5,8,128]{2,1,0:T(8,128)S(1)}, u32[]{:S(2)}, u32[]{:S(2)}) collective-permute-start(f32[5,8,128]{2,1,0:T(8,128)S(1)} %get-tuple-element.74), channel_id=1, source_target_pairs={{0,2},{1,3},{2,0},{3,1},{4,6},{5,7},{6,4},{7,5},{8,10},{9,11},{10,... | collective-permute-start | bytes 61448 | tf_op jit(solution)/shard_map/ppermute | solution.py:21
  45.2 5.6 %collective-permute-start.12 = (f32[5,8,128]{2,1,0:T(8,128)S(1)}, f32[5,8,128]{2,1,0:T(8,128)S(1)}, u32[]{:S(2)}, u32[]{:S(2)}) collective-permute-start(f32[5,8,128]{2,1,0:T(8,128)S(1)} %get-tuple-element.74), channel_id=1, source_target_pairs={{0,1},{1,2},{2,3},{3,0},{4,5},{5,6},{6,7},{7,4},{8,9},{9,10},{10,1... | collective-permute-start | bytes 61448 | tf_op jit(solution)/shard_map/ppermute | solution.py:21
  50.8 5.4 %collective-permute-start.16 = (f32[20,8,128]{2,1,0:T(8,128)S(1)}, f32[20,8,128]{2,1,0:T(8,128)S(1)}, u32[]{:S(2)}, u32[]{:S(2)}) collective-permute-start(f32[20,8,128]{2,1,0:T(8,128)S(1)} %constant_dynamic-update-slice_fusion.4.refs_0_), channel_id=1, source_target_pairs={{0,8},{4,12},{8,0},{12,4},{1,9},{5,13},{9,1},{13,5},{2,10},{6,14},... | collective-permute-start | bytes 245768 | tf_op jit(solution)/shard_map/ppermute | solution.py:21
  51.2 5.3 %collective-permute-start.15 = (f32[20,8,128]{2,1,0:T(8,128)S(1)}, f32[20,8,128]{2,1,0:T(8,128)S(1)}, u32[]{:S(2)}, u32[]{:S(2)}) collective-permute-start(f32[20,8,128]{2,1,0:T(8,128)S(1)} %constant_dynamic-update-slice_fusion.4.refs_0_), channel_id=1, source_target_pairs={{0,4},{4,8},{8,12},{12,0},{1,5},{5,9},{9,13},{13,1},{2,6},{6,10},{... | collective-permute-start | bytes 245768 | tf_op jit(solution)/shard_map/ppermute | solution.py:21
  60.5 5.7 %collective-permute-start.18 = (f32[8,8,128]{2,1,0:T(8,128)S(1)}, f32[8,8,128]{2,1,0:T(8,128)S(1)}, u32[]{:S(2)}, u32[]{:S(2)}) collective-permute-start(f32[8,8,128]{2,1,0:T(8,128)S(1)} %get-tuple-element.81), channel_id=1, source_target_pairs={{0,1},{1,2},{2,3},{3,0},{4,5},{5,6},{6,7},{7,4},{8,9},{9,10},{10,1... | collective-permute-start | bytes 98312 | tf_op jit(solution)/shard_map/ppermute | solution.py:21
  66.3 10.2 %collective-permute-start.25 = (f32[32,8,128]{2,1,0:T(8,128)S(1)}, f32[32,8,128]{2,1,0:T(8,128)S(1)}, u32[]{:S(2)}, u32[]{:S(2)}) collective-permute-start(f32[32,8,128]{2,1,0:T(8,128)S(1)} %pad_maximum_fusion.refs_0_), channel_id=1, source_target_pairs={{0,12},{4,0},{8,4},{12,8},{1,13},{5,1},{9,5},{13,9},{2,14},{6,2},{... | collective-permute-start | bytes 393224 | tf_op jit(solution)/shard_map/ppermute | solution.py:21
  67.2 9.2 %collective-permute-start.24 = (f32[32,8,128]{2,1,0:T(8,128)S(1)}, f32[32,8,128]{2,1,0:T(8,128)S(1)}, u32[]{:S(2)}, u32[]{:S(2)}) collective-permute-start(f32[32,8,128]{2,1,0:T(8,128)S(1)} %pad_maximum_fusion.refs_0_), channel_id=1, source_target_pairs={{0,8},{4,12},{8,0},{12,4},{1,9},{5,13},{9,1},{13,5},{2,10},{6,14},... | collective-permute-start | bytes 393224 | tf_op jit(solution)/shard_map/ppermute | solution.py:21
  68.3 8.2 %collective-permute-start.23 = (f32[32,8,128]{2,1,0:T(8,128)S(1)}, f32[32,8,128]{2,1,0:T(8,128)S(1)}, u32[]{:S(2)}, u32[]{:S(2)}) collective-permute-start(f32[32,8,128]{2,1,0:T(8,128)S(1)} %pad_maximum_fusion.refs_0_), channel_id=1, source_target_pairs={{0,4},{4,8},{8,12},{12,0},{1,5},{5,9},{9,13},{13,1},{2,6},{6,10},{... | collective-permute-start | bytes 393224 | tf_op jit(solution)/shard_map/ppermute | solution.py:21
  68.3 6.4 %collective-permute-start.26 = (f32[48,256]{1,0:T(8,128)S(1)}, f32[48,256]{1,0:T(8,128)S(1)}, u32[]{:S(2)}, u32[]{:S(2)}) collective-permute-start(f32[48,256]{1,0:T(8,128)S(1)} %get-tuple-element.88), channel_id=1, source_target_pairs={{0,1},{1,2},{2,3},{3,0},{4,5},{5,6},{6,7},{7,4},{8,9},{9,10},{10,1... | collective-permute-start | bytes 147464 | tf_op jit(solution)/shard_map/ppermute | solution.py:21
  70.7 5.0 %collective-permute-start.27 = (f32[48,256]{1,0:T(8,128)S(1)}, f32[48,256]{1,0:T(8,128)S(1)}, u32[]{:S(2)}, u32[]{:S(2)}) collective-permute-start(f32[48,256]{1,0:T(8,128)S(1)} %get-tuple-element.89), channel_id=1, source_target_pairs={{0,3},{1,0},{2,1},{3,2},{4,7},{5,4},{6,5},{7,6},{8,11},{9,8},{10,9... | collective-permute-start | bytes 147464 | tf_op jit(solution)/shard_map/ppermute | solution.py:21
  79.1 8.3 %collective-permute-start.30 = (f32[5,8,128]{2,1,0:T(8,128)S(1)}, f32[5,8,128]{2,1,0:T(8,128)S(1)}, u32[]{:S(2)}, u32[]{:S(2)}) collective-permute-start(f32[5,8,128]{2,1,0:T(8,128)S(1)} %get-tuple-element.94), channel_id=1, source_target_pairs={{0,3},{1,0},{2,1},{3,2},{4,7},{5,4},{6,5},{7,6},{8,11},{9,8},{10,9... | collective-permute-start | bytes 61448 | tf_op jit(solution)/shard_map/ppermute | solution.py:21
  81.8 5.6 %collective-permute-start.29 = (f32[5,8,128]{2,1,0:T(8,128)S(1)}, f32[5,8,128]{2,1,0:T(8,128)S(1)}, u32[]{:S(2)}, u32[]{:S(2)}) collective-permute-start(f32[5,8,128]{2,1,0:T(8,128)S(1)} %get-tuple-element.94), channel_id=1, source_target_pairs={{0,2},{1,3},{2,0},{3,1},{4,6},{5,7},{6,4},{7,5},{8,10},{9,11},{10,... | collective-permute-start | bytes 61448 | tf_op jit(solution)/shard_map/ppermute | solution.py:21
  81.8 5.6 %collective-permute-start.28 = (f32[5,8,128]{2,1,0:T(8,128)S(1)}, f32[5,8,128]{2,1,0:T(8,128)S(1)}, u32[]{:S(2)}, u32[]{:S(2)}) collective-permute-start(f32[5,8,128]{2,1,0:T(8,128)S(1)} %get-tuple-element.94), channel_id=1, source_target_pairs={{0,1},{1,2},{2,3},{3,0},{4,5},{5,6},{6,7},{7,4},{8,9},{9,10},{10,1... | collective-permute-start | bytes 61448 | tf_op jit(solution)/shard_map/ppermute | solution.py:21
  87.5 5.6 %collective-permute-start.32 = (f32[20,8,128]{2,1,0:T(8,128)S(1)}, f32[20,8,128]{2,1,0:T(8,128)S(1)}, u32[]{:S(2)}, u32[]{:S(2)}) collective-permute-start(f32[20,8,128]{2,1,0:T(8,128)S(1)} %constant_dynamic-update-slice_fusion.8.refs_0_), channel_id=1, source_target_pairs={{0,8},{4,12},{8,0},{12,4},{1,9},{5,13},{9,1},{13,5},{2,10},{6,14},... | collective-permute-start | bytes 245768 | tf_op jit(solution)/shard_map/ppermute | solution.py:21
  (16 other events, 44.5 us)

commit v6 on v5

--- a/solution.py
+++ b/solution.py
@@ -4,6 +4,7 @@
 from jax.experimental import pallas as pl
 from jax.experimental.pallas import tpu as pltpu
 from jax.sharding import PartitionSpec as P
+
 
 DAMPING = 0.8
 KEPT = 0.2
@@ -220,7 +221,7 @@
         pairs[x, :rows, :] = swap_sum(pair + (off1(2 * x) + off1(2 * x + 1)), 1, 1)
     coarse = [row_pairs(pairs, x, rows) for x in range(half)]
     iterate = [rd2[x] * coarse[x] for x in range(half)]
-    for sweep in range(COARSE_SWEEPS - 1):
+    for _ in range(COARSE_SWEEPS - 1):
         new = []
         for x in range(half):
             low = iterate[x - 1] if x > 0 else None
@@ -288,7 +289,6 @@
 
 
 def prior_rows(center, low, high, up, down, x_low, x_high, y_mask, z_mask, outside):
-    rows, lanes = center.shape
     y_next = shifted(y_mask, -1, 0)
     z_next = shifted(z_mask, -1, 1)
     out = (PRIOR_MASS + outside) * center + x_low * (center - low) + x_high * (center - high)
@@ -410,8 +410,8 @@
 
 
 def gathered_row(own):
-    size = lax.axis_size("gy")
-    return jnp.concatenate([own] + [rotate(own, "gy", t) for t in range(1, size)], axis=0)
+    parts = [rotate(own, "gy", t) for t in range(1, lax.axis_size("gy"))]
+    return jnp.concatenate([own] + parts, axis=0)
 
 
 def gathered_rows(row):
@@ -1048,11 +1048,13 @@
         sizes, gathered(b1), per, levels, fine, second, curved, cond, faces, source
     )
     row = gathered_row(b1)
-    low, high = rotate(last, "gx", 1), rotate(first, "gx", -1)
+    low = rotate(last, "gx", 1)
+    high = rotate(first, "gx", -1)
     first, last = pack_edges(remaining, low, high)
     row, first, last = lax.optimization_barrier((row, first, last))
     blocks = gathered_rows(row)
-    before, after = rotate(last, "gy", 1), rotate(first, "gy", -1)
+    before = rotate(last, "gy", 1)
+    after = rotate(first, "gy", -1)
     direction, z = begin(remaining, low, high, before, after, cond, faces)
     b1, second, combined, curved, norm = middle(
         sizes, blocks, per + 3, levels, fine, z, direction, prior_part(sizes, direction), weight,
@@ -1069,6 +1071,7 @@
 def solution(mesh):
     field = P(("ens", "gx"), "gy", None)
     sensors = P(("ens", "gx", "gy"))
+
     return jax.shard_map(
         on_device,
         mesh=mesh,

time: 96.4 us -> 96.4 us (level)
  no operation moved by 1% of the time
where the time goes in v6:
time: 96.4 us; the launch traced here: 96.1 us
  waiting for transfers between devices  39.7 us (41%)
  starting transfers between devices  38.2 us (40%)
  Pallas kernels  15.5 us (16%)
  local copies, waits for them, and re-layouts  1.75 us (2%)
    ppermute x28, waiting for transfers between devices, rotate(): return lax.ppermute(x, axis, [(i, (i + shift) % size) for i in range(size)])  38.1 us
    ppermute x28, starting transfers between devices, rotate(): return lax.ppermute(x, axis, [(i, (i + shift) % size) for i in range(size)])  28.6 us
    pallas_call x13, Pallas kernels, call(): pl.pallas_call(kernel, out_shape=[jax.ShapeDtypeStruct(shape, jnp.float32...  15.5 us
    ppermute x3, starting transfers between devices, exchange(): lax.ppermute(even_pairs, axis, outer)  7.66 us
    ppermute x3, starting transfers between devices, exchange(): lax.ppermute(odd_pairs, axis, inner)  1.98 us
  transfers between devices with their start and end apart: 34, of which 16 were waited for; matrix products, arithmetic and copies ran while one was open for 0% of the time, Pallas kernels for 1%

profile of v6, /device:TPU:0, one launch (start us, length us, event | category | flops | bytes accessed | tf_op | source)
XLA Modules:
  0.0 96.1 jit_solution(16206144871898787603)
XLA Ops:
  4.8 2.6 %collective-permute-start.2 = (f32[152,256]{1,0:T(8,128)S(1)}, f32[152,256]{1,0:T(8,128)S(1)}, u32[]{:S(2)}, u32[]{:S(2)}) collective-permute-start(f32[152,256]{1,0:T(8,128)S(1)} %get-tuple-element.53), channel_id=1, source_target_pairs={{0,1},{1,0},{2,3},{3,2},{4,5},{5,4},{6,7},{7,6},{8,9},{9,8},{10,11... | collective-permute-start | bytes 466952 | tf_op jit(solution)/shard_map/ppermute | solution.py:31
  8.2 4.5 %collective-permute-start.4 = (f32[64,256]{1,0:T(8,128)S(1)}, f32[64,256]{1,0:T(8,128)S(1)}, u32[]{:S(2)}, u32[]{:S(2)}) collective-permute-start(f32[64,256]{1,0:T(8,128)S(1)} %get-tuple-element.55), channel_id=1, source_target_pairs={{0,1},{1,0},{2,3},{3,2},{4,5},{5,4},{6,7},{7,6},{8,9},{9,8},{10,11... | collective-permute-start | bytes 196616 | tf_op jit(solution)/shard_map/ppermute | solution.py:31
  13.4 1.6 %collective-permute-done.4.refs_9_ = f32[64,256]{1,0:T(8,128)S(1)} collective-permute-done((f32[64,256]{1,0:T(8,128)S(1)}, f32[64,256]{1,0:T(8,128)S(1)}, u32[]{:S(2)}, u32[]{:S(2)}) %collective-permute-start.4) | collective-permute-done | bytes 65568 | tf_op jit(solution)/shard_map/ppermute | solution.py:31
  14.9 2.3 %shard_map.80 = (f32[16,24,256]{2,1,0:T(8,128)S(1)}, f32[16,24,256]{2,1,0:T(8,128)S(1)}, f32[16,24,256]{2,1,0:T(8,128)S(1)}, f32[16,24,256]{2,1,0:T(8,128)S(1)},...) custom-call(f32[8,16,256]{2,1,0:T(8,128)S(1)} %copy-done, ...), custom_call_target="tpu_custom_call" | custom-call | tf_op jit(solution)/shard_map/pallas_call | solution.py:335
  17.3 1.7 %collective-permute-start.8 = (f32[8,8,128]{2,1,0:T(8,128)S(1)}, f32[8,8,128]{2,1,0:T(8,128)S(1)}, u32[]{:S(2)}, u32[]{:S(2)}) collective-permute-start(f32[8,8,128]{2,1,0:T(8,128)S(1)} %get-tuple-element.58), channel_id=1, source_target_pairs={{0,3},{1,0},{2,1},{3,2},{4,7},{5,4},{6,5},{7,6},{8,11},{9,8},{10,9... | collective-permute-start | bytes 98312 | tf_op jit(solution)/shard_map/ppermute | solution.py:22
  18.9 3.8 %collective-permute-start.7 = (f32[8,8,128]{2,1,0:T(8,128)S(1)}, f32[8,8,128]{2,1,0:T(8,128)S(1)}, u32[]{:S(2)}, u32[]{:S(2)}) collective-permute-start(f32[8,8,128]{2,1,0:T(8,128)S(1)} %get-tuple-element.58), channel_id=1, source_target_pairs={{0,2},{1,3},{2,0},{3,1},{4,6},{5,7},{6,4},{7,5},{8,10},{9,11},{10,... | collective-permute-start | bytes 98312 | tf_op jit(solution)/shard_map/ppermute | solution.py:22
  23.4 5.0 %collective-permute-done.6 = f32[8,8,128]{2,1,0:T(8,128)S(1)} collective-permute-done((f32[8,8,128]{2,1,0:T(8,128)S(1)}, f32[8,8,128]{2,1,0:T(8,128)S(1)}, u32[]{:S(2)}, u32[]{:S(2)}) %collective-permute-start.6) | collective-permute-done | bytes 32800 | tf_op jit(solution)/shard_map/ppermute | solution.py:22
  28.5 5.1 %collective-permute-start.10 = (f32[32,8,128]{2,1,0:T(8,128)S(1)}, f32[32,8,128]{2,1,0:T(8,128)S(1)}, u32[]{:S(2)}, u32[]{:S(2)}) collective-permute-start(f32[32,8,128]{2,1,0:T(8,128)S(1)} %constant_dynamic-update-slice_fusion.refs_0_), channel_id=1, source_target_pairs={{0,8},{4,12},{8,0},{12,4},{1,9},{5,13},{9,1},{13,5},{2,10},{6,14},... | collective-permute-start | bytes 393224 | tf_op jit(solution)/shard_map/ppermute | solution.py:22
  34.0 6.5 %collective-permute-done.10.refs_2_ = f32[32,8,128]{2,1,0:T(8,128)S(1)} collective-permute-done((f32[32,8,128]{2,1,0:T(8,128)S(1)}, f32[32,8,128]{2,1,0:T(8,128)S(1)}, u32[]{:S(2)}, u32[]{:S(2)}) %collective-permute-start.10) | collective-permute-done | bytes 131104 | tf_op jit(solution)/shard_map/ppermute | solution.py:22
  41.1 2.4 %shard_map.83 = (f32[5,8,128]{2,1,0:T(8,128)S(1)}, f32[16,24,256]{2,1,0:T(8,128)S(1)}, f32[16,24,256]{2,1,0:T(8,128)S(1)}) custom-call(f32[32,8,128]{2,1,0:T(8,128)S(1)} %constant_dynamic-update-slice_fusion.refs_0_, f32[32,8,128]{2,1,0:T(8,128)S(1)} %collective-permute-done.9.refs_1_, f32[32,8,128]{2,1,0:T(8,128)S(1)} %collective-permute-done.10.refs_2_, ...), custom_call_target="tpu_custom_call" | custom-call | tf_op jit(solution)/shard_map/pallas_call | solution.py:335
  45.6 5.2 %collective-permute-done.12 = f32[5,8,128]{2,1,0:T(8,128)S(1)} collective-permute-done((f32[5,8,128]{2,1,0:T(8,128)S(1)}, f32[5,8,128]{2,1,0:T(8,128)S(1)}, u32[]{:S(2)}, u32[]{:S(2)}) %collective-permute-start.12) | collective-permute-done | bytes 20512 | tf_op jit(solution)/shard_map/ppermute | solution.py:22
  51.4 2.2 %collective-permute-done.17.refs_3_ = f32[20,8,128]{2,1,0:T(8,128)S(1)} collective-permute-done((f32[20,8,128]{2,1,0:T(8,128)S(1)}, f32[20,8,128]{2,1,0:T(8,128)S(1)}, u32[]{:S(2)}, u32[]{:S(2)}) %collective-permute-start.17) | collective-permute-done | bytes 81952 | tf_op jit(solution)/shard_map/ppermute | solution.py:22
  53.6 2.6 %collective-permute-done.16.refs_2_ = f32[20,8,128]{2,1,0:T(8,128)S(1)} collective-permute-done((f32[20,8,128]{2,1,0:T(8,128)S(1)}, f32[20,8,128]{2,1,0:T(8,128)S(1)}, u32[]{:S(2)}, u32[]{:S(2)}) %collective-permute-start.16) | collective-permute-done | bytes 81952 | tf_op jit(solution)/shard_map/ppermute | solution.py:22
  56.6 2.9 %shard_map.84 = (f32[4,16,256]{2,1,0:T(8,128)S(1)}, f32[4,16,256]{2,1,0:T(8,128)S(1)}, f32[8,16,256]{2,1,0:T(8,128)S(1)}, f32[8,8,128]{2,1,0:T(8,128)S(1)}, f32[8,128]{1,0:T(8,128)S(1)}, /*index=5*/f32[8,128]{1,0:T(8,128)S(1)}) custom-call(f32[20,8,128]{2,1,0:T(8,128)S(1)} %constant_dynamic-update-slice_fusion.4.refs_0_, ...), custom_call_target="tpu_custom_call" | custom-call | tf_op jit(solution)/shard_map/pallas_call | solution.py:335
  61.5 1.7 %collective-permute-start.22 = (f32[4,16,256]{2,1,0:T(8,128)S(1)}, f32[4,16,256]{2,1,0:T(8,128)S(1)}, u32[]{:S(2)}, u32[]{:S(2)}) collective-permute-start(f32[4,16,256]{2,1,0:T(8,128)S(1)} %get-tuple-element.84), channel_id=1, source_target_pairs={{0,12},{4,0},{8,4},{12,8},{1,13},{5,1},{9,5},{13,9},{2,14},{6,2},{... | collective-permute-start | bytes 196616 | tf_op jit(solution)/shard_map/ppermute | solution.py:22
  63.4 1.9 %collective-permute-done.19 = f32[8,8,128]{2,1,0:T(8,128)S(1)} collective-permute-done((f32[8,8,128]{2,1,0:T(8,128)S(1)}, f32[8,8,128]{2,1,0:T(8,128)S(1)}, u32[]{:S(2)}, u32[]{:S(2)}) %collective-permute-start.19) | collective-permute-done | bytes 32800 | tf_op jit(solution)/shard_map/ppermute | solution.py:22
  68.3 2.4 %collective-permute-start.26 = (f32[48,256]{1,0:T(8,128)S(1)}, f32[48,256]{1,0:T(8,128)S(1)}, u32[]{:S(2)}, u32[]{:S(2)}) collective-permute-start(f32[48,256]{1,0:T(8,128)S(1)} %get-tuple-element.88), channel_id=1, source_target_pairs={{0,1},{1,2},{2,3},{3,0},{4,5},{5,6},{6,7},{7,4},{8,9},{9,10},{10,1... | collective-permute-start | bytes 147464 | tf_op jit(solution)/shard_map/ppermute | solution.py:22
  70.7 1.4 %collective-permute-start.27 = (f32[48,256]{1,0:T(8,128)S(1)}, f32[48,256]{1,0:T(8,128)S(1)}, u32[]{:S(2)}, u32[]{:S(2)}) collective-permute-start(f32[48,256]{1,0:T(8,128)S(1)} %get-tuple-element.89), channel_id=1, source_target_pairs={{0,3},{1,0},{2,1},{3,2},{4,7},{5,4},{6,5},{7,6},{8,11},{9,8},{10,9... | collective-permute-start | bytes 147464 | tf_op jit(solution)/shard_map/ppermute | solution.py:22
  72.1 2.5 %collective-permute-done.26.before = f32[48,256]{1,0:T(8,128)S(1)} collective-permute-done((f32[48,256]{1,0:T(8,128)S(1)}, f32[48,256]{1,0:T(8,128)S(1)}, u32[]{:S(2)}, u32[]{:S(2)}) %collective-permute-start.26) | collective-permute-done | bytes 49184 | tf_op jit(solution)/shard_map/ppermute | solution.py:22
  76.5 2.6 %shard_map.88 = (f32[5,8,128]{2,1,0:T(8,128)S(1)}, f32[16,24,256]{2,1,0:T(8,128)S(1)}, f32[8,24,256]{2,1,0:T(8,128)S(1)}, f32[8,24,256]{2,1,0:T(8,128)S(1)}, f32[8,128]{1,0:T(8,128)S(1)}) custom-call(f32[32,8,128]{2,1,0:T(8,128)S(1)} %pad_maximum_fusion.refs_0_, f32[32,8,128]{2,1,0:T(8,128)S(1)} %collective-permute-done.23.refs_1_, ...), custom_call_target="tpu_custom_call" | custom-call | tf_op jit(solution)/shard_map/pallas_call | solution.py:335
  79.1 2.7 %collective-permute-start.30 = (f32[5,8,128]{2,1,0:T(8,128)S(1)}, f32[5,8,128]{2,1,0:T(8,128)S(1)}, u32[]{:S(2)}, u32[]{:S(2)}) collective-permute-start(f32[5,8,128]{2,1,0:T(8,128)S(1)} %get-tuple-element.94), channel_id=1, source_target_pairs={{0,3},{1,0},{2,1},{3,2},{4,7},{5,4},{6,5},{7,6},{8,11},{9,8},{10,9... | collective-permute-start | bytes 61448 | tf_op jit(solution)/shard_map/ppermute | solution.py:22
  82.6 4.8 %collective-permute-done.28 = f32[5,8,128]{2,1,0:T(8,128)S(1)} collective-permute-done((f32[5,8,128]{2,1,0:T(8,128)S(1)}, f32[5,8,128]{2,1,0:T(8,128)S(1)}, u32[]{:S(2)}, u32[]{:S(2)}) %collective-permute-start.28) | collective-permute-done | bytes 20512 | tf_op jit(solution)/shard_map/ppermute | solution.py:22
  89.7 3.3 %collective-permute-done.32.refs_2_ = f32[20,8,128]{2,1,0:T(8,128)S(1)} collective-permute-done((f32[20,8,128]{2,1,0:T(8,128)S(1)}, f32[20,8,128]{2,1,0:T(8,128)S(1)}, u32[]{:S(2)}, u32[]{:S(2)}) %collective-permute-start.32) | collective-permute-done | bytes 81952 | tf_op jit(solution)/shard_map/ppermute | solution.py:22
  93.6 2.6 %shard_map.89 = (f32[8,16,256]{2,1,0:T(8,128)}, f32[8,16,256]{2,1,0:T(8,128)}) custom-call(f32[20,8,128]{2,1,0:T(8,128)S(1)} %constant_dynamic-update-slice_fusion.8.refs_0_, f32[20,8,128]{2,1,0:T(8,128)S(1)} %collective-permute-done.31.refs_1_, f32[20,8,128]{2,1,0:T(8,128)S(1)} %collective-permute-done.32.refs_2_, ...), custom_call_target="tpu_custom_call" | custom-call | tf_op jit(solution)/shard_map/pallas_call | solution.py:335
  (82 shorter events, 20.9 us)
Async XLA Ops:
  4.8 8.5 %collective-permute-start.2 = (f32[152,256]{1,0:T(8,128)S(1)}, f32[152,256]{1,0:T(8,128)S(1)}, u32[]{:S(2)}, u32[]{:S(2)}) collective-permute-start(f32[152,256]{1,0:T(8,128)S(1)} %get-tuple-element.53), channel_id=1, source_target_pairs={{0,1},{1,0},{2,3},{3,2},{4,5},{5,4},{6,7},{7,6},{8,9},{9,8},{10,11... | collective-permute-start | bytes 466952 | tf_op jit(solution)/shard_map/ppermute | solution.py:31
  7.4 5.9 %collective-permute-start.3 = (f32[152,256]{1,0:T(8,128)S(1)}, f32[152,256]{1,0:T(8,128)S(1)}, u32[]{:S(2)}, u32[]{:S(2)}) collective-permute-start(f32[152,256]{1,0:T(8,128)S(1)} %get-tuple-element.54), channel_id=1, source_target_pairs={{0,0},{3,3},{1,2},{2,1},{4,4},{7,7},{5,6},{6,5},{8,8},{11,11},{9,1... | collective-permute-start | bytes 466952 | tf_op jit(solution)/shard_map/ppermute | solution.py:31
  8.2 6.7 %collective-permute-start.4 = (f32[64,256]{1,0:T(8,128)S(1)}, f32[64,256]{1,0:T(8,128)S(1)}, u32[]{:S(2)}, u32[]{:S(2)}) collective-permute-start(f32[64,256]{1,0:T(8,128)S(1)} %get-tuple-element.55), channel_id=1, source_target_pairs={{0,1},{1,0},{2,3},{3,2},{4,5},{5,4},{6,7},{7,6},{8,9},{9,8},{10,11... | collective-permute-start | bytes 196616 | tf_op jit(solution)/shard_map/ppermute | solution.py:31
  17.3 11.2 %collective-permute-start.8 = (f32[8,8,128]{2,1,0:T(8,128)S(1)}, f32[8,8,128]{2,1,0:T(8,128)S(1)}, u32[]{:S(2)}, u32[]{:S(2)}) collective-permute-start(f32[8,8,128]{2,1,0:T(8,128)S(1)} %get-tuple-element.58), channel_id=1, source_target_pairs={{0,3},{1,0},{2,1},{3,2},{4,7},{5,4},{6,5},{7,6},{8,11},{9,8},{10,9... | collective-permute-start | bytes 98312 | tf_op jit(solution)/shard_map/ppermute | solution.py:22
  18.9 9.5 %collective-permute-start.7 = (f32[8,8,128]{2,1,0:T(8,128)S(1)}, f32[8,8,128]{2,1,0:T(8,128)S(1)}, u32[]{:S(2)}, u32[]{:S(2)}) collective-permute-start(f32[8,8,128]{2,1,0:T(8,128)S(1)} %get-tuple-element.58), channel_id=1, source_target_pairs={{0,2},{1,3},{2,0},{3,1},{4,6},{5,7},{6,4},{7,5},{8,10},{9,11},{10,... | collective-permute-start | bytes 98312 | tf_op jit(solution)/shard_map/ppermute | solution.py:22
  22.7 5.7 %collective-permute-start.6 = (f32[8,8,128]{2,1,0:T(8,128)S(1)}, f32[8,8,128]{2,1,0:T(8,128)S(1)}, u32[]{:S(2)}, u32[]{:S(2)}) collective-permute-start(f32[8,8,128]{2,1,0:T(8,128)S(1)} %get-tuple-element.58), channel_id=1, source_target_pairs={{0,1},{1,2},{2,3},{3,0},{4,5},{5,6},{6,7},{7,4},{8,9},{9,10},{10,1... | collective-permute-start | bytes 98312 | tf_op jit(solution)/shard_map/ppermute | solution.py:22
  28.5 5.5 %collective-permute-start.11 = (f32[32,8,128]{2,1,0:T(8,128)S(1)}, f32[32,8,128]{2,1,0:T(8,128)S(1)}, u32[]{:S(2)}, u32[]{:S(2)}) collective-permute-start(f32[32,8,128]{2,1,0:T(8,128)S(1)} %constant_dynamic-update-slice_fusion.refs_0_), channel_id=1, source_target_pairs={{0,12},{4,0},{8,4},{12,8},{1,13},{5,1},{9,5},{13,9},{2,14},{6,2},{... | collective-permute-start | bytes 393224 | tf_op jit(solution)/shard_map/ppermute | solution.py:22
  28.5 12.0 %collective-permute-start.10 = (f32[32,8,128]{2,1,0:T(8,128)S(1)}, f32[32,8,128]{2,1,0:T(8,128)S(1)}, u32[]{:S(2)}, u32[]{:S(2)}) collective-permute-start(f32[32,8,128]{2,1,0:T(8,128)S(1)} %constant_dynamic-update-slice_fusion.refs_0_), channel_id=1, source_target_pairs={{0,8},{4,12},{8,0},{12,4},{1,9},{5,13},{9,1},{13,5},{2,10},{6,14},... | collective-permute-start | bytes 393224 | tf_op jit(solution)/shard_map/ppermute | solution.py:22
  33.6 6.9 %collective-permute-start.9 = (f32[32,8,128]{2,1,0:T(8,128)S(1)}, f32[32,8,128]{2,1,0:T(8,128)S(1)}, u32[]{:S(2)}, u32[]{:S(2)}) collective-permute-start(f32[32,8,128]{2,1,0:T(8,128)S(1)} %constant_dynamic-update-slice_fusion.refs_0_), channel_id=1, source_target_pairs={{0,4},{4,8},{8,12},{12,0},{1,5},{5,9},{9,13},{13,1},{2,6},{6,10},{... | collective-permute-start | bytes 393224 | tf_op jit(solution)/shard_map/ppermute | solution.py:22
  43.5 7.3 %collective-permute-start.14 = (f32[5,8,128]{2,1,0:T(8,128)S(1)}, f32[5,8,128]{2,1,0:T(8,128)S(1)}, u32[]{:S(2)}, u32[]{:S(2)}) collective-permute-start(f32[5,8,128]{2,1,0:T(8,128)S(1)} %get-tuple-element.74), channel_id=1, source_target_pairs={{0,3},{1,0},{2,1},{3,2},{4,7},{5,4},{6,5},{7,6},{8,11},{9,8},{10,9... | collective-permute-start | bytes 61448 | tf_op jit(solution)/shard_map/ppermute | solution.py:22
  44.0 6.7 %collective-permute-start.13 = (f32[5,8,128]{2,1,0:T(8,128)S(1)}, f32[5,8,128]{2,1,0:T(8,128)S(1)}, u32[]{:S(2)}, u32[]{:S(2)}) collective-permute-start(f32[5,8,128]{2,1,0:T(8,128)S(1)} %get-tuple-element.74), channel_id=1, source_target_pairs={{0,2},{1,3},{2,0},{3,1},{4,6},{5,7},{6,4},{7,5},{8,10},{9,11},{10,... | collective-permute-start | bytes 61448 | tf_op jit(solution)/shard_map/ppermute | solution.py:22
  45.2 5.6 %collective-permute-start.12 = (f32[5,8,128]{2,1,0:T(8,128)S(1)}, f32[5,8,128]{2,1,0:T(8,128)S(1)}, u32[]{:S(2)}, u32[]{:S(2)}) collective-permute-start(f32[5,8,128]{2,1,0:T(8,128)S(1)} %get-tuple-element.74), channel_id=1, source_target_pairs={{0,1},{1,2},{2,3},{3,0},{4,5},{5,6},{6,7},{7,4},{8,9},{9,10},{10,1... | collective-permute-start | bytes 61448 | tf_op jit(solution)/shard_map/ppermute | solution.py:22
  50.8 5.4 %collective-permute-start.16 = (f32[20,8,128]{2,1,0:T(8,128)S(1)}, f32[20,8,128]{2,1,0:T(8,128)S(1)}, u32[]{:S(2)}, u32[]{:S(2)}) collective-permute-start(f32[20,8,128]{2,1,0:T(8,128)S(1)} %constant_dynamic-update-slice_fusion.4.refs_0_), channel_id=1, source_target_pairs={{0,8},{4,12},{8,0},{12,4},{1,9},{5,13},{9,1},{13,5},{2,10},{6,14},... | collective-permute-start | bytes 245768 | tf_op jit(solution)/shard_map/ppermute | solution.py:22
  51.2 5.3 %collective-permute-start.15 = (f32[20,8,128]{2,1,0:T(8,128)S(1)}, f32[20,8,128]{2,1,0:T(8,128)S(1)}, u32[]{:S(2)}, u32[]{:S(2)}) collective-permute-start(f32[20,8,128]{2,1,0:T(8,128)S(1)} %constant_dynamic-update-slice_fusion.4.refs_0_), channel_id=1, source_target_pairs={{0,4},{4,8},{8,12},{12,0},{1,5},{5,9},{9,13},{13,1},{2,6},{6,10},{... | collective-permute-start | bytes 245768 | tf_op jit(solution)/shard_map/ppermute | solution.py:22
  60.5 5.7 %collective-permute-start.18 = (f32[8,8,128]{2,1,0:T(8,128)S(1)}, f32[8,8,128]{2,1,0:T(8,128)S(1)}, u32[]{:S(2)}, u32[]{:S(2)}) collective-permute-start(f32[8,8,128]{2,1,0:T(8,128)S(1)} %get-tuple-element.81), channel_id=1, source_target_pairs={{0,1},{1,2},{2,3},{3,0},{4,5},{5,6},{6,7},{7,4},{8,9},{9,10},{10,1... | collective-permute-start | bytes 98312 | tf_op jit(solution)/shard_map/ppermute | solution.py:22
  66.3 10.2 %collective-permute-start.25 = (f32[32,8,128]{2,1,0:T(8,128)S(1)}, f32[32,8,128]{2,1,0:T(8,128)S(1)}, u32[]{:S(2)}, u32[]{:S(2)}) collective-permute-start(f32[32,8,128]{2,1,0:T(8,128)S(1)} %pad_maximum_fusion.refs_0_), channel_id=1, source_target_pairs={{0,12},{4,0},{8,4},{12,8},{1,13},{5,1},{9,5},{13,9},{2,14},{6,2},{... | collective-permute-start | bytes 393224 | tf_op jit(solution)/shard_map/ppermute | solution.py:22
  67.2 9.2 %collective-permute-start.24 = (f32[32,8,128]{2,1,0:T(8,128)S(1)}, f32[32,8,128]{2,1,0:T(8,128)S(1)}, u32[]{:S(2)}, u32[]{:S(2)}) collective-permute-start(f32[32,8,128]{2,1,0:T(8,128)S(1)} %pad_maximum_fusion.refs_0_), channel_id=1, source_target_pairs={{0,8},{4,12},{8,0},{12,4},{1,9},{5,13},{9,1},{13,5},{2,10},{6,14},... | collective-permute-start | bytes 393224 | tf_op jit(solution)/shard_map/ppermute | solution.py:22
  68.3 8.2 %collective-permute-start.23 = (f32[32,8,128]{2,1,0:T(8,128)S(1)}, f32[32,8,128]{2,1,0:T(8,128)S(1)}, u32[]{:S(2)}, u32[]{:S(2)}) collective-permute-start(f32[32,8,128]{2,1,0:T(8,128)S(1)} %pad_maximum_fusion.refs_0_), channel_id=1, source_target_pairs={{0,4},{4,8},{8,12},{12,0},{1,5},{5,9},{9,13},{13,1},{2,6},{6,10},{... | collective-permute-start | bytes 393224 | tf_op jit(solution)/shard_map/ppermute | solution.py:22
  68.3 6.4 %collective-permute-start.26 = (f32[48,256]{1,0:T(8,128)S(1)}, f32[48,256]{1,0:T(8,128)S(1)}, u32[]{:S(2)}, u32[]{:S(2)}) collective-permute-start(f32[48,256]{1,0:T(8,128)S(1)} %get-tuple-element.88), channel_id=1, source_target_pairs={{0,1},{1,2},{2,3},{3,0},{4,5},{5,6},{6,7},{7,4},{8,9},{9,10},{10,1... | collective-permute-start | bytes 147464 | tf_op jit(solution)/shard_map/ppermute | solution.py:22
  70.7 5.0 %collective-permute-start.27 = (f32[48,256]{1,0:T(8,128)S(1)}, f32[48,256]{1,0:T(8,128)S(1)}, u32[]{:S(2)}, u32[]{:S(2)}) collective-permute-start(f32[48,256]{1,0:T(8,128)S(1)} %get-tuple-element.89), channel_id=1, source_target_pairs={{0,3},{1,0},{2,1},{3,2},{4,7},{5,4},{6,5},{7,6},{8,11},{9,8},{10,9... | collective-permute-start | bytes 147464 | tf_op jit(solution)/shard_map/ppermute | solution.py:22
  79.1 8.3 %collective-permute-start.30 = (f32[5,8,128]{2,1,0:T(8,128)S(1)}, f32[5,8,128]{2,1,0:T(8,128)S(1)}, u32[]{:S(2)}, u32[]{:S(2)}) collective-permute-start(f32[5,8,128]{2,1,0:T(8,128)S(1)} %get-tuple-element.94), channel_id=1, source_target_pairs={{0,3},{1,0},{2,1},{3,2},{4,7},{5,4},{6,5},{7,6},{8,11},{9,8},{10,9... | collective-permute-start | bytes 61448 | tf_op jit(solution)/shard_map/ppermute | solution.py:22
  81.8 5.6 %collective-permute-start.29 = (f32[5,8,128]{2,1,0:T(8,128)S(1)}, f32[5,8,128]{2,1,0:T(8,128)S(1)}, u32[]{:S(2)}, u32[]{:S(2)}) collective-permute-start(f32[5,8,128]{2,1,0:T(8,128)S(1)} %get-tuple-element.94), channel_id=1, source_target_pairs={{0,2},{1,3},{2,0},{3,1},{4,6},{5,7},{6,4},{7,5},{8,10},{9,11},{10,... | collective-permute-start | bytes 61448 | tf_op jit(solution)/shard_map/ppermute | solution.py:22
  81.8 5.6 %collective-permute-start.28 = (f32[5,8,128]{2,1,0:T(8,128)S(1)}, f32[5,8,128]{2,1,0:T(8,128)S(1)}, u32[]{:S(2)}, u32[]{:S(2)}) collective-permute-start(f32[5,8,128]{2,1,0:T(8,128)S(1)} %get-tuple-element.94), channel_id=1, source_target_pairs={{0,1},{1,2},{2,3},{3,0},{4,5},{5,6},{6,7},{7,4},{8,9},{9,10},{10,1... | collective-permute-start | bytes 61448 | tf_op jit(solution)/shard_map/ppermute | solution.py:22
  87.5 5.6 %collective-permute-start.32 = (f32[20,8,128]{2,1,0:T(8,128)S(1)}, f32[20,8,128]{2,1,0:T(8,128)S(1)}, u32[]{:S(2)}, u32[]{:S(2)}) collective-permute-start(f32[20,8,128]{2,1,0:T(8,128)S(1)} %constant_dynamic-update-slice_fusion.8.refs_0_), channel_id=1, source_target_pairs={{0,8},{4,12},{8,0},{12,4},{1,9},{5,13},{9,1},{13,5},{2,10},{6,14},... | collective-permute-start | bytes 245768 | tf_op jit(solution)/shard_map/ppermute | solution.py:22
  (16 other events, 44.5 us)

commit v7 on v6

--- a/solution.py
+++ b/solution.py
@@ -14,7 +14,6 @@
 DEEP = 5
 WIDE = 2
 VMEM_LIMIT = 24 * 1024 * 1024
-EXACT = lax.Precision.HIGHEST
 
 
 def rotate(x, axis, shift):
@@ -40,10 +39,28 @@
     return pltpu.roll(v, step % size, dim)
 
 
-def dot(a, b):
-    return lax.dot_general(
-        a, b, (((1,), (0,)), ((), ())), precision=EXACT, preferred_element_type=jnp.float32
-    )
+def pieces(v):
+    high = v.astype(jnp.bfloat16)
+    rest = v - high.astype(jnp.float32)
+    middle = rest.astype(jnp.bfloat16)
+    return high, middle, (rest - middle.astype(jnp.float32)).astype(jnp.bfloat16)
+
+
+def product(a, b, contract):
+    dims = ((contract[:1], contract[1:]), ((), ()))
+    return lax.dot_general(a, b, dims, preferred_element_type=jnp.float32)
+
+
+def pick_rows(picks, v, contract=(1, 0)):
+    picks = picks.astype(jnp.bfloat16)
+    high, middle, low = (product(picks, part, contract) for part in pieces(v))
+    return high + (middle + low)
+
+
+def pick_lanes(v, picks):
+    picks = picks.astype(jnp.bfloat16)
+    joined = jnp.concatenate(pieces(v), axis=1)
+    return product(joined, jnp.concatenate([picks] * 3, axis=0), (1, 0))
 
 
 def iota(shape, dim):
@@ -84,8 +101,8 @@
     halves = []
     for x in range(0, len(planes), 2):
         pair = jnp.where(inside, planes[x] + planes[x + 1], 0.0)
-        halves.append(dot(pick, pair))
-    packed = dot(jnp.concatenate(halves, axis=0), z_pairs(planes[0].shape[1]))
+        halves.append(pick_rows(pick, pair))
+    packed = pick_lanes(jnp.concatenate(halves, axis=0), z_pairs(planes[0].shape[1]))
     return packed.reshape(len(planes) // 2, rows // 2, packed.shape[1])
 
 
@@ -256,9 +273,13 @@
             fy1[a, window, :], fz1[a, window, :],
         )
         smooth = KEPT * value[x] + rd1[a, window, :] * (source[a, window, :] + off)
-        parts.append(dot(pick, smooth))
-    wide = dot(jnp.concatenate(parts, axis=0), z_copies(lanes))
+        parts.append(pick_rows(pick, smooth))
+    wide = pick_lanes(jnp.concatenate(parts, axis=0), z_copies(lanes))
     return [wide[x * frame_rows : (x + 1) * frame_rows] for x in range(len(parts))]
+
+
+def pairs_room(frame):
+    return (frame[2] // 128, frame[0] // 2 - HALO, frame[1], 128)
 
 
 def coarse_scratch(own, sizes):
@@ -310,6 +331,35 @@
         out_ref[x] = coarse[x]
 
 
+def fine_restricted_by_rows(base, fields, fx, fy, fz, out_ref, room, first, own):
+    halves = []
+    for x in range(first, first + own, 2):
+        pair = 0.0
+        for at in (x, x + 1):
+            off = off_diagonal(
+                fields[at], fields[at - 1], fields[at + 1],
+                fx[at], fx[at + 1], fy[at], fz[at],
+            )
+            pair = pair + (KEPT * base[at] + off)
+        rows, lanes = pair.shape
+        for part in range(0, lanes, 128):
+            room[part // 128, (x - first) // 2] = pair[:, part : part + 128]
+        number = rows // 2 - first
+        halves.append(
+            jnp.concatenate(
+                [
+                    room[part, (x - first) // 2, pl.ds(first, number, stride=2), :]
+                    + room[part, (x - first) // 2, pl.ds(first + 1, number, stride=2), :]
+                    for part in range(lanes // 128)
+                ],
+                axis=1,
+            )
+        )
+    packed = pick_lanes(jnp.concatenate(halves, axis=0), z_pairs(lanes))
+    for x in range(len(halves)):
+        out_ref[x] = packed[x * number : (x + 1) * number]
+
+
 def sensitivity_planes(q, hux, huy, huz, nbu, first, last):
     faces = {x: hux[x] * (q(x) + q(x - 1)) for x in range(first, last + 1)}
     out = {}
@@ -358,10 +408,7 @@
         count = cell.shape[1]
         picks = flag(iota((own_x * own_y, count), 0) == row)
         values = jnp.where(iota((lanes, count), 0) == at_z, precision[...], 0.0)
-        weight = lax.dot_general(
-            picks, values, (((1,), (1,)), ((), ())),
-            precision=EXACT, preferred_element_type=jnp.float32,
-        )
+        weight = pick_rows(picks, values, (1, 1))
         for x in range(own_x):
             out_ref[x] = weight[x * own_y : (x + 1) * own_y]
 
@@ -679,7 +726,7 @@
             (kept,) = take(1)
         else:
             combined, curved_out, norm_ref = take(3)
-        source, whole_mid, pairs, mid, *room = refs[at:]
+        source, whole_mid, pairs, mid, pair_rows, *room = refs[at:]
         frame_rows = iota((rows, lanes), 0)
         own_rows = (frame_rows >= HALO) & (frame_rows < rows - HALO)
         if first_time:
@@ -728,7 +775,7 @@
             if first_time:
                 kept[x] = zero
         iterate = {x: rd[x] * rights[x] for x in range(HALO - 1, planes - HALO + 1)}
-        fine_restricted(rights, iterate, fx, fy, fz, b1, HALO, own_x)
+        fine_restricted_by_rows(rights, iterate, fx, fy, fz, b1, pair_rows, HALO, own_x)
         tile = fold(jnp.where(own_rows, forms, 0.0))
         if first_time:
             tile = halved(tile, fold(jnp.where(own_rows, squares, 0.0)))
@@ -740,7 +787,9 @@
     return call(
         kernel,
         [(coarse[0] + 1,) + coarse[1:], frame] + ([frame] if first_time else [own, own, (8, 128)]),
-        coarse_scratch(coarse, sizes) + [frame] + ([] if first_time else [margin]),
+        coarse_scratch(coarse, sizes)
+        + [frame, pairs_room(frame)]
+        + ([] if first_time else [margin]),
         inputs,
     )
 
@@ -815,10 +864,10 @@
     frame_rows = iota((rows, lanes), 0)
     inside = (frame_rows >= margin) & (frame_rows < rows - margin)
     halves = [
-        dot(pick, jnp.where(inside, planes[x] + planes[x + 1], 0.0))
+        pick_rows(pick, jnp.where(inside, planes[x] + planes[x + 1], 0.0))
         for x in range(0, len(planes), 2)
     ]
-    packed = dot(jnp.concatenate(halves, axis=0), z_pairs(lanes))
+    packed = pick_lanes(jnp.concatenate(halves, axis=0), z_pairs(lanes))
     tops, borders = [], []
     for x in range(len(halves)):
         at = 2 * block_rows * x

time: 96.4 us -> 94.7 us (0.982)
  Pallas kernels: 15.5 us -> 13.7 us
    pallas_call x13, Pallas kernels: 15.5 us -> 13.7 us  [call(): pl.pallas_call(kernel, out_shape=[jax.ShapeDtypeStruct(shape, jnp.float32...]
where the time goes in v7:
time: 94.7 us; the launch traced here: 94.5 us
  waiting for transfers between devices  39.7 us (42%)
  starting transfers between devices  38.2 us (40%)
  Pallas kernels  13.7 us (14%)
  local copies, waits for them, and re-layouts  1.97 us (2%)
    ppermute x28, waiting for transfers between devices, rotate(): return lax.ppermute(x, axis, [(i, (i + shift) % size) for i in range(size)])  38.1 us
    ppermute x28, starting transfers between devices, rotate(): return lax.ppermute(x, axis, [(i, (i + shift) % size) for i in range(size)])  28.6 us
    pallas_call x13, Pallas kernels, call(): pl.pallas_call(kernel, out_shape=[jax.ShapeDtypeStruct(shape, jnp.float32...  13.7 us
    ppermute x3, starting transfers between devices, exchange(): lax.ppermute(even_pairs, axis, outer)  7.66 us
    ppermute x3, starting transfers between devices, exchange(): lax.ppermute(odd_pairs, axis, inner)  1.98 us
    unnamed x21, local copies, waits for them, and re-layouts  1.96 us
  transfers between devices with their start and end apart: 34, of which 16 were waited for; matrix products, arithmetic and copies ran while one was open for 0% of the time, Pallas kernels for 1%

profile of v7, /device:TPU:0, one launch (start us, length us, event | category | flops | bytes accessed | tf_op | source)
XLA Modules:
  0.0 94.5 jit_solution(3257642749531980515)
XLA Ops:
  4.7 2.6 %collective-permute-start.2 = (f32[152,256]{1,0:T(8,128)S(1)}, f32[152,256]{1,0:T(8,128)S(1)}, u32[]{:S(2)}, u32[]{:S(2)}) collective-permute-start(f32[152,256]{1,0:T(8,128)S(1)} %get-tuple-element.53), channel_id=1, source_target_pairs={{0,1},{1,0},{2,3},{3,2},{4,5},{5,4},{6,7},{7,6},{8,9},{9,8},{10,11... | collective-permute-start | bytes 466952 | tf_op jit(solution)/shard_map/ppermute | solution.py:30
  8.2 4.5 %collective-permute-start.4 = (f32[64,256]{1,0:T(8,128)S(1)}, f32[64,256]{1,0:T(8,128)S(1)}, u32[]{:S(2)}, u32[]{:S(2)}) collective-permute-start(f32[64,256]{1,0:T(8,128)S(1)} %get-tuple-element.55), channel_id=1, source_target_pairs={{0,1},{1,0},{2,3},{3,2},{4,5},{5,4},{6,7},{7,6},{8,9},{9,8},{10,11... | collective-permute-start | bytes 196616 | tf_op jit(solution)/shard_map/ppermute | solution.py:30
  13.3 1.6 %collective-permute-done.4.refs_9_ = f32[64,256]{1,0:T(8,128)S(1)} collective-permute-done((f32[64,256]{1,0:T(8,128)S(1)}, f32[64,256]{1,0:T(8,128)S(1)}, u32[]{:S(2)}, u32[]{:S(2)}) %collective-permute-start.4) | collective-permute-done | bytes 65568 | tf_op jit(solution)/shard_map/ppermute | solution.py:30
  14.9 2.4 %shard_map.80 = (f32[16,24,256]{2,1,0:T(8,128)S(1)}, f32[16,24,256]{2,1,0:T(8,128)S(1)}, f32[16,24,256]{2,1,0:T(8,128)S(1)}, f32[16,24,256]{2,1,0:T(8,128)S(1)},...) custom-call(f32[8,16,256]{2,1,0:T(8,128)S(1)} %copy-done, ...), custom_call_target="tpu_custom_call" | custom-call | tf_op jit(solution)/shard_map/pallas_call | solution.py:385
  17.3 1.7 %collective-permute-start.8 = (f32[8,8,128]{2,1,0:T(8,128)S(1)}, f32[8,8,128]{2,1,0:T(8,128)S(1)}, u32[]{:S(2)}, u32[]{:S(2)}) collective-permute-start(f32[8,8,128]{2,1,0:T(8,128)S(1)} %get-tuple-element.58), channel_id=1, source_target_pairs={{0,3},{1,0},{2,1},{3,2},{4,7},{5,4},{6,5},{7,6},{8,11},{9,8},{10,9... | collective-permute-start | bytes 98312 | tf_op jit(solution)/shard_map/ppermute | solution.py:21
  19.0 3.8 %collective-permute-start.7 = (f32[8,8,128]{2,1,0:T(8,128)S(1)}, f32[8,8,128]{2,1,0:T(8,128)S(1)}, u32[]{:S(2)}, u32[]{:S(2)}) collective-permute-start(f32[8,8,128]{2,1,0:T(8,128)S(1)} %get-tuple-element.58), channel_id=1, source_target_pairs={{0,2},{1,3},{2,0},{3,1},{4,6},{5,7},{6,4},{7,5},{8,10},{9,11},{10,... | collective-permute-start | bytes 98312 | tf_op jit(solution)/shard_map/ppermute | solution.py:21
  23.4 5.0 %collective-permute-done.6 = f32[8,8,128]{2,1,0:T(8,128)S(1)} collective-permute-done((f32[8,8,128]{2,1,0:T(8,128)S(1)}, f32[8,8,128]{2,1,0:T(8,128)S(1)}, u32[]{:S(2)}, u32[]{:S(2)}) %collective-permute-start.6) | collective-permute-done | bytes 32800 | tf_op jit(solution)/shard_map/ppermute | solution.py:21
  28.6 5.1 %collective-permute-start.10 = (f32[32,8,128]{2,1,0:T(8,128)S(1)}, f32[32,8,128]{2,1,0:T(8,128)S(1)}, u32[]{:S(2)}, u32[]{:S(2)}) collective-permute-start(f32[32,8,128]{2,1,0:T(8,128)S(1)} %constant_dynamic-update-slice_fusion.refs_0_), channel_id=1, source_target_pairs={{0,8},{4,12},{8,0},{12,4},{1,9},{5,13},{9,1},{13,5},{2,10},{6,14},... | collective-permute-start | bytes 393224 | tf_op jit(solution)/shard_map/ppermute | solution.py:21
  34.0 6.5 %collective-permute-done.10.refs_2_ = f32[32,8,128]{2,1,0:T(8,128)S(1)} collective-permute-done((f32[32,8,128]{2,1,0:T(8,128)S(1)}, f32[32,8,128]{2,1,0:T(8,128)S(1)}, u32[]{:S(2)}, u32[]{:S(2)}) %collective-permute-start.10) | collective-permute-done | bytes 131104 | tf_op jit(solution)/shard_map/ppermute | solution.py:21
  41.1 1.9 %shard_map.83 = (f32[5,8,128]{2,1,0:T(8,128)S(1)}, f32[16,24,256]{2,1,0:T(8,128)S(1)}, f32[16,24,256]{2,1,0:T(8,128)S(1)}) custom-call(f32[32,8,128]{2,1,0:T(8,128)S(1)} %constant_dynamic-update-slice_fusion.refs_0_, f32[32,8,128]{2,1,0:T(8,128)S(1)} %collective-permute-done.9.refs_1_, f32[32,8,128]{2,1,0:T(8,128)S(1)} %collective-permute-done.10.refs_2_, ...), custom_call_target="tpu_custom_call" | custom-call | tf_op jit(solution)/shard_map/pallas_call | solution.py:385
  45.1 5.2 %collective-permute-done.12 = f32[5,8,128]{2,1,0:T(8,128)S(1)} collective-permute-done((f32[5,8,128]{2,1,0:T(8,128)S(1)}, f32[5,8,128]{2,1,0:T(8,128)S(1)}, u32[]{:S(2)}, u32[]{:S(2)}) %collective-permute-start.12) | collective-permute-done | bytes 20512 | tf_op jit(solution)/shard_map/ppermute | solution.py:21
  50.9 2.2 %collective-permute-done.17.refs_3_ = f32[20,8,128]{2,1,0:T(8,128)S(1)} collective-permute-done((f32[20,8,128]{2,1,0:T(8,128)S(1)}, f32[20,8,128]{2,1,0:T(8,128)S(1)}, u32[]{:S(2)}, u32[]{:S(2)}) %collective-permute-start.17) | collective-permute-done | bytes 81952 | tf_op jit(solution)/shard_map/ppermute | solution.py:21
  53.2 2.6 %collective-permute-done.16.refs_2_ = f32[20,8,128]{2,1,0:T(8,128)S(1)} collective-permute-done((f32[20,8,128]{2,1,0:T(8,128)S(1)}, f32[20,8,128]{2,1,0:T(8,128)S(1)}, u32[]{:S(2)}, u32[]{:S(2)}) %collective-permute-start.16) | collective-permute-done | bytes 81952 | tf_op jit(solution)/shard_map/ppermute | solution.py:21
  56.1 2.4 %shard_map.84 = (f32[4,16,256]{2,1,0:T(8,128)S(1)}, f32[4,16,256]{2,1,0:T(8,128)S(1)}, f32[8,16,256]{2,1,0:T(8,128)S(1)}, f32[8,8,128]{2,1,0:T(8,128)S(1)}, f32[8,128]{1,0:T(8,128)S(1)}, /*index=5*/f32[8,128]{1,0:T(8,128)S(1)}) custom-call(f32[20,8,128]{2,1,0:T(8,128)S(1)} %constant_dynamic-update-slice_fusion.4.refs_0_, ...), custom_call_target="tpu_custom_call" | custom-call | tf_op jit(solution)/shard_map/pallas_call | solution.py:385
  60.6 1.7 %collective-permute-start.22 = (f32[4,16,256]{2,1,0:T(8,128)S(1)}, f32[4,16,256]{2,1,0:T(8,128)S(1)}, u32[]{:S(2)}, u32[]{:S(2)}) collective-permute-start(f32[4,16,256]{2,1,0:T(8,128)S(1)} %get-tuple-element.84), channel_id=1, source_target_pairs={{0,12},{4,0},{8,4},{12,8},{1,13},{5,1},{9,5},{13,9},{2,14},{6,2},{... | collective-permute-start | bytes 196616 | tf_op jit(solution)/shard_map/ppermute | solution.py:21
  62.5 1.9 %collective-permute-done.19 = f32[8,8,128]{2,1,0:T(8,128)S(1)} collective-permute-done((f32[8,8,128]{2,1,0:T(8,128)S(1)}, f32[8,8,128]{2,1,0:T(8,128)S(1)}, u32[]{:S(2)}, u32[]{:S(2)}) %collective-permute-start.19) | collective-permute-done | bytes 32800 | tf_op jit(solution)/shard_map/ppermute | solution.py:21
  67.3 2.4 %collective-permute-start.26 = (f32[48,256]{1,0:T(8,128)S(1)}, f32[48,256]{1,0:T(8,128)S(1)}, u32[]{:S(2)}, u32[]{:S(2)}) collective-permute-start(f32[48,256]{1,0:T(8,128)S(1)} %get-tuple-element.88), channel_id=1, source_target_pairs={{0,1},{1,2},{2,3},{3,0},{4,5},{5,6},{6,7},{7,4},{8,9},{9,10},{10,1... | collective-permute-start | bytes 147464 | tf_op jit(solution)/shard_map/ppermute | solution.py:21
  69.8 1.4 %collective-permute-start.27 = (f32[48,256]{1,0:T(8,128)S(1)}, f32[48,256]{1,0:T(8,128)S(1)}, u32[]{:S(2)}, u32[]{:S(2)}) collective-permute-start(f32[48,256]{1,0:T(8,128)S(1)} %get-tuple-element.89), channel_id=1, source_target_pairs={{0,3},{1,0},{2,1},{3,2},{4,7},{5,4},{6,5},{7,6},{8,11},{9,8},{10,9... | collective-permute-start | bytes 147464 | tf_op jit(solution)/shard_map/ppermute | solution.py:21
  71.2 2.5 %collective-permute-done.26.before = f32[48,256]{1,0:T(8,128)S(1)} collective-permute-done((f32[48,256]{1,0:T(8,128)S(1)}, f32[48,256]{1,0:T(8,128)S(1)}, u32[]{:S(2)}, u32[]{:S(2)}) %collective-permute-start.26) | collective-permute-done | bytes 49184 | tf_op jit(solution)/shard_map/ppermute | solution.py:21
  75.5 2.1 %shard_map.88 = (f32[5,8,128]{2,1,0:T(8,128)S(1)}, f32[16,24,256]{2,1,0:T(8,128)S(1)}, f32[8,24,256]{2,1,0:T(8,128)S(1)}, f32[8,24,256]{2,1,0:T(8,128)S(1)}, f32[8,128]{1,0:T(8,128)S(1)}) custom-call(f32[32,8,128]{2,1,0:T(8,128)S(1)} %pad_maximum_fusion.refs_0_, f32[32,8,128]{2,1,0:T(8,128)S(1)} %collective-permute-done.23.refs_1_, ...), custom_call_target="tpu_custom_call" | custom-call | tf_op jit(solution)/shard_map/pallas_call | solution.py:385
  77.7 2.7 %collective-permute-start.30 = (f32[5,8,128]{2,1,0:T(8,128)S(1)}, f32[5,8,128]{2,1,0:T(8,128)S(1)}, u32[]{:S(2)}, u32[]{:S(2)}) collective-permute-start(f32[5,8,128]{2,1,0:T(8,128)S(1)} %get-tuple-element.94), channel_id=1, source_target_pairs={{0,3},{1,0},{2,1},{3,2},{4,7},{5,4},{6,5},{7,6},{8,11},{9,8},{10,9... | collective-permute-start | bytes 61448 | tf_op jit(solution)/shard_map/ppermute | solution.py:21
  81.1 4.8 %collective-permute-done.28 = f32[5,8,128]{2,1,0:T(8,128)S(1)} collective-permute-done((f32[5,8,128]{2,1,0:T(8,128)S(1)}, f32[5,8,128]{2,1,0:T(8,128)S(1)}, u32[]{:S(2)}, u32[]{:S(2)}) %collective-permute-start.28) | collective-permute-done | bytes 20512 | tf_op jit(solution)/shard_map/ppermute | solution.py:21
  88.3 3.3 %collective-permute-done.32.refs_2_ = f32[20,8,128]{2,1,0:T(8,128)S(1)} collective-permute-done((f32[20,8,128]{2,1,0:T(8,128)S(1)}, f32[20,8,128]{2,1,0:T(8,128)S(1)}, u32[]{:S(2)}, u32[]{:S(2)}) %collective-permute-start.32) | collective-permute-done | bytes 81952 | tf_op jit(solution)/shard_map/ppermute | solution.py:21
  92.1 2.4 %shard_map.89 = (f32[8,16,256]{2,1,0:T(8,128)}, f32[8,16,256]{2,1,0:T(8,128)}) custom-call(f32[20,8,128]{2,1,0:T(8,128)S(1)} %constant_dynamic-update-slice_fusion.8.refs_0_, f32[20,8,128]{2,1,0:T(8,128)S(1)} %collective-permute-done.31.refs_1_, f32[20,8,128]{2,1,0:T(8,128)S(1)} %collective-permute-done.32.refs_2_, ...), custom_call_target="tpu_custom_call" | custom-call | tf_op jit(solution)/shard_map/pallas_call | solution.py:385
  (82 shorter events, 20.8 us)
Async XLA Ops:
  4.7 8.5 %collective-permute-start.2 = (f32[152,256]{1,0:T(8,128)S(1)}, f32[152,256]{1,0:T(8,128)S(1)}, u32[]{:S(2)}, u32[]{:S(2)}) collective-permute-start(f32[152,256]{1,0:T(8,128)S(1)} %get-tuple-element.53), channel_id=1, source_target_pairs={{0,1},{1,0},{2,3},{3,2},{4,5},{5,4},{6,7},{7,6},{8,9},{9,8},{10,11... | collective-permute-start | bytes 466952 | tf_op jit(solution)/shard_map/ppermute | solution.py:30
  7.4 5.9 %collective-permute-start.3 = (f32[152,256]{1,0:T(8,128)S(1)}, f32[152,256]{1,0:T(8,128)S(1)}, u32[]{:S(2)}, u32[]{:S(2)}) collective-permute-start(f32[152,256]{1,0:T(8,128)S(1)} %get-tuple-element.54), channel_id=1, source_target_pairs={{0,0},{3,3},{1,2},{2,1},{4,4},{7,7},{5,6},{6,5},{8,8},{11,11},{9,1... | collective-permute-start | bytes 466952 | tf_op jit(solution)/shard_map/ppermute | solution.py:30
  8.2 6.7 %collective-permute-start.4 = (f32[64,256]{1,0:T(8,128)S(1)}, f32[64,256]{1,0:T(8,128)S(1)}, u32[]{:S(2)}, u32[]{:S(2)}) collective-permute-start(f32[64,256]{1,0:T(8,128)S(1)} %get-tuple-element.55), channel_id=1, source_target_pairs={{0,1},{1,0},{2,3},{3,2},{4,5},{5,4},{6,7},{7,6},{8,9},{9,8},{10,11... | collective-permute-start | bytes 196616 | tf_op jit(solution)/shard_map/ppermute | solution.py:30
  17.3 11.2 %collective-permute-start.8 = (f32[8,8,128]{2,1,0:T(8,128)S(1)}, f32[8,8,128]{2,1,0:T(8,128)S(1)}, u32[]{:S(2)}, u32[]{:S(2)}) collective-permute-start(f32[8,8,128]{2,1,0:T(8,128)S(1)} %get-tuple-element.58), channel_id=1, source_target_pairs={{0,3},{1,0},{2,1},{3,2},{4,7},{5,4},{6,5},{7,6},{8,11},{9,8},{10,9... | collective-permute-start | bytes 98312 | tf_op jit(solution)/shard_map/ppermute | solution.py:21
  19.0 9.5 %collective-permute-start.7 = (f32[8,8,128]{2,1,0:T(8,128)S(1)}, f32[8,8,128]{2,1,0:T(8,128)S(1)}, u32[]{:S(2)}, u32[]{:S(2)}) collective-permute-start(f32[8,8,128]{2,1,0:T(8,128)S(1)} %get-tuple-element.58), channel_id=1, source_target_pairs={{0,2},{1,3},{2,0},{3,1},{4,6},{5,7},{6,4},{7,5},{8,10},{9,11},{10,... | collective-permute-start | bytes 98312 | tf_op jit(solution)/shard_map/ppermute | solution.py:21
  22.7 5.7 %collective-permute-start.6 = (f32[8,8,128]{2,1,0:T(8,128)S(1)}, f32[8,8,128]{2,1,0:T(8,128)S(1)}, u32[]{:S(2)}, u32[]{:S(2)}) collective-permute-start(f32[8,8,128]{2,1,0:T(8,128)S(1)} %get-tuple-element.58), channel_id=1, source_target_pairs={{0,1},{1,2},{2,3},{3,0},{4,5},{5,6},{6,7},{7,4},{8,9},{9,10},{10,1... | collective-permute-start | bytes 98312 | tf_op jit(solution)/shard_map/ppermute | solution.py:21
  28.5 5.5 %collective-permute-start.11 = (f32[32,8,128]{2,1,0:T(8,128)S(1)}, f32[32,8,128]{2,1,0:T(8,128)S(1)}, u32[]{:S(2)}, u32[]{:S(2)}) collective-permute-start(f32[32,8,128]{2,1,0:T(8,128)S(1)} %constant_dynamic-update-slice_fusion.refs_0_), channel_id=1, source_target_pairs={{0,12},{4,0},{8,4},{12,8},{1,13},{5,1},{9,5},{13,9},{2,14},{6,2},{... | collective-permute-start | bytes 393224 | tf_op jit(solution)/shard_map/ppermute | solution.py:21
  28.6 12.0 %collective-permute-start.10 = (f32[32,8,128]{2,1,0:T(8,128)S(1)}, f32[32,8,128]{2,1,0:T(8,128)S(1)}, u32[]{:S(2)}, u32[]{:S(2)}) collective-permute-start(f32[32,8,128]{2,1,0:T(8,128)S(1)} %constant_dynamic-update-slice_fusion.refs_0_), channel_id=1, source_target_pairs={{0,8},{4,12},{8,0},{12,4},{1,9},{5,13},{9,1},{13,5},{2,10},{6,14},... | collective-permute-start | bytes 393224 | tf_op jit(solution)/shard_map/ppermute | solution.py:21
  33.7 6.9 %collective-permute-start.9 = (f32[32,8,128]{2,1,0:T(8,128)S(1)}, f32[32,8,128]{2,1,0:T(8,128)S(1)}, u32[]{:S(2)}, u32[]{:S(2)}) collective-permute-start(f32[32,8,128]{2,1,0:T(8,128)S(1)} %constant_dynamic-update-slice_fusion.refs_0_), channel_id=1, source_target_pairs={{0,4},{4,8},{8,12},{12,0},{1,5},{5,9},{9,13},{13,1},{2,6},{6,10},{... | collective-permute-start | bytes 393224 | tf_op jit(solution)/shard_map/ppermute | solution.py:21
  43.0 7.3 %collective-permute-start.14 = (f32[5,8,128]{2,1,0:T(8,128)S(1)}, f32[5,8,128]{2,1,0:T(8,128)S(1)}, u32[]{:S(2)}, u32[]{:S(2)}) collective-permute-start(f32[5,8,128]{2,1,0:T(8,128)S(1)} %get-tuple-element.74), channel_id=1, source_target_pairs={{0,3},{1,0},{2,1},{3,2},{4,7},{5,4},{6,5},{7,6},{8,11},{9,8},{10,9... | collective-permute-start | bytes 61448 | tf_op jit(solution)/shard_map/ppermute | solution.py:21
  43.5 6.7 %collective-permute-start.13 = (f32[5,8,128]{2,1,0:T(8,128)S(1)}, f32[5,8,128]{2,1,0:T(8,128)S(1)}, u32[]{:S(2)}, u32[]{:S(2)}) collective-permute-start(f32[5,8,128]{2,1,0:T(8,128)S(1)} %get-tuple-element.74), channel_id=1, source_target_pairs={{0,2},{1,3},{2,0},{3,1},{4,6},{5,7},{6,4},{7,5},{8,10},{9,11},{10,... | collective-permute-start | bytes 61448 | tf_op jit(solution)/shard_map/ppermute | solution.py:21
  44.7 5.6 %collective-permute-start.12 = (f32[5,8,128]{2,1,0:T(8,128)S(1)}, f32[5,8,128]{2,1,0:T(8,128)S(1)}, u32[]{:S(2)}, u32[]{:S(2)}) collective-permute-start(f32[5,8,128]{2,1,0:T(8,128)S(1)} %get-tuple-element.74), channel_id=1, source_target_pairs={{0,1},{1,2},{2,3},{3,0},{4,5},{5,6},{6,7},{7,4},{8,9},{9,10},{10,1... | collective-permute-start | bytes 61448 | tf_op jit(solution)/shard_map/ppermute | solution.py:21
  50.4 5.4 %collective-permute-start.16 = (f32[20,8,128]{2,1,0:T(8,128)S(1)}, f32[20,8,128]{2,1,0:T(8,128)S(1)}, u32[]{:S(2)}, u32[]{:S(2)}) collective-permute-start(f32[20,8,128]{2,1,0:T(8,128)S(1)} %constant_dynamic-update-slice_fusion.4.refs_0_), channel_id=1, source_target_pairs={{0,8},{4,12},{8,0},{12,4},{1,9},{5,13},{9,1},{13,5},{2,10},{6,14},... | collective-permute-start | bytes 245768 | tf_op jit(solution)/shard_map/ppermute | solution.py:21
  50.8 5.3 %collective-permute-start.15 = (f32[20,8,128]{2,1,0:T(8,128)S(1)}, f32[20,8,128]{2,1,0:T(8,128)S(1)}, u32[]{:S(2)}, u32[]{:S(2)}) collective-permute-start(f32[20,8,128]{2,1,0:T(8,128)S(1)} %constant_dynamic-update-slice_fusion.4.refs_0_), channel_id=1, source_target_pairs={{0,4},{4,8},{8,12},{12,0},{1,5},{5,9},{9,13},{13,1},{2,6},{6,10},{... | collective-permute-start | bytes 245768 | tf_op jit(solution)/shard_map/ppermute | solution.py:21
  59.5 5.7 %collective-permute-start.18 = (f32[8,8,128]{2,1,0:T(8,128)S(1)}, f32[8,8,128]{2,1,0:T(8,128)S(1)}, u32[]{:S(2)}, u32[]{:S(2)}) collective-permute-start(f32[8,8,128]{2,1,0:T(8,128)S(1)} %get-tuple-element.81), channel_id=1, source_target_pairs={{0,1},{1,2},{2,3},{3,0},{4,5},{5,6},{6,7},{7,4},{8,9},{9,10},{10,1... | collective-permute-start | bytes 98312 | tf_op jit(solution)/shard_map/ppermute | solution.py:21
  65.3 10.2 %collective-permute-start.25 = (f32[32,8,128]{2,1,0:T(8,128)S(1)}, f32[32,8,128]{2,1,0:T(8,128)S(1)}, u32[]{:S(2)}, u32[]{:S(2)}) collective-permute-start(f32[32,8,128]{2,1,0:T(8,128)S(1)} %pad_maximum_fusion.refs_0_), channel_id=1, source_target_pairs={{0,12},{4,0},{8,4},{12,8},{1,13},{5,1},{9,5},{13,9},{2,14},{6,2},{... | collective-permute-start | bytes 393224 | tf_op jit(solution)/shard_map/ppermute | solution.py:21
  66.3 9.3 %collective-permute-start.24 = (f32[32,8,128]{2,1,0:T(8,128)S(1)}, f32[32,8,128]{2,1,0:T(8,128)S(1)}, u32[]{:S(2)}, u32[]{:S(2)}) collective-permute-start(f32[32,8,128]{2,1,0:T(8,128)S(1)} %pad_maximum_fusion.refs_0_), channel_id=1, source_target_pairs={{0,8},{4,12},{8,0},{12,4},{1,9},{5,13},{9,1},{13,5},{2,10},{6,14},... | collective-permute-start | bytes 393224 | tf_op jit(solution)/shard_map/ppermute | solution.py:21
  67.3 8.2 %collective-permute-start.23 = (f32[32,8,128]{2,1,0:T(8,128)S(1)}, f32[32,8,128]{2,1,0:T(8,128)S(1)}, u32[]{:S(2)}, u32[]{:S(2)}) collective-permute-start(f32[32,8,128]{2,1,0:T(8,128)S(1)} %pad_maximum_fusion.refs_0_), channel_id=1, source_target_pairs={{0,4},{4,8},{8,12},{12,0},{1,5},{5,9},{9,13},{13,1},{2,6},{6,10},{... | collective-permute-start | bytes 393224 | tf_op jit(solution)/shard_map/ppermute | solution.py:21
  67.3 6.4 %collective-permute-start.26 = (f32[48,256]{1,0:T(8,128)S(1)}, f32[48,256]{1,0:T(8,128)S(1)}, u32[]{:S(2)}, u32[]{:S(2)}) collective-permute-start(f32[48,256]{1,0:T(8,128)S(1)} %get-tuple-element.88), channel_id=1, source_target_pairs={{0,1},{1,2},{2,3},{3,0},{4,5},{5,6},{6,7},{7,4},{8,9},{9,10},{10,1... | collective-permute-start | bytes 147464 | tf_op jit(solution)/shard_map/ppermute | solution.py:21
  69.8 5.0 %collective-permute-start.27 = (f32[48,256]{1,0:T(8,128)S(1)}, f32[48,256]{1,0:T(8,128)S(1)}, u32[]{:S(2)}, u32[]{:S(2)}) collective-permute-start(f32[48,256]{1,0:T(8,128)S(1)} %get-tuple-element.89), channel_id=1, source_target_pairs={{0,3},{1,0},{2,1},{3,2},{4,7},{5,4},{6,5},{7,6},{8,11},{9,8},{10,9... | collective-permute-start | bytes 147464 | tf_op jit(solution)/shard_map/ppermute | solution.py:21
  77.7 8.3 %collective-permute-start.30 = (f32[5,8,128]{2,1,0:T(8,128)S(1)}, f32[5,8,128]{2,1,0:T(8,128)S(1)}, u32[]{:S(2)}, u32[]{:S(2)}) collective-permute-start(f32[5,8,128]{2,1,0:T(8,128)S(1)} %get-tuple-element.94), channel_id=1, source_target_pairs={{0,3},{1,0},{2,1},{3,2},{4,7},{5,4},{6,5},{7,6},{8,11},{9,8},{10,9... | collective-permute-start | bytes 61448 | tf_op jit(solution)/shard_map/ppermute | solution.py:21
  80.3 5.6 %collective-permute-start.29 = (f32[5,8,128]{2,1,0:T(8,128)S(1)}, f32[5,8,128]{2,1,0:T(8,128)S(1)}, u32[]{:S(2)}, u32[]{:S(2)}) collective-permute-start(f32[5,8,128]{2,1,0:T(8,128)S(1)} %get-tuple-element.94), channel_id=1, source_target_pairs={{0,2},{1,3},{2,0},{3,1},{4,6},{5,7},{6,4},{7,5},{8,10},{9,11},{10,... | collective-permute-start | bytes 61448 | tf_op jit(solution)/shard_map/ppermute | solution.py:21
  80.3 5.6 %collective-permute-start.28 = (f32[5,8,128]{2,1,0:T(8,128)S(1)}, f32[5,8,128]{2,1,0:T(8,128)S(1)}, u32[]{:S(2)}, u32[]{:S(2)}) collective-permute-start(f32[5,8,128]{2,1,0:T(8,128)S(1)} %get-tuple-element.94), channel_id=1, source_target_pairs={{0,1},{1,2},{2,3},{3,0},{4,5},{5,6},{6,7},{7,4},{8,9},{9,10},{10,1... | collective-permute-start | bytes 61448 | tf_op jit(solution)/shard_map/ppermute | solution.py:21
  86.0 5.6 %collective-permute-start.32 = (f32[20,8,128]{2,1,0:T(8,128)S(1)}, f32[20,8,128]{2,1,0:T(8,128)S(1)}, u32[]{:S(2)}, u32[]{:S(2)}) collective-permute-start(f32[20,8,128]{2,1,0:T(8,128)S(1)} %constant_dynamic-update-slice_fusion.8.refs_0_), channel_id=1, source_target_pairs={{0,8},{4,12},{8,0},{12,4},{1,9},{5,13},{9,1},{13,5},{2,10},{6,14},... | collective-permute-start | bytes 245768 | tf_op jit(solution)/shard_map/ppermute | solution.py:21
  (16 other events, 44.5 us)
